TPU v7x, 512 devices: a whole 4x8x8 slice. The times are simulated.
512 devices in a mesh: dp: 64 (over y_lo, z, core), shard: 8 (over y_hi, x).
Axes of the slice: x: 4, y: 8 (y_hi: 2, y_lo: 4; y = y_hi * 4 + y_lo), z: 8, core: 2. Of those that a mesh axis runs over, the one named last changes fastest.
Arguments:
- hidden: bfloat16 [131072, 2560], P(('dp', 'shard')), may hold values from -6 to 6
- resid: bfloat16 [1280, 131072], P('shard', 'dp'), may hold values from -6 to 6
- target: bfloat16 [1280, 131072], P('shard', 'dp'), may hold values from -6 to 6
- w_out: bfloat16 [1280, 2560], P('shard'), may hold values from -0.125 to 0.125
- signs: int32 [40, 2560], P('shard'), may hold values from -2147483648 to 2147483646
- m_old: float32 [25600, 128], P(('shard', 'dp')), may hold values from -4 to 4
- v_old: float32 [25600, 128], P(('shard', 'dp')), may hold values from 13.1072 to 131.072
Outputs:
- new_w: bfloat16 [1280, 2560], P('shard')
- new_m: float32 [25600, 128], P(('shard', 'dp'))
- new_v: float32 [25600, 128], P(('shard', 'dp'))
Inputs may be any that keep to these rules, and one draw needn't show every extreme that they name: Every word carries 32 independent signs, bit b of word k belonging to output feature 32 k + b.
All inputs are finite; a program needn't handle non-finite values.
Results may differ from a plain program's by a relative error of at most 0.0023.
Values may be sent and summed in bfloat16 or wider, within the bound.
No kernel may reach another device: no remote copies, remote signals or barrier semaphores. Data moves between devices by JAX's collectives and lax.ppermute only.
A program may use at most 64 MiB of HBM per device.

v0:
```python
import math

import jax
import jax.numpy as jnp
from jax import lax
from jax.sharding import PartitionSpec as P

OPT_STEP = 10


beta_one = 0.9
beta_two = 0.999
learn_rate = 0.15
epsilon = 0.0001


def in_order(blocks, dim):
    blocks = jnp.moveaxis(blocks, 0, dim)
    shape = blocks.shape
    return blocks.reshape(*shape[:dim], shape[dim] * shape[dim + 1], *shape[dim + 2 :])


def from_everyone(shard, axis):
    count = lax.axis_size(axis)
    return lax.all_to_all(
        jnp.broadcast_to(shard[None], (count, *shard.shape)), axis, 0, 0, tiled=True
    )


def collect(shard, axis, dim):
    return in_order(from_everyone(shard, axis), dim)


def unpack_signs(signs):
    shifts = jnp.arange(32, dtype=jnp.int32)
    bit_values = jnp.bitwise_and(jnp.right_shift(signs[:, None, :], shifts[None, :, None]), 1)
    return (1 - 2 * bit_values).reshape(signs.shape[0] * 32, signs.shape[1]).astype(jnp.bfloat16)


def on_device(hidden, resid, target, w_out, signs, m_old, v_old):
    features = w_out.shape[0]
    probes = unpack_signs(signs)
    gathered = lax.all_gather(hidden, "shard", axis=0, tiled=True)
    stacked = jnp.concatenate([w_out, probes], axis=0)
    forward = lax.dot_general(
        stacked, gathered, (((1,), (1,)), ((), ())), preferred_element_type=jnp.float32
    )
    output = forward[:features]
    tangent = forward[features:]
    misfit = resid.astype(jnp.float32) + output - target.astype(jnp.float32)
    spread = 1.0 + misfit * misfit
    rooted = jnp.sqrt(spread)
    slopes = (misfit / rooted).astype(jnp.bfloat16)
    bends = (tangent / (spread * rooted)).astype(jnp.bfloat16)
    joined = jnp.concatenate([slopes, bends], axis=0)
    products = jnp.dot(joined, gathered, preferred_element_type=jnp.float32)
    grad_flat = products[:features].reshape(-1, 128)
    curve_flat = products[features:].reshape(-1, 128)
    replicas = lax.axis_size("dp")
    rows_each = grad_flat.shape[0] // replicas
    row_start = lax.axis_index("dp") * rows_each
    grad_mine, curve_mine = (
        lax.psum_scatter(grad_flat, "dp", scatter_dimension=0, tiled=True),
        lax.psum_scatter(curve_flat, "dp", scatter_dimension=0, tiled=True),
    )
    tokens_all = hidden.shape[0] * replicas * lax.axis_size("shard")
    scaling = 1.0 / math.sqrt(tokens_all)
    gradient = grad_mine * scaling
    curvature = curve_mine * scaling
    my_probes = lax.dynamic_slice_in_dim(probes.reshape(-1, 128), row_start, rows_each, 0)
    diag_est = my_probes.astype(jnp.float32) * curvature
    new_m = beta_one * m_old + (1.0 - beta_one) * gradient
    new_v = beta_two * v_old + (1.0 - beta_two) * diag_est * diag_est
    first_fix = 1.0 - beta_one**OPT_STEP
    second_fix = 1.0 - beta_two**OPT_STEP
    update = new_m / first_fix / (jnp.sqrt(new_v / second_fix) + epsilon)
    own_rows = lax.dynamic_slice_in_dim(w_out.reshape(-1, 128), row_start, rows_each, 0)
    fresh_rows = (own_rows.astype(jnp.float32) - learn_rate * update).astype(jnp.bfloat16)
    new_w = collect(fresh_rows, "dp", 0).reshape(w_out.shape)
    return (new_w, new_m, new_v)


def solution(mesh):
    return jax.shard_map(
        on_device,
        mesh=mesh,
        in_specs=(
            P(("dp", "shard"), None),
            P("shard", "dp"),
            P("shard", "dp"),
            P("shard", None),
            P("shard", None),
            P(("shard", "dp"), None),
            P(("shard", "dp"), None),
        ),
        out_specs=(P("shard", None), P(("shard", "dp"), None), P(("shard", "dp"), None)),
        check_vma=False,
    )
```

profile of v0, /device:TPU:1, one launch (start us, length us, event | category | flops | bytes accessed | tf_op | source)
XLA Modules:
  0.0 543.6 jit_solution(15848608162034212737)
XLA Ops:
  7.2 0.0 copy-start
  7.2 0.0 all-gather.2.cloned.1.call-start
  7.2 0.7 all-gather.2.cloned.1.call-update
  7.9 0.1 shift_right_arithmetic.38
  8.0 1.2 fusion.9
  9.2 0.0 copy-start.2
  9.3 0.0 copy-start.3
  9.3 218.6 %all-gather.2.cloned.1.call-done = bf16[2048,2560]{1,0:T(8,128)(2,1)} async-done(((bf16[256,2560]{1,0:T(8,128)(2,1)}), bf16[2048,2560]{1,0:T(8,128)(2,1)}) %all-gather.2.cloned.1.call-update) | async-done | bytes 10485776 | tf_op jit(solution)/shard_map/all_gather | solution.py:43
  227.9 6.3 %fusion.2 = f32[320,2048]{1,0:T(8,128)S(1)} fusion(bf16[2048,2560]{1,0:T(8,128)(2,1)} %all-gather.2.cloned.1.call-done, bf16[160,2560]{1,0:T(8,128)(2,1)S(1)} %fusion.9, bf16[160,2560]{1,0:T(8,128)(2,1)S(1)} %copy-done), kind=kOutput, calls=%fused_computation.2 | convolution fusion | flops 3358720000 | bytes 14745600 | tf_op jit(solution)/shard_map/dot_general | solution.py:45
  234.2 0.9 fusion.10
  235.1 6.3 %fusion.14 = f32[320,2560]{1,0:T(8,128)S(1)} fusion(bf16[2048,2560]{1,0:T(8,128)(2,1)} %all-gather.2.cloned.1.call-done, bf16[160,2048]{1,0:T(8,128)(2,1)S(1)} %get-tuple-element.11, bf16[160,2048]{1,0:T(8,128)(2,1)S(1)} %get-tuple-element.10), kind=kOutput, calls=%fused_computation.16 | convolution fusion | flops 3358064640 | bytes 15073280 | tf_op jit(solution)/shard_map/dot_general | solution.py:56
  241.4 1.4 fusion.30
  242.8 1.4 reshape.24
  244.3 1.3 reshape.25
  245.6 156.3 %fusion.27 = (f32[64,128]{1,0:T(8,128)S(1)}, f32[64,128]{1,0:T(8,128)S(1)}) fusion(f32[3200,128]{1,0:T(8,128)} %reshape.25, f32[3200,128]{1,0:T(8,128)S(1)} %reshape.24), kind=kCustom, calls=%all-reduce-scatter.2 | all-reduce-scatter fusion | flops 1048577 | bytes 3344384
  401.8 0.0 copy-start.4
  401.9 2.1 collective-permute-start.14
  403.9 1.3 collective-permute-start.27
  405.2 1.3 collective-permute-start.13
  406.5 1.3 collective-permute-start.15
  407.8 1.3 collective-permute-start.16
  409.1 0.0 collective-permute-done.27
  409.2 0.0 copy-start.23
  409.2 1.3 collective-permute-start.17
  410.5 0.0 collective-permute-done.13
  410.5 0.0 copy-start.22
  410.5 1.3 collective-permute-start.18
  411.8 4.5 collective-permute-start.19
  416.3 5.2 collective-permute-start.20
  421.5 14.0 %collective-permute-start.21 = (f32[64,128]{1,0:T(8,128)S(1)}, f32[64,128]{1,0:T(8,128)S(1)}, u32[]{:S(2)}, u32[]{:S(2)}) collective-permute-start(f32[64,128]{1,0:T(8,128)S(1)} %get-tuple-element.5), channel_id=1, source_target_pairs={{0,64},{8,72},{16,80},{24,88},{32,96},{40,104},{48,112},{56,120},{... | collective-permute-start | bytes 98312
  435.6 0.0 collective-permute-done.17
  435.6 1.6 collective-permute-start.22
  437.2 4.9 collective-permute-start.23
  442.1 2.5 collective-permute-start.24
  444.6 1.3 collective-permute-start.25
  445.9 1.3 collective-permute-start.26
  447.2 2.5 collective-permute-start
  449.8 1.8 collective-permute-start.1
  451.7 2.2 collective-permute-start.10
  453.9 2.9 collective-permute-start.11
  456.8 1.3 collective-permute-start.12
  458.2 3.4 collective-permute-start.2
  461.5 2.3 collective-permute-start.3
  463.9 3.6 collective-permute-start.4
  467.5 3.6 collective-permute-start.5
  471.1 2.3 collective-permute-start.6
  473.4 3.0 collective-permute-start.7
  476.4 1.9 collective-permute-start.8
  478.3 1.9 collective-permute-start.9
  480.2 1.9 reshape.23
  482.1 0.1 shift_right_arithmetic.42
  482.3 0.1 shift_right_arithmetic.43
  482.4 0.2 shift_right_arithmetic.35
  482.6 0.1 shift_right_arithmetic.41
  482.7 0.0 copy-start.20
  482.7 0.0 copy-start.21
  482.7 0.1 dynamic-slice.4
  482.8 1.3 dynamic-slice.7
  484.8 7.6 %concatenate.9 = f32[946,128]{1,0:T(8,128)S(1)} concatenate(f32[50,128]{1,0:T(8,128)} %copy-done.23, f32[64,128]{1,0:T(8,128)} %copy-done.13, f32[64,128]{1,0:T(8,128)} %copy-done.11, f32[64,128]{1,0:T(8,128)} %copy-done.9, f32[64,128]{1,0:T(8,128)} %copy-done.8, f32[64,128]{1,0:T(8,128)} %copy-done.7, f32[64,128]{1,0:T(8,128)} %copy-done.6, f32[64,128]{1,0:T(8,128)} %copy-done.5, ...), dimensions={0} | concatenate | bytes 968704
  492.4 11.4 %concatenate.8 = f32[946,128]{1,0:T(8,128)S(1)} concatenate(f32[50,128]{1,0:T(8,128)} %copy-done.22, f32[64,128]{1,0:T(8,128)} %copy-done.16, f32[64,128]{1,0:T(8,128)} %copy-done.15, f32[64,128]{1,0:T(8,128)} %copy-done.14, f32[64,128]{1,0:T(8,128)} %collective-permute-done.9, f32[64,128]{1,0:T(8,128)} %collective-permute-done.8, f32[64,128]{1,0:T(8,128)} %collective-permute-done.7, ...), dimensions={0} | concatenate | bytes 968704
  503.9 1.4 subtract_convert_fusion
  505.3 0.1 broadcast_in_dim.2
  505.4 29.5 %all_to_all.5 = bf16[64,50,128]{2,1,0:T(8,128)(2,1)S(1)} all-to-all(bf16[64,50,128]{2,1,0:T(8,128)(2,1)S(1)} %broadcast_in_dim.2), channel_id=1, replica_groups=mesh['dp'=64,'shard'=8] {'dp'}, dimensions={0} | all-to-all | bytes 1638400 | tf_op jit(solution)/shard_map/all_to_all | solution.py:25
  535.0 1.8 reshape_reshape.3
  (68 shorter events, 0.2 us)
Async XLA Ops:
  7.2 220.7 %copy-start = (bf16[160,2560]{1,0:T(8,128)(2,1)S(1)}, bf16[160,2560]{1,0:T(8,128)(2,1)}, u32[]{:S(2)}) copy-start(bf16[160,2560]{1,0:T(8,128)(2,1)} %param.10) | copy-start | bytes 2457604
  7.2 220.7 %all-gather.2.cloned.1.call-start = ((), (), s32[]{:S(2)}) async-start(), calls=%async_computation.1 | async-start | bytes 11796480 | tf_op jit(solution)/shard_map/all_gather | solution.py:43
  9.2 224.9 %copy-start.2 = (bf16[160,2048]{1,0:T(8,128)(2,1)S(1)}, bf16[160,2048]{1,0:T(8,128)(2,1)}, u32[]{:S(2)}) copy-start(bf16[160,2048]{1,0:T(8,128)(2,1)} %param.9) | copy-start | bytes 1966084
  9.3 224.9 %copy-start.3 = (bf16[160,2048]{1,0:T(8,128)(2,1)S(1)}, bf16[160,2048]{1,0:T(8,128)(2,1)}, u32[]{:S(2)}) copy-start(bf16[160,2048]{1,0:T(8,128)(2,1)} %param.8) | copy-start | bytes 1966084
  245.6 234.6 %copy-start.1 = (bf16[160,2560]{1,0:T(8,128)(2,1)S(1)}, bf16[160,2560]{1,0:T(8,128)(2,1)}, u32[]{:S(2)}) copy-start(bf16[160,2560]{1,0:T(8,128)(2,1)} %param.10) | copy-start | bytes 2457604
  401.8 80.6 %copy-start.4 = (s32[5,2560]{1,0:T(8,128)S(1)}, s32[5,2560]{1,0:T(8,128)}, u32[]{:S(2)}) copy-start(s32[5,2560]{1,0:T(8,128)} %param.11) | copy-start | bytes 153604
  401.9 9.9 %collective-permute-start.14 = (f32[64,128]{1,0:T(8,128)S(1)}, f32[64,128]{1,0:T(8,128)S(1)}, u32[]{:S(2)}, u32[]{:S(2)}) collective-permute-start(f32[64,128]{1,0:T(8,128)S(1)} %get-tuple-element.5), channel_id=1, source_target_pairs={{0,8},{8,16},{16,24},{24,32},{32,40},{40,48},{48,56},{56,64},{64,7... | collective-permute-start | bytes 98312
  403.9 5.2 collective-permute-start.27
  405.2 5.2 collective-permute-start.13
  406.5 9.7 %collective-permute-start.15 = (f32[64,128]{1,0:T(8,128)S(1)}, f32[64,128]{1,0:T(8,128)S(1)}, u32[]{:S(2)}, u32[]{:S(2)}) collective-permute-start(f32[64,128]{1,0:T(8,128)S(1)} %get-tuple-element.5), channel_id=1, source_target_pairs={{0,16},{8,24},{16,32},{24,40},{32,48},{40,56},{48,64},{56,72},{64,... | collective-permute-start | bytes 98312
  407.8 13.7 %collective-permute-start.16 = (f32[64,128]{1,0:T(8,128)S(1)}, f32[64,128]{1,0:T(8,128)S(1)}, u32[]{:S(2)}, u32[]{:S(2)}) collective-permute-start(f32[64,128]{1,0:T(8,128)S(1)} %get-tuple-element.5), channel_id=1, source_target_pairs={{0,24},{8,32},{16,40},{24,48},{32,56},{40,64},{48,72},{56,80},{64,... | collective-permute-start | bytes 98312
  409.2 26.4 %copy-start.23 = (f32[50,128]{1,0:T(8,128)}, f32[50,128]{1,0:T(8,128)S(1)}, u32[]{:S(2)}) copy-start(f32[50,128]{1,0:T(8,128)S(1)} %collective-permute-done.27) | copy-start | bytes 76804
  409.2 26.4 %collective-permute-start.17 = (f32[64,128]{1,0:T(8,128)S(1)}, f32[64,128]{1,0:T(8,128)S(1)}, u32[]{:S(2)}, u32[]{:S(2)}) collective-permute-start(f32[64,128]{1,0:T(8,128)S(1)} %get-tuple-element.5), channel_id=1, source_target_pairs={{0,32},{8,40},{16,48},{24,56},{32,64},{40,72},{48,80},{56,88},{64,... | collective-permute-start | bytes 98312
  410.5 11.0 %copy-start.22 = (f32[50,128]{1,0:T(8,128)}, f32[50,128]{1,0:T(8,128)S(1)}, u32[]{:S(2)}) copy-start(f32[50,128]{1,0:T(8,128)S(1)} %collective-permute-done.13) | copy-start | bytes 76804
  410.5 26.7 %collective-permute-start.18 = (f32[64,128]{1,0:T(8,128)S(1)}, f32[64,128]{1,0:T(8,128)S(1)}, u32[]{:S(2)}, u32[]{:S(2)}) collective-permute-start(f32[64,128]{1,0:T(8,128)S(1)} %get-tuple-element.5), channel_id=1, source_target_pairs={{0,40},{8,48},{16,56},{24,64},{32,72},{40,80},{48,88},{56,96},{64,... | collective-permute-start | bytes 98312
  411.8 30.3 %collective-permute-start.19 = (f32[64,128]{1,0:T(8,128)S(1)}, f32[64,128]{1,0:T(8,128)S(1)}, u32[]{:S(2)}, u32[]{:S(2)}) collective-permute-start(f32[64,128]{1,0:T(8,128)S(1)} %get-tuple-element.5), channel_id=1, source_target_pairs={{0,48},{8,56},{16,64},{24,72},{32,80},{40,88},{48,96},{56,104},{64... | collective-permute-start | bytes 98312
  416.3 28.3 %collective-permute-start.20 = (f32[64,128]{1,0:T(8,128)S(1)}, f32[64,128]{1,0:T(8,128)S(1)}, u32[]{:S(2)}, u32[]{:S(2)}) collective-permute-start(f32[64,128]{1,0:T(8,128)S(1)} %get-tuple-element.5), channel_id=1, source_target_pairs={{0,56},{8,64},{16,72},{24,80},{32,88},{40,96},{48,104},{56,112},{6... | collective-permute-start | bytes 98312
  421.5 24.4 %collective-permute-start.21 = (f32[64,128]{1,0:T(8,128)S(1)}, f32[64,128]{1,0:T(8,128)S(1)}, u32[]{:S(2)}, u32[]{:S(2)}) collective-permute-start(f32[64,128]{1,0:T(8,128)S(1)} %get-tuple-element.5), channel_id=1, source_target_pairs={{0,64},{8,72},{16,80},{24,88},{32,96},{40,104},{48,112},{56,120},{... | collective-permute-start | bytes 98312
  435.6 11.7 %collective-permute-start.22 = (f32[64,128]{1,0:T(8,128)S(1)}, f32[64,128]{1,0:T(8,128)S(1)}, u32[]{:S(2)}, u32[]{:S(2)}) collective-permute-start(f32[64,128]{1,0:T(8,128)S(1)} %get-tuple-element.5), channel_id=1, source_target_pairs={{0,72},{8,80},{16,88},{24,96},{32,104},{40,112},{48,120},{56,128},... | collective-permute-start | bytes 98312
  437.2 12.6 %collective-permute-start.23 = (f32[64,128]{1,0:T(8,128)S(1)}, f32[64,128]{1,0:T(8,128)S(1)}, u32[]{:S(2)}, u32[]{:S(2)}) collective-permute-start(f32[64,128]{1,0:T(8,128)S(1)} %get-tuple-element.5), channel_id=1, source_target_pairs={{0,80},{8,88},{16,96},{24,104},{32,112},{40,120},{48,128},{56,136}... | collective-permute-start | bytes 98312
  442.1 9.5 %collective-permute-start.24 = (f32[64,128]{1,0:T(8,128)S(1)}, f32[64,128]{1,0:T(8,128)S(1)}, u32[]{:S(2)}, u32[]{:S(2)}) collective-permute-start(f32[64,128]{1,0:T(8,128)S(1)} %get-tuple-element.5), channel_id=1, source_target_pairs={{0,88},{8,96},{16,104},{24,112},{32,120},{40,128},{48,136},{56,144... | collective-permute-start | bytes 98312
  444.6 37.6 %copy-start.5 = (f32[64,128]{1,0:T(8,128)}, f32[64,128]{1,0:T(8,128)S(1)}, u32[]{:S(2)}) copy-start(f32[64,128]{1,0:T(8,128)S(1)} %collective-permute-done.20) | copy-start | bytes 98308
  444.6 9.3 %collective-permute-start.25 = (f32[64,128]{1,0:T(8,128)S(1)}, f32[64,128]{1,0:T(8,128)S(1)}, u32[]{:S(2)}, u32[]{:S(2)}) collective-permute-start(f32[64,128]{1,0:T(8,128)S(1)} %get-tuple-element.5), channel_id=1, source_target_pairs={{0,96},{8,104},{16,112},{24,120},{32,128},{40,136},{48,144},{56,15... | collective-permute-start | bytes 98312
  445.9 36.3 %copy-start.6 = (f32[64,128]{1,0:T(8,128)}, f32[64,128]{1,0:T(8,128)S(1)}, u32[]{:S(2)}) copy-start(f32[64,128]{1,0:T(8,128)S(1)} %collective-permute-done.21) | copy-start | bytes 98308
  445.9 10.9 %collective-permute-start.26 = (f32[64,128]{1,0:T(8,128)S(1)}, f32[64,128]{1,0:T(8,128)S(1)}, u32[]{:S(2)}, u32[]{:S(2)}) collective-permute-start(f32[64,128]{1,0:T(8,128)S(1)} %get-tuple-element.5), channel_id=1, source_target_pairs={{0,104},{8,112},{16,120},{24,128},{32,136},{40,144},{48,152},{56,1... | collective-permute-start | bytes 98312
  447.2 34.9 %copy-start.7 = (f32[64,128]{1,0:T(8,128)}, f32[64,128]{1,0:T(8,128)S(1)}, u32[]{:S(2)}) copy-start(f32[64,128]{1,0:T(8,128)S(1)} %collective-permute-done.22) | copy-start | bytes 98308
  447.2 10.9 %collective-permute-start = (f32[64,128]{1,0:T(8,128)S(1)}, f32[64,128]{1,0:T(8,128)S(1)}, u32[]{:S(2)}, u32[]{:S(2)}) collective-permute-start(f32[64,128]{1,0:T(8,128)S(1)} %get-tuple-element.6), channel_id=1, source_target_pairs={{0,8},{8,16},{16,24},{24,32},{32,40},{40,48},{48,56},{56,64},{64,7... | collective-permute-start | bytes 98312
  449.8 32.4 %copy-start.8 = (f32[64,128]{1,0:T(8,128)}, f32[64,128]{1,0:T(8,128)S(1)}, u32[]{:S(2)}) copy-start(f32[64,128]{1,0:T(8,128)S(1)} %collective-permute-done.23) | copy-start | bytes 98308
  449.8 11.7 %collective-permute-start.1 = (f32[64,128]{1,0:T(8,128)S(1)}, f32[64,128]{1,0:T(8,128)S(1)}, u32[]{:S(2)}, u32[]{:S(2)}) collective-permute-start(f32[64,128]{1,0:T(8,128)S(1)} %get-tuple-element.6), channel_id=1, source_target_pairs={{0,16},{8,24},{16,32},{24,40},{32,48},{40,56},{48,64},{56,72},{64,... | collective-permute-start | bytes 98312
  451.7 30.5 %copy-start.9 = (f32[64,128]{1,0:T(8,128)}, f32[64,128]{1,0:T(8,128)S(1)}, u32[]{:S(2)}) copy-start(f32[64,128]{1,0:T(8,128)S(1)} %collective-permute-done.24) | copy-start | bytes 98308
  451.7 12.2 %collective-permute-start.10 = (f32[64,128]{1,0:T(8,128)S(1)}, f32[64,128]{1,0:T(8,128)S(1)}, u32[]{:S(2)}, u32[]{:S(2)}) collective-permute-start(f32[64,128]{1,0:T(8,128)S(1)} %get-tuple-element.6), channel_id=1, source_target_pairs={{0,88},{8,96},{16,104},{24,112},{32,120},{40,128},{48,136},{56,144... | collective-permute-start | bytes 98312
  453.9 28.3 %copy-start.11 = (f32[64,128]{1,0:T(8,128)}, f32[64,128]{1,0:T(8,128)S(1)}, u32[]{:S(2)}) copy-start(f32[64,128]{1,0:T(8,128)S(1)} %collective-permute-done.25) | copy-start | bytes 98308
  453.9 13.6 %collective-permute-start.11 = (f32[64,128]{1,0:T(8,128)S(1)}, f32[64,128]{1,0:T(8,128)S(1)}, u32[]{:S(2)}, u32[]{:S(2)}) collective-permute-start(f32[64,128]{1,0:T(8,128)S(1)} %get-tuple-element.6), channel_id=1, source_target_pairs={{0,96},{8,104},{16,112},{24,120},{32,128},{40,136},{48,144},{56,15... | collective-permute-start | bytes 98312
  456.8 25.4 %copy-start.13 = (f32[64,128]{1,0:T(8,128)}, f32[64,128]{1,0:T(8,128)S(1)}, u32[]{:S(2)}) copy-start(f32[64,128]{1,0:T(8,128)S(1)} %collective-permute-done.26) | copy-start | bytes 98308
  456.8 14.3 %collective-permute-start.12 = (f32[64,128]{1,0:T(8,128)S(1)}, f32[64,128]{1,0:T(8,128)S(1)}, u32[]{:S(2)}, u32[]{:S(2)}) collective-permute-start(f32[64,128]{1,0:T(8,128)S(1)} %get-tuple-element.6), channel_id=1, source_target_pairs={{0,104},{8,112},{16,120},{24,128},{32,136},{40,144},{48,152},{56,1... | collective-permute-start | bytes 98312
  458.1 24.1 %copy-start.10 = (f32[64,128]{1,0:T(8,128)}, f32[64,128]{1,0:T(8,128)S(1)}, u32[]{:S(2)}) copy-start(f32[64,128]{1,0:T(8,128)S(1)} %collective-permute-done) | copy-start | bytes 98308
  458.2 15.2 %collective-permute-start.2 = (f32[64,128]{1,0:T(8,128)S(1)}, f32[64,128]{1,0:T(8,128)S(1)}, u32[]{:S(2)}, u32[]{:S(2)}) collective-permute-start(f32[64,128]{1,0:T(8,128)S(1)} %get-tuple-element.6), channel_id=1, source_target_pairs={{0,24},{8,32},{16,40},{24,48},{32,56},{40,64},{48,72},{56,80},{64,... | collective-permute-start | bytes 98312
  461.5 20.7 %copy-start.12 = (f32[64,128]{1,0:T(8,128)}, f32[64,128]{1,0:T(8,128)S(1)}, u32[]{:S(2)}) copy-start(f32[64,128]{1,0:T(8,128)S(1)} %collective-permute-done.1) | copy-start | bytes 98308
  461.5 14.9 %collective-permute-start.3 = (f32[64,128]{1,0:T(8,128)S(1)}, f32[64,128]{1,0:T(8,128)S(1)}, u32[]{:S(2)}, u32[]{:S(2)}) collective-permute-start(f32[64,128]{1,0:T(8,128)S(1)} %get-tuple-element.6), channel_id=1, source_target_pairs={{0,32},{8,40},{16,48},{24,56},{32,64},{40,72},{48,80},{56,88},{64,... | collective-permute-start | bytes 98312
  463.9 18.4 %copy-start.14 = (f32[64,128]{1,0:T(8,128)}, f32[64,128]{1,0:T(8,128)S(1)}, u32[]{:S(2)}) copy-start(f32[64,128]{1,0:T(8,128)S(1)} %collective-permute-done.10) | copy-start | bytes 98308
  463.9 14.4 %collective-permute-start.4 = (f32[64,128]{1,0:T(8,128)S(1)}, f32[64,128]{1,0:T(8,128)S(1)}, u32[]{:S(2)}, u32[]{:S(2)}) collective-permute-start(f32[64,128]{1,0:T(8,128)S(1)} %get-tuple-element.6), channel_id=1, source_target_pairs={{0,40},{8,48},{16,56},{24,64},{32,72},{40,80},{48,88},{56,96},{64,... | collective-permute-start | bytes 98312
  467.5 14.7 %copy-start.15 = (f32[64,128]{1,0:T(8,128)}, f32[64,128]{1,0:T(8,128)S(1)}, u32[]{:S(2)}) copy-start(f32[64,128]{1,0:T(8,128)S(1)} %collective-permute-done.11) | copy-start | bytes 98308
  467.5 24.8 %collective-permute-start.5 = (f32[64,128]{1,0:T(8,128)S(1)}, f32[64,128]{1,0:T(8,128)}, u32[]{:S(2)}, u32[]{:S(2)}) collective-permute-start(f32[64,128]{1,0:T(8,128)S(1)} %get-tuple-element.6), channel_id=1, source_target_pairs={{0,48},{8,56},{16,64},{24,72},{32,80},{40,88},{48,96},{56,104},{64... | collective-permute-start | bytes 98312
  471.1 11.1 %copy-start.16 = (f32[64,128]{1,0:T(8,128)}, f32[64,128]{1,0:T(8,128)S(1)}, u32[]{:S(2)}) copy-start(f32[64,128]{1,0:T(8,128)S(1)} %collective-permute-done.12) | copy-start | bytes 98308
  471.1 21.3 %collective-permute-start.6 = (f32[64,128]{1,0:T(8,128)S(1)}, f32[64,128]{1,0:T(8,128)}, u32[]{:S(2)}, u32[]{:S(2)}) collective-permute-start(f32[64,128]{1,0:T(8,128)S(1)} %get-tuple-element.6), channel_id=1, source_target_pairs={{0,56},{8,64},{16,72},{24,80},{32,88},{40,96},{48,104},{56,112},{6... | collective-permute-start | bytes 98312
  473.4 8.9 %copy-start.17 = (f32[64,128]{1,0:T(8,128)}, f32[64,128]{1,0:T(8,128)S(1)}, u32[]{:S(2)}) copy-start(f32[64,128]{1,0:T(8,128)S(1)} %collective-permute-done.2) | copy-start | bytes 98308
  473.4 19.0 %collective-permute-start.7 = (f32[64,128]{1,0:T(8,128)S(1)}, f32[64,128]{1,0:T(8,128)}, u32[]{:S(2)}, u32[]{:S(2)}) collective-permute-start(f32[64,128]{1,0:T(8,128)S(1)} %get-tuple-element.6), channel_id=1, source_target_pairs={{0,64},{8,72},{16,80},{24,88},{32,96},{40,104},{48,112},{56,120},{... | collective-permute-start | bytes 98312
  476.4 5.9 %copy-start.18 = (f32[64,128]{1,0:T(8,128)}, f32[64,128]{1,0:T(8,128)S(1)}, u32[]{:S(2)}) copy-start(f32[64,128]{1,0:T(8,128)S(1)} %collective-permute-done.3) | copy-start | bytes 98308
  476.4 16.0 %collective-permute-start.8 = (f32[64,128]{1,0:T(8,128)S(1)}, f32[64,128]{1,0:T(8,128)}, u32[]{:S(2)}, u32[]{:S(2)}) collective-permute-start(f32[64,128]{1,0:T(8,128)S(1)} %get-tuple-element.6), channel_id=1, source_target_pairs={{0,72},{8,80},{16,88},{24,96},{32,104},{40,112},{48,120},{56,128},... | collective-permute-start | bytes 98312
  478.3 4.0 copy-start.19
  478.3 14.1 %collective-permute-start.9 = (f32[64,128]{1,0:T(8,128)S(1)}, f32[64,128]{1,0:T(8,128)}, u32[]{:S(2)}, u32[]{:S(2)}) collective-permute-start(f32[64,128]{1,0:T(8,128)S(1)} %get-tuple-element.6), channel_id=1, source_target_pairs={{0,80},{8,88},{16,96},{24,104},{32,112},{40,120},{48,128},{56,136}... | collective-permute-start | bytes 98312
  482.7 21.2 %copy-start.20 = (f32[50,128]{1,0:T(8,128)S(1)}, f32[50,128]{1,0:T(8,128)}, u32[]{:S(2)}) copy-start(f32[50,128]{1,0:T(8,128)} %param.12) | copy-start | bytes 76804
  482.7 21.2 %copy-start.21 = (f32[50,128]{1,0:T(8,128)S(1)}, f32[50,128]{1,0:T(8,128)}, u32[]{:S(2)}) copy-start(f32[50,128]{1,0:T(8,128)} %param.13) | copy-start | bytes 76804
Sparse Core Ops, SparseCore 0:
  11.2 216.6 all-gather.1
where the time goes:
time: 546 us; the launch traced here: 544 us
  waiting for transfers between devices  219 us (40%)
  blocking collectives  186 us (34%)
  starting transfers between devices  77.8 us (14%)
  local copies, waits for them, and re-layouts  29.1 us (5%)
  between operations  15.5 us (3%)
  matrix products  12.6 us (2%)
    all_gather x1, waiting for transfers between devices, on_device(): gathered = lax.all_gather(hidden, 'shard', axis=0, tiled=True)  219 us
    unnamed x1, blocking collectives  156 us
    unnamed x28, starting transfers between devices  77.8 us
    all_to_all x1, blocking collectives, from_everyone(): lax.all_to_all(jnp.broadcast_to(shard[None], (count, *shard.shape)), axis...  29.5 us
    unnamed x53, local copies, waits for them, and re-layouts  20.5 us
  transfers between devices with their start and end apart: 29, of which 1 were waited for; matrix products, arithmetic and copies ran while one was open for 2% of the time, Pallas kernels for 0%

commit v1 on v0

v1 whole, which is shorter than its diff:
```python
import math

import jax
import jax.numpy as jnp
from jax import lax
from jax.sharding import Mesh, PartitionSpec as P

OPT_STEP = 10


beta_one = 0.9
beta_two = 0.999
learn_rate = 0.15
epsilon = 0.0001


def size(axis):
    return 8 if axis == "y" else lax.axis_size(axis)


def place(axis):
    if axis == "y":
        return lax.axis_index("yh") * 4 + lax.axis_index("yl")
    return lax.axis_index(axis)


def shift(value, axis, by):
    n = size(axis)
    hops = [(i, (i + by) % n) for i in range(n)]
    if axis == "y":
        at = [2 * (y % 4) + y // 4 for y in range(n)]
        return lax.ppermute(value, ("yl", "yh"), [(at[i], at[j]) for i, j in hops])
    return lax.ppermute(value, axis, hops)


def unpack_signs(signs):
    shifts = jnp.arange(32, dtype=jnp.int32)
    bit_values = jnp.bitwise_and(jnp.right_shift(signs[:, None, :], shifts[None, :, None]), 1)
    return (1 - 2 * bit_values).reshape(signs.shape[0] * 32, signs.shape[1]).astype(jnp.bfloat16)


def exchange_sum(pieces, axis, wire):
    n = size(axis)
    me = place(axis)
    total = lax.dynamic_index_in_dim(pieces, me, 0, keepdims=False)
    arrived = []
    for by in range(1, n):
        piece = lax.dynamic_index_in_dim(pieces, (me + by) % n, 0, keepdims=False)
        arrived.append(shift(piece.astype(wire), axis, by))
    for term in arrived:
        total = total + term.astype(jnp.float32)
    return total


def exchange_blocks(block, axis):
    n = lax.axis_size(axis)
    me = lax.axis_index(axis)
    blocks = [block] + [shift(block, axis, by) for by in range(1, n)]
    stacked = jnp.stack(blocks[:1] + blocks[:0:-1])
    return jnp.roll(stacked, me, axis=0)


def on_device(hidden, resid, target, w_out, signs, m_old, v_old):
    features, width = w_out.shape
    tokens = hidden.shape[0]
    group = tokens * lax.axis_size("x")
    half = lax.axis_index("yh")
    core = lax.axis_index("c")
    col = lax.axis_index("x")

    from_left = shift(hidden, "x", 1)
    from_right = shift(hidden, "x", -1)
    far_top = shift(from_left[: tokens // 2], "x", 1)
    far_low = shift(from_right[tokens // 2 :], "x", -1)

    pair = jnp.stack([resid, target])
    other_pair = shift(lax.dynamic_slice_in_dim(pair, (1 - half) * group, group, 2), "yh", 1)
    other_signs = shift(signs, "yh", 1)
    rows = features // 2
    part = shift(lax.dynamic_slice_in_dim(w_out, core * rows, rows, 0), "yh", 1)
    twin = shift(part, "c", 1)
    other_w = jnp.concatenate(
        [jnp.where(core == 0, part, twin), jnp.where(core == 0, twin, part)], axis=0
    )
    probes = unpack_signs(signs)
    other_probes = unpack_signs(other_signs)
    own_pair = lax.dynamic_slice_in_dim(pair, half * group, group, 2)

    def in_order(own, other):
        first = jnp.where(half == 0, own, other)
        second = jnp.where(half == 0, other, own)
        return jnp.concatenate([first, second], axis=0)

    stacked = jnp.concatenate([in_order(w_out, other_w), in_order(probes, other_probes)], axis=0)
    pair_all = jnp.concatenate(
        [jnp.where(half == 0, own_pair, other_pair), jnp.where(half == 0, other_pair, own_pair)], axis=1
    )
    count = 2 * features

    def run(block, places):
        cols = [lax.dynamic_slice_in_dim(pair_all, ((col + k) % 4) * tokens, tokens, 2) for k in places]
        here = jnp.concatenate(cols, axis=2) if len(cols) > 1 else cols[0]
        forward = lax.dot_general(
            stacked, block, (((1,), (1,)), ((), ())), preferred_element_type=jnp.float32
        )
        misfit = here[0].astype(jnp.float32) + forward[:count] - here[1].astype(jnp.float32)
        spread = 1.0 + misfit * misfit
        rooted = jnp.sqrt(spread)
        slopes = (misfit / rooted).astype(jnp.bfloat16)
        bends = (forward[count:] / (spread * rooted)).astype(jnp.bfloat16)
        away = jnp.where(core == 0, bends, slopes)
        kept = jnp.where(core == 0, slopes, bends)
        return away, kept

    near = jnp.concatenate([hidden, from_left, from_right], axis=0)
    away_near, kept_near = run(near, (0, 3, 1))
    sum_away = jnp.dot(away_near, near, preferred_element_type=jnp.float32)
    sum_kept = jnp.dot(kept_near, near, preferred_element_type=jnp.float32)
    far = jnp.concatenate([far_top, far_low], axis=0)
    away_far, kept_far = run(far, (2,))
    sum_away = sum_away + jnp.dot(away_far, far, preferred_element_type=jnp.float32)
    got = shift(sum_away, "c", 1)
    sum_kept = sum_kept + jnp.dot(kept_far, far, preferred_element_type=jnp.float32)
    mine = sum_kept + got

    across, deep = 8, lax.axis_size("z")
    per = count * width // (across * deep * 128)
    pieces = jnp.moveaxis(mine.reshape(across, deep, per, 128), 1, 0)
    over_z = exchange_sum(pieces, "z", jnp.bfloat16)
    over_y = exchange_sum(over_z, "y", jnp.float32)
    each = per // 2
    keep_rows = lax.dynamic_slice_in_dim(over_y, core * each, each, 0)
    send_rows = lax.dynamic_slice_in_dim(over_y, (1 - core) * each, each, 0)
    got_rows = shift(send_rows, "c", 1)
    grad_mine = jnp.where(core == 0, keep_rows, got_rows)
    curve_mine = jnp.where(core == 0, got_rows, keep_rows)

    scaling = 1.0 / math.sqrt(tokens * 512)
    gradient = grad_mine * scaling
    curvature = curve_mine * scaling
    row_start = (
        (lax.axis_index("yl") * lax.axis_size("z") + lax.axis_index("z")) * 2 + core
    ) * each
    my_probes = lax.dynamic_slice_in_dim(probes.reshape(-1, 128), row_start, each, 0)
    diag_est = my_probes.astype(jnp.float32) * curvature
    new_m = beta_one * m_old + (1.0 - beta_one) * gradient
    new_v = beta_two * v_old + (1.0 - beta_two) * diag_est * diag_est
    first_fix = 1.0 - beta_one**OPT_STEP
    second_fix = 1.0 - beta_two**OPT_STEP
    update = new_m / first_fix / (jnp.sqrt(new_v / second_fix) + epsilon)
    own_rows = lax.dynamic_slice_in_dim(w_out.reshape(-1, 128), row_start, each, 0)
    fresh = (own_rows.astype(jnp.float32) - learn_rate * update).astype(jnp.bfloat16)

    by_y = exchange_blocks(fresh, "yl")
    by_z = exchange_blocks(by_y, "z")
    twin_z = shift(by_z, "c", 1)
    both = jnp.stack([jnp.where(core == 0, by_z, twin_z), jnp.where(core == 0, twin_z, by_z)])
    new_w = jnp.transpose(both, (2, 1, 0, 3, 4)).reshape(w_out.shape)
    return (new_w, new_m, new_v)


def solution(mesh):
    fine = Mesh(mesh.devices.reshape(4, 8, 2, 2, 4), ("yl", "z", "c", "yh", "x"))
    dp, shard = ("yl", "z", "c"), ("yh", "x")
    return jax.shard_map(
        on_device,
        mesh=fine,
        in_specs=(
            P(dp + shard, None),
            P(shard, dp),
            P(shard, dp),
            P(shard, None),
            P(shard, None),
            P(shard + dp, None),
            P(shard + dp, None),
        ),
        out_specs=(P(shard, None), P(shard + dp, None), P(shard + dp, None)),
        check_vma=False,
    )
```

time: 546 us -> 262 us (0.48)
  blocking collectives: 186 us -> 0 us
  waiting for transfers between devices: 219 us -> 70.9 us
  starting transfers between devices: 77.8 us -> 153 us
  local copies, waits for them, and re-layouts: 29.1 us -> 13 us
  between operations: 15.5 us -> 1.75 us
  other arithmetic: 3.6 us -> 10.4 us
    all_gather x1 -> x0, waiting for transfers between devices: 219 us -> none  [on_device(): gathered = lax.all_gather(hidden, 'shard', axis=0, tiled=True)]
    unnamed x1 -> x0, blocking collectives: 156 us -> none
    ppermute x0 -> x35, starting transfers between devices: none -> 153 us  [the longest x28 124 us: shift(): return lax.ppermute(value, axis, hops)]
    unnamed x28 -> x0, starting transfers between devices: 77.8 us -> none
    ppermute x0 -> x35, waiting for transfers between devices: none -> 70.9 us  [the longest x28 69.3 us: shift(): return lax.ppermute(value, axis, hops)]
    all_to_all x1 -> x0, blocking collectives: 29.5 us -> none  [from_everyone(): lax.all_to_all(jnp.broadcast_to(shard[None], (count, *shard.shape)), axis...]
    unnamed x53 -> x52, local copies, waits for them, and re-layouts: 20.5 us -> 3.51 us
    dot_general x2 -> x6, matrix products: 12.6 us -> 11.6 us  [the longest x2 3.78 us: run(): lax.dot_general(stacked, block, (((1,), (1,)), ((), ())), preferred_eleme...]
  transfers between devices with their start and end apart: 29 -> 35, of which waited for: 1 -> 13; matrix products, arithmetic and copies ran while one was open for 2% -> 6% of each run, Pallas kernels for 0% -> 0%
where the time goes in v1:
time: 262 us; the launch traced here: 261 us
  starting transfers between devices  153 us (58%)
  waiting for transfers between devices  70.9 us (27%)
  local copies, waits for them, and re-layouts  13 us (5%)
  matrix products  11.6 us (4%)
  other arithmetic  10.4 us (4%)
    ppermute x28, starting transfers between devices, shift(): return lax.ppermute(value, axis, hops)  124 us
    ppermute x28, waiting for transfers between devices, shift(): return lax.ppermute(value, axis, hops)  69.3 us
    ppermute x7, starting transfers between devices, shift(): return lax.ppermute(value, ('yl', 'yh'), [(at[i], at[j]) for i, j in hops])  29.1 us
  transfers between devices with their start and end apart: 35, of which 13 were waited for; matrix products, arithmetic and copies ran while one was open for 6% of the time, Pallas kernels for 0%

profile of v1, /device:TPU:1, one launch (start us, length us, event | category | flops | bytes accessed | tf_op | source)
XLA Modules:
  0.0 260.6 jit_solution(14830409117340363256)
XLA Ops:
  0.7 2.0 fusion.15
  2.7 8.3 %collective-permute-start = (bf16[2,160,1024]{2,1,0:T(8,128)(2,1)}, bf16[2,160,1024]{2,1,0:T(8,128)(2,1)}, u32[]{:S(2)}, u32[]{:S(2)}) collective-permute-start(bf16[2,160,1024]{2,1,0:T(8,128)(2,1)} %fusion.15), channel_id=1, source_target_pairs={{0,4},{4,0},{1,5},{5,1},{2,6},{6,2},{3,7},{7,3},{8,12},{12,8},{9,1... | collective-permute-start | bytes 1966088 | tf_op jit(solution)/shard_map/ppermute | solution.py:33
  11.0 0.8 constant_dynamic-slice_fusion.3
  11.8 1.9 collective-permute-start.1
  13.7 3.1 %collective-permute-start.4 = (bf16[256,2560]{1,0:T(8,128)(2,1)}, bf16[256,2560]{1,0:T(8,128)(2,1)S(1)}, u32[]{:S(2)}, u32[]{:S(2)}) collective-permute-start(bf16[256,2560]{1,0:T(8,128)(2,1)} %param.7), channel_id=1, source_target_pairs={{0,1},{1,2},{2,3},{3,0},{4,5},{5,6},{6,7},{7,4},{8,9},{9,10},{10,1... | collective-permute-start | bytes 3932168 | tf_op jit(solution)/shard_map/ppermute | solution.py:33
  16.8 3.4 %collective-permute-start.5 = (bf16[256,2560]{1,0:T(8,128)(2,1)}, bf16[256,2560]{1,0:T(8,128)(2,1)S(1)}, u32[]{:S(2)}, u32[]{:S(2)}) collective-permute-start(bf16[256,2560]{1,0:T(8,128)(2,1)} %param.7), channel_id=1, source_target_pairs={{0,3},{1,0},{2,1},{3,2},{4,7},{5,4},{6,5},{7,6},{8,11},{9,8},{10,9... | collective-permute-start | bytes 3932168 | tf_op jit(solution)/shard_map/ppermute | solution.py:33
  20.2 7.3 %collective-permute-start.3 = (s32[5,2560]{1,0:T(8,128)S(1)}, s32[5,2560]{1,0:T(8,128)}, u32[]{:S(2)}, u32[]{:S(2)}) collective-permute-start(s32[5,2560]{1,0:T(8,128)S(1)} %copy-done.11), channel_id=1, source_target_pairs={{0,4},{4,0},{1,5},{5,1},{2,6},{6,2},{3,7},{7,3},{8,12},{12,8},{9,1... | collective-permute-start | bytes 153608 | tf_op jit(solution)/shard_map/ppermute | solution.py:33
  27.5 2.5 constant_dynamic-update-slice_fusion.2
  30.1 19.3 %collective-permute-done.3 = s32[5,2560]{1,0:T(8,128)} collective-permute-done((s32[5,2560]{1,0:T(8,128)S(1)}, s32[5,2560]{1,0:T(8,128)}, u32[]{:S(2)}, u32[]{:S(2)}) %collective-permute-start.3) | collective-permute-done | bytes 51232 | tf_op jit(solution)/shard_map/ppermute | solution.py:33
  49.4 1.6 fusion.14
  51.0 14.0 %collective-permute-start.2 = (bf16[80,2560]{1,0:T(8,128)(2,1)}, bf16[80,2560]{1,0:T(8,128)(2,1)S(1)}, u32[]{:S(2)}, u32[]{:S(2)}) collective-permute-start(bf16[80,2560]{1,0:T(8,128)(2,1)} %collective-permute-done.1), channel_id=1, source_target_pairs={{0,8},{8,0},{1,9},{9,1},{2,10},{10,2},{3,11},{11,3},{4,12},{12,4},... | collective-permute-start | bytes 1228808 | tf_op jit(solution)/shard_map/ppermute | solution.py:33
  65.1 1.4 broadcast_select_fusion.2
  66.8 1.1 broadcast_select_fusion.5
  68.2 3.4 %collective-permute-start.6 = (bf16[128,2560]{1,0:T(8,128)(2,1)S(1)}, bf16[128,2560]{1,0:T(8,128)(2,1)S(1)}, u32[]{:S(2)}, u32[]{:S(2)}) collective-permute-start(bf16[128,2560]{1,0:T(8,128)(2,1)S(1)} %slice.45), channel_id=1, source_target_pairs={{0,1},{1,2},{2,3},{3,0},{4,5},{5,6},{6,7},{7,4},{8,9},{9,10},{10,1... | collective-permute-start | bytes 1966088 | tf_op jit(solution)/shard_map/ppermute | solution.py:33
  71.7 3.4 %collective-permute-start.7 = (bf16[128,2560]{1,0:T(8,128)(2,1)S(1)}, bf16[128,2560]{1,0:T(8,128)(2,1)S(1)}, u32[]{:S(2)}, u32[]{:S(2)}) collective-permute-start(bf16[128,2560]{1,0:T(8,128)(2,1)S(1)} %slice.46), channel_id=1, source_target_pairs={{0,3},{1,0},{2,1},{3,2},{4,7},{5,4},{6,5},{7,6},{8,11},{9,8},{10,9... | collective-permute-start | bytes 1966088 | tf_op jit(solution)/shard_map/ppermute | solution.py:33
  75.2 2.7 %fusion.18 = f32[640,768]{1,0:T(8,128)S(1)} fusion(bf16[768,2560]{1,0:T(8,128)(2,1)S(1)} %constant_dynamic-update-slice_fusion, bf16[160,2560]{1,0:T(8,128)(2,1)S(1)} %get-tuple-element.40, bf16[160,2560]{1,0:T(8,128)(2,1)S(1)} %get-tuple-element.39, bf16[160,2560]{1,0:T(8,128)(2,1)S(1)} %get-tuple-element.21, bf16[160,2560]{1,0:T(8,128)(2,1)S(1)} %get-tuple-element.20), kind=kOutput, calls=%fused_computation.46 | convolution fusion | flops 2529689600 | bytes 9175040 | tf_op jit(solution)/shard_map/dot_general | solution.py:103
  78.0 0.7 fusion.9
  78.7 8.9 %collective-permute-done.6 = bf16[128,2560]{1,0:T(8,128)(2,1)S(1)} collective-permute-done((bf16[128,2560]{1,0:T(8,128)(2,1)S(1)}, bf16[128,2560]{1,0:T(8,128)(2,1)S(1)}, u32[]{:S(2)}, u32[]{:S(2)}) %collective-permute-start.6) | collective-permute-done | bytes 655392 | tf_op jit(solution)/shard_map/ppermute | solution.py:33
  87.7 1.7 collective-permute-done.7
  89.4 1.0 fusion.17
  91.3 3.3 %convolution_add_fusion = f32[320,2560]{1,0:T(8,128)} fusion(f32[320,2560]{1,0:T(8,128)S(1)} %fusion.44, bf16[768,2560]{1,0:T(8,128)(2,1)S(1)} %constant_dynamic-update-slice_fusion, bf16[320,768]{1,0:T(8,128)(2,1)S(1)} %get-tuple-element.17, bf16[320,768]{1,0:T(8,128)(2,1)S(1)} %get-tuple-element.16, pred[]{:T(512)S(6)} %eq.44), kind=kOutput, calls=%fused_computation | convolution fusion | flops 1259356160 | bytes 11468801 | tf_op jit(solution)/shard_map/dot_general | solution.py:117
  94.6 3.2 %collective-permute-start.8 = (f32[320,2560]{1,0:T(8,128)}, f32[320,2560]{1,0:T(8,128)}, u32[]{:S(2)}, u32[]{:S(2)}) collective-permute-start(f32[320,2560]{1,0:T(8,128)} %convolution_add_fusion), channel_id=1, source_target_pairs={{0,8},{8,0},{1,9},{9,1},{2,10},{10,2},{3,11},{11,3},{4,12},{12,4},... | collective-permute-start | bytes 9830408 | tf_op jit(solution)/shard_map/ppermute | solution.py:33
  98.5 5.1 %collective-permute-done.8 = f32[320,2560]{1,0:T(8,128)} collective-permute-done((f32[320,2560]{1,0:T(8,128)}, f32[320,2560]{1,0:T(8,128)}, u32[]{:S(2)}, u32[]{:S(2)}) %collective-permute-start.8) | collective-permute-done | bytes 3276832 | tf_op jit(solution)/shard_map/ppermute | solution.py:33
  103.6 3.4 %fusion = f32[320,2560]{1,0:T(8,128)S(1)} fusion(f32[320,2560]{1,0:T(8,128)} %collective-permute-done.8, f32[320,2560]{1,0:T(8,128)S(1)} %fusion.46, bf16[768,2560]{1,0:T(8,128)(2,1)S(1)} %copy-done.2, bf16[320,768]{1,0:T(8,128)(2,1)S(1)} %copy-done.4, bf16[320,768]{1,0:T(8,128)(2,1)S(1)} %copy-done.6, pred[]{:T(512)S(6)} %eq.44), kind=kOutput, calls=%fused_computation.2 | convolution fusion | flops 1260175360 | bytes 14745601 | tf_op jit(solution)/shard_map/dot_general | solution.py:118
  107.0 2.0 reshape.58
  109.0 2.0 fusion.38
  111.0 6.0 %collective-permute-start.10 = (bf16[8,100,128]{2,1,0:T(8,128)(2,1)S(1)}, bf16[8,100,128]{2,1,0:T(8,128)(2,1)S(1)}, u32[]{:S(2)}, u32[]{:S(2)}) collective-permute-start(bf16[8,100,128]{2,1,0:T(8,128)(2,1)S(1)} %get-tuple-element.13), channel_id=1, source_target_pairs={{0,32},{16,48},{32,64},{48,80},{64,96},{80,112},{96,0},{112,16},{1... | collective-permute-start | bytes 614408 | tf_op jit(solution)/shard_map/ppermute | solution.py:33
  117.0 7.9 %collective-permute-start.11 = (bf16[8,100,128]{2,1,0:T(8,128)(2,1)S(1)}, bf16[8,100,128]{2,1,0:T(8,128)(2,1)S(1)}, u32[]{:S(2)}, u32[]{:S(2)}) collective-permute-start(bf16[8,100,128]{2,1,0:T(8,128)(2,1)S(1)} %get-tuple-element.12), channel_id=1, source_target_pairs={{0,48},{16,64},{32,80},{48,96},{64,112},{80,0},{96,16},{112,32},{1... | collective-permute-start | bytes 614408 | tf_op jit(solution)/shard_map/ppermute | solution.py:33
  124.9 3.7 %collective-permute-start.12 = (bf16[8,100,128]{2,1,0:T(8,128)(2,1)S(1)}, bf16[8,100,128]{2,1,0:T(8,128)(2,1)S(1)}, u32[]{:S(2)}, u32[]{:S(2)}) collective-permute-start(bf16[8,100,128]{2,1,0:T(8,128)(2,1)S(1)} %get-tuple-element.11), channel_id=1, source_target_pairs={{0,64},{16,80},{32,96},{48,112},{64,0},{80,16},{96,32},{112,48},{1... | collective-permute-start | bytes 614408 | tf_op jit(solution)/shard_map/ppermute | solution.py:33
  128.7 5.5 %collective-permute-start.13 = (bf16[8,100,128]{2,1,0:T(8,128)(2,1)S(1)}, bf16[8,100,128]{2,1,0:T(8,128)(2,1)S(1)}, u32[]{:S(2)}, u32[]{:S(2)}) collective-permute-start(bf16[8,100,128]{2,1,0:T(8,128)(2,1)S(1)} %get-tuple-element.10), channel_id=1, source_target_pairs={{0,80},{16,96},{32,112},{48,0},{64,16},{80,32},{96,48},{112,64},{1... | collective-permute-start | bytes 614408 | tf_op jit(solution)/shard_map/ppermute | solution.py:33
  134.2 3.4 %collective-permute-start.14 = (bf16[8,100,128]{2,1,0:T(8,128)(2,1)S(1)}, bf16[8,100,128]{2,1,0:T(8,128)(2,1)S(1)}, u32[]{:S(2)}, u32[]{:S(2)}) collective-permute-start(bf16[8,100,128]{2,1,0:T(8,128)(2,1)S(1)} %get-tuple-element.15), channel_id=1, source_target_pairs={{0,96},{16,112},{32,0},{48,16},{64,32},{80,48},{96,64},{112,80},{1... | collective-permute-start | bytes 614408 | tf_op jit(solution)/shard_map/ppermute | solution.py:33
  137.6 1.9 collective-permute-start.15
  139.5 12.1 %collective-permute-done.11 = bf16[8,100,128]{2,1,0:T(8,128)(2,1)S(1)} collective-permute-done((bf16[8,100,128]{2,1,0:T(8,128)(2,1)S(1)}, bf16[8,100,128]{2,1,0:T(8,128)(2,1)S(1)}, u32[]{:S(2)}, u32[]{:S(2)}) %collective-permute-start.11) | collective-permute-done | bytes 204832 | tf_op jit(solution)/shard_map/ppermute | solution.py:33
  151.5 1.9 collective-permute-start.9
  153.9 10.4 %collective-permute-done.14 = bf16[8,100,128]{2,1,0:T(8,128)(2,1)S(1)} collective-permute-done((bf16[8,100,128]{2,1,0:T(8,128)(2,1)S(1)}, bf16[8,100,128]{2,1,0:T(8,128)(2,1)S(1)}, u32[]{:S(2)}, u32[]{:S(2)}) %collective-permute-start.14) | collective-permute-done | bytes 204832 | tf_op jit(solution)/shard_map/ppermute | solution.py:33
  164.3 1.5 collective-permute-done.15
  165.8 1.2 fusion.28
  167.1 3.6 %collective-permute-start.16 = (f32[100,128]{1,0:T(8,128)S(1)}, f32[100,128]{1,0:T(8,128)S(1)}, u32[]{:S(2)}, u32[]{:S(2)}) collective-permute-start(f32[100,128]{1,0:T(8,128)S(1)} %get-tuple-element.32), channel_id=1, source_target_pairs={{0,128},{128,256},{256,384},{384,4},{4,132},{132,260},{260,388},{3... | collective-permute-start | bytes 153608 | tf_op jit(solution)/shard_map/ppermute | solution.py:32
  170.7 3.2 %collective-permute-start.17 = (f32[100,128]{1,0:T(8,128)S(1)}, f32[100,128]{1,0:T(8,128)S(1)}, u32[]{:S(2)}, u32[]{:S(2)}) collective-permute-start(f32[100,128]{1,0:T(8,128)S(1)} %get-tuple-element.38), channel_id=1, source_target_pairs={{0,256},{128,384},{256,4},{384,132},{4,260},{132,388},{260,0},{388... | collective-permute-start | bytes 153608 | tf_op jit(solution)/shard_map/ppermute | solution.py:32
  173.9 5.5 %collective-permute-start.18 = (f32[100,128]{1,0:T(8,128)S(1)}, f32[100,128]{1,0:T(8,128)S(1)}, u32[]{:S(2)}, u32[]{:S(2)}) collective-permute-start(f32[100,128]{1,0:T(8,128)S(1)} %get-tuple-element.37), channel_id=1, source_target_pairs={{0,384},{128,4},{256,132},{384,260},{4,388},{132,0},{260,128},{388... | collective-permute-start | bytes 153608 | tf_op jit(solution)/shard_map/ppermute | solution.py:32
  179.4 4.0 %collective-permute-start.19 = (f32[100,128]{1,0:T(8,128)S(1)}, f32[100,128]{1,0:T(8,128)S(1)}, u32[]{:S(2)}, u32[]{:S(2)}) collective-permute-start(f32[100,128]{1,0:T(8,128)S(1)} %get-tuple-element.36), channel_id=1, source_target_pairs={{0,4},{128,132},{256,260},{384,388},{4,0},{132,128},{260,256},{388... | collective-permute-start | bytes 153608 | tf_op jit(solution)/shard_map/ppermute | solution.py:32
  183.4 4.3 %collective-permute-start.20 = (f32[100,128]{1,0:T(8,128)S(1)}, f32[100,128]{1,0:T(8,128)S(1)}, u32[]{:S(2)}, u32[]{:S(2)}) collective-permute-start(f32[100,128]{1,0:T(8,128)S(1)} %get-tuple-element.35), channel_id=1, source_target_pairs={{0,132},{128,260},{256,388},{384,0},{4,128},{132,256},{260,384},{3... | collective-permute-start | bytes 153608 | tf_op jit(solution)/shard_map/ppermute | solution.py:32
  187.7 5.3 %collective-permute-start.21 = (f32[100,128]{1,0:T(8,128)S(1)}, f32[100,128]{1,0:T(8,128)S(1)}, u32[]{:S(2)}, u32[]{:S(2)}) collective-permute-start(f32[100,128]{1,0:T(8,128)S(1)} %get-tuple-element.34), channel_id=1, source_target_pairs={{0,260},{128,388},{256,0},{384,128},{4,256},{132,384},{260,4},{388... | collective-permute-start | bytes 153608 | tf_op jit(solution)/shard_map/ppermute | solution.py:32
  193.0 3.3 %collective-permute-start.22 = (f32[100,128]{1,0:T(8,128)S(1)}, f32[100,128]{1,0:T(8,128)S(1)}, u32[]{:S(2)}, u32[]{:S(2)}) collective-permute-start(f32[100,128]{1,0:T(8,128)S(1)} %get-tuple-element.33), channel_id=1, source_target_pairs={{0,388},{128,0},{256,128},{384,256},{4,384},{132,4},{260,132},{388... | collective-permute-start | bytes 153608 | tf_op jit(solution)/shard_map/ppermute | solution.py:32
  196.3 1.7 collective-permute-done.22
  198.0 6.2 %collective-permute-start.23 = (f32[50,128]{1,0:T(8,128)S(1)}, f32[50,128]{1,0:T(8,128)S(1)}, u32[]{:S(2)}, u32[]{:S(2)}) collective-permute-start(f32[50,128]{1,0:T(8,128)S(1)} %constant_dynamic-slice_fusion.2), channel_id=1, source_target_pairs={{0,8},{8,0},{1,9},{9,1},{2,10},{10,2},{3,11},{11,3},{4,12},{12,4},... | collective-permute-start | bytes 76808 | tf_op jit(solution)/shard_map/ppermute | solution.py:33
  204.2 1.9 reshape.57
  207.2 1.4 constant_dynamic-update-slice_fusion.12
  208.6 1.9 collective-permute-start.24
  210.6 2.5 collective-permute-start.25
  213.0 2.8 %collective-permute-start.26 = (bf16[50,128]{1,0:T(8,128)(2,1)S(1)}, bf16[50,128]{1,0:T(8,128)(2,1)S(1)}, u32[]{:S(2)}, u32[]{:S(2)}) collective-permute-start(bf16[50,128]{1,0:T(8,128)(2,1)S(1)} %get-tuple-element.6), channel_id=1, source_target_pairs={{0,128},{128,256},{256,384},{384,0},{1,129},{129,257},{257,385},{3... | collective-permute-start | bytes 38408 | tf_op jit(solution)/shard_map/ppermute | solution.py:33
  215.9 3.4 %collective-permute-done.26 = bf16[50,128]{1,0:T(8,128)(2,1)S(1)} collective-permute-done((bf16[50,128]{1,0:T(8,128)(2,1)S(1)}, bf16[50,128]{1,0:T(8,128)(2,1)S(1)}, u32[]{:S(2)}, u32[]{:S(2)}) %collective-permute-start.26) | collective-permute-done | bytes 12832 | tf_op jit(solution)/shard_map/ppermute | solution.py:33
  219.4 4.3 %collective-permute-start.27 = (bf16[4,50,128]{2,1,0:T(8,128)(2,1)S(1)}, bf16[4,50,128]{2,1,0:T(8,128)(2,1)S(1)}, u32[]{:S(2)}, u32[]{:S(2)}) collective-permute-start(bf16[4,50,128]{2,1,0:T(8,128)(2,1)S(1)} %get-tuple-element.4), channel_id=1, source_target_pairs={{0,112},{16,0},{32,16},{48,32},{64,48},{80,64},{96,80},{112,96},{1... | collective-permute-start | bytes 153608 | tf_op jit(solution)/shard_map/ppermute | solution.py:33
  223.7 3.1 %collective-permute-start.28 = (bf16[4,50,128]{2,1,0:T(8,128)(2,1)S(1)}, bf16[4,50,128]{2,1,0:T(8,128)(2,1)S(1)}, u32[]{:S(2)}, u32[]{:S(2)}) collective-permute-start(bf16[4,50,128]{2,1,0:T(8,128)(2,1)S(1)} %get-tuple-element.4), channel_id=1, source_target_pairs={{0,96},{16,112},{32,0},{48,16},{64,32},{80,48},{96,64},{112,80},{1... | collective-permute-start | bytes 153608 | tf_op jit(solution)/shard_map/ppermute | solution.py:33
  226.8 4.8 %collective-permute-start.29 = (bf16[4,50,128]{2,1,0:T(8,128)(2,1)S(1)}, bf16[4,50,128]{2,1,0:T(8,128)(2,1)S(1)}, u32[]{:S(2)}, u32[]{:S(2)}) collective-permute-start(bf16[4,50,128]{2,1,0:T(8,128)(2,1)S(1)} %get-tuple-element.4), channel_id=1, source_target_pairs={{0,80},{16,96},{32,112},{48,0},{64,16},{80,32},{96,48},{112,64},{1... | collective-permute-start | bytes 153608 | tf_op jit(solution)/shard_map/ppermute | solution.py:33
  231.7 3.5 %collective-permute-start.30 = (bf16[4,50,128]{2,1,0:T(8,128)(2,1)S(1)}, bf16[4,50,128]{2,1,0:T(8,128)(2,1)S(1)}, u32[]{:S(2)}, u32[]{:S(2)}) collective-permute-start(bf16[4,50,128]{2,1,0:T(8,128)(2,1)S(1)} %get-tuple-element.4), channel_id=1, source_target_pairs={{0,64},{16,80},{32,96},{48,112},{64,0},{80,16},{96,32},{112,48},{1... | collective-permute-start | bytes 153608 | tf_op jit(solution)/shard_map/ppermute | solution.py:33
  235.2 4.1 %collective-permute-start.31 = (bf16[4,50,128]{2,1,0:T(8,128)(2,1)S(1)}, bf16[4,50,128]{2,1,0:T(8,128)(2,1)S(1)}, u32[]{:S(2)}, u32[]{:S(2)}) collective-permute-start(bf16[4,50,128]{2,1,0:T(8,128)(2,1)S(1)} %get-tuple-element.4), channel_id=1, source_target_pairs={{0,48},{16,64},{32,80},{48,96},{64,112},{80,0},{96,16},{112,32},{1... | collective-permute-start | bytes 153608 | tf_op jit(solution)/shard_map/ppermute | solution.py:33
  239.3 4.9 %collective-permute-start.32 = (bf16[4,50,128]{2,1,0:T(8,128)(2,1)S(1)}, bf16[4,50,128]{2,1,0:T(8,128)(2,1)S(1)}, u32[]{:S(2)}, u32[]{:S(2)}) collective-permute-start(bf16[4,50,128]{2,1,0:T(8,128)(2,1)S(1)} %get-tuple-element.4), channel_id=1, source_target_pairs={{0,32},{16,48},{32,64},{48,80},{64,96},{80,112},{96,0},{112,16},{1... | collective-permute-start | bytes 153608 | tf_op jit(solution)/shard_map/ppermute | solution.py:33
  244.3 1.9 collective-permute-start.33
  246.3 2.2 collective-permute-done.32
  248.5 2.9 %collective-permute-done.33 = bf16[4,50,128]{2,1,0:T(8,128)(2,1)S(1)} collective-permute-done((bf16[4,50,128]{2,1,0:T(8,128)(2,1)S(1)}, bf16[4,50,128]{2,1,0:T(8,128)(2,1)S(1)}, u32[]{:S(2)}, u32[]{:S(2)}) %collective-permute-start.33) | collective-permute-done | bytes 51232 | tf_op jit(solution)/shard_map/ppermute | solution.py:33
  251.6 5.5 %collective-permute-start.34 = (bf16[8,4,50,128]{3,2,1,0:T(8,128)(2,1)S(1)}, bf16[8,4,50,128]{3,2,1,0:T(8,128)(2,1)S(1)}, u32[]{:S(2)}, u32[]{:S(2)}) collective-permute-start(bf16[8,4,50,128]{3,2,1,0:T(8,128)(2,1)S(1)} %constant_dynamic-slice_fusion), channel_id=1, source_target_pairs={{0,8},{8,0},{1,9},{9,1},{2,10},{10,2},{3,11},{11,3},{4,12},{12,4},... | collective-permute-start | bytes 1228808 | tf_op jit(solution)/shard_map/ppermute | solution.py:33
  257.1 1.4 collective-permute-done.34
  258.8 1.8 reshape.59
  (100 shorter events, 4.6 us)
Async XLA Ops:
  0.6 10.3 %copy-start.7 = (bf16[160,2560]{1,0:T(8,128)(2,1)S(1)}, bf16[160,2560]{1,0:T(8,128)(2,1)}, u32[]{:S(2)}) copy-start(bf16[160,2560]{1,0:T(8,128)(2,1)} %param.10) | copy-start | bytes 2457604
  0.6 19.6 %copy-start.11 = (s32[5,2560]{1,0:T(8,128)S(1)}, s32[5,2560]{1,0:T(8,128)}, u32[]{:S(2)}) copy-start(s32[5,2560]{1,0:T(8,128)} %param.11) | copy-start | bytes 153604
  2.7 62.4 %collective-permute-start = (bf16[2,160,1024]{2,1,0:T(8,128)(2,1)}, bf16[2,160,1024]{2,1,0:T(8,128)(2,1)}, u32[]{:S(2)}, u32[]{:S(2)}) collective-permute-start(bf16[2,160,1024]{2,1,0:T(8,128)(2,1)} %fusion.15), channel_id=1, source_target_pairs={{0,4},{4,0},{1,5},{5,1},{2,6},{6,2},{3,7},{7,3},{8,12},{12,8},{9,1... | collective-permute-start | bytes 1966088 | tf_op jit(solution)/shard_map/ppermute | solution.py:33
  11.8 39.3 %collective-permute-start.1 = (bf16[80,2560]{1,0:T(8,128)(2,1)}, bf16[80,2560]{1,0:T(8,128)(2,1)}, u32[]{:S(2)}, u32[]{:S(2)}) collective-permute-start(bf16[80,2560]{1,0:T(8,128)(2,1)} %constant_dynamic-slice_fusion.3), channel_id=1, source_target_pairs={{0,4},{4,0},{1,5},{5,1},{2,6},{6,2},{3,7},{7,3},{8,12},{12,8},{9,1... | collective-permute-start | bytes 1228808 | tf_op jit(solution)/shard_map/ppermute | solution.py:33
  13.7 54.5 %collective-permute-start.4 = (bf16[256,2560]{1,0:T(8,128)(2,1)}, bf16[256,2560]{1,0:T(8,128)(2,1)S(1)}, u32[]{:S(2)}, u32[]{:S(2)}) collective-permute-start(bf16[256,2560]{1,0:T(8,128)(2,1)} %param.7), channel_id=1, source_target_pairs={{0,1},{1,2},{2,3},{3,0},{4,5},{5,6},{6,7},{7,4},{8,9},{9,10},{10,1... | collective-permute-start | bytes 3932168 | tf_op jit(solution)/shard_map/ppermute | solution.py:33
  16.8 54.8 %collective-permute-start.5 = (bf16[256,2560]{1,0:T(8,128)(2,1)}, bf16[256,2560]{1,0:T(8,128)(2,1)S(1)}, u32[]{:S(2)}, u32[]{:S(2)}) collective-permute-start(bf16[256,2560]{1,0:T(8,128)(2,1)} %param.7), channel_id=1, source_target_pairs={{0,3},{1,0},{2,1},{3,2},{4,7},{5,4},{6,5},{7,6},{8,11},{9,8},{10,9... | collective-permute-start | bytes 3932168 | tf_op jit(solution)/shard_map/ppermute | solution.py:33
  20.2 29.2 %collective-permute-start.3 = (s32[5,2560]{1,0:T(8,128)S(1)}, s32[5,2560]{1,0:T(8,128)}, u32[]{:S(2)}, u32[]{:S(2)}) collective-permute-start(s32[5,2560]{1,0:T(8,128)S(1)} %copy-done.11), channel_id=1, source_target_pairs={{0,4},{4,0},{1,5},{5,1},{2,6},{6,2},{3,7},{7,3},{8,12},{12,8},{9,1... | collective-permute-start | bytes 153608 | tf_op jit(solution)/shard_map/ppermute | solution.py:33
  30.1 35.0 %copy-start.9 = (bf16[160,2048]{1,0:T(8,128)(2,1)S(1)}, bf16[160,2048]{1,0:T(8,128)(2,1)}, u32[]{:S(2)}) copy-start(bf16[160,2048]{1,0:T(8,128)(2,1)} %param.8) | copy-start | bytes 1966084
  30.1 35.0 %copy-start.10 = (bf16[160,2048]{1,0:T(8,128)(2,1)S(1)}, bf16[160,2048]{1,0:T(8,128)(2,1)}, u32[]{:S(2)}) copy-start(bf16[160,2048]{1,0:T(8,128)(2,1)} %param.9) | copy-start | bytes 1966084
  51.0 15.7 %collective-permute-start.2 = (bf16[80,2560]{1,0:T(8,128)(2,1)}, bf16[80,2560]{1,0:T(8,128)(2,1)S(1)}, u32[]{:S(2)}, u32[]{:S(2)}) collective-permute-start(bf16[80,2560]{1,0:T(8,128)(2,1)} %collective-permute-done.1), channel_id=1, source_target_pairs={{0,8},{8,0},{1,9},{9,1},{2,10},{10,2},{3,11},{11,3},{4,12},{12,4},... | collective-permute-start | bytes 1228808 | tf_op jit(solution)/shard_map/ppermute | solution.py:33
  67.9 7.2 %copy-start = (bf16[768,2560]{1,0:T(8,128)(2,1)S(1)}, bf16[768,2560]{1,0:T(8,128)(2,1)}, u32[]{:S(2)}) copy-start(bf16[768,2560]{1,0:T(8,128)(2,1)} %constant_dynamic-update-slice_fusion.2) | copy-start | bytes 11796484
  68.2 19.5 %collective-permute-start.6 = (bf16[128,2560]{1,0:T(8,128)(2,1)S(1)}, bf16[128,2560]{1,0:T(8,128)(2,1)S(1)}, u32[]{:S(2)}, u32[]{:S(2)}) collective-permute-start(bf16[128,2560]{1,0:T(8,128)(2,1)S(1)} %slice.45), channel_id=1, source_target_pairs={{0,1},{1,2},{2,3},{3,0},{4,5},{5,6},{6,7},{7,4},{8,9},{9,10},{10,1... | collective-permute-start | bytes 1966088 | tf_op jit(solution)/shard_map/ppermute | solution.py:33
  71.7 17.7 %collective-permute-start.7 = (bf16[128,2560]{1,0:T(8,128)(2,1)S(1)}, bf16[128,2560]{1,0:T(8,128)(2,1)S(1)}, u32[]{:S(2)}, u32[]{:S(2)}) collective-permute-start(bf16[128,2560]{1,0:T(8,128)(2,1)S(1)} %slice.46), channel_id=1, source_target_pairs={{0,3},{1,0},{2,1},{3,2},{4,7},{5,4},{6,5},{7,6},{8,11},{9,8},{10,9... | collective-permute-start | bytes 1966088 | tf_op jit(solution)/shard_map/ppermute | solution.py:33
  75.2 16.1 %copy-start.1 = (bf16[768,2560]{1,0:T(8,128)(2,1)}, bf16[768,2560]{1,0:T(8,128)(2,1)S(1)}, u32[]{:S(2)}) copy-start(bf16[768,2560]{1,0:T(8,128)(2,1)S(1)} %constant_dynamic-update-slice_fusion) | copy-start | bytes 11796484
  78.7 12.6 %copy-start.3 = (bf16[320,768]{1,0:T(8,128)(2,1)}, bf16[320,768]{1,0:T(8,128)(2,1)S(1)}, u32[]{:S(2)}) copy-start(bf16[320,768]{1,0:T(8,128)(2,1)S(1)} %get-tuple-element.16) | copy-start | bytes 1474564
  78.7 12.6 %copy-start.5 = (bf16[320,768]{1,0:T(8,128)(2,1)}, bf16[320,768]{1,0:T(8,128)(2,1)S(1)}, u32[]{:S(2)}) copy-start(bf16[320,768]{1,0:T(8,128)(2,1)S(1)} %get-tuple-element.17) | copy-start | bytes 1474564
  94.6 9.0 %collective-permute-start.8 = (f32[320,2560]{1,0:T(8,128)}, f32[320,2560]{1,0:T(8,128)}, u32[]{:S(2)}, u32[]{:S(2)}) collective-permute-start(f32[320,2560]{1,0:T(8,128)} %convolution_add_fusion), channel_id=1, source_target_pairs={{0,8},{8,0},{1,9},{9,1},{2,10},{10,2},{3,11},{11,3},{4,12},{12,4},... | collective-permute-start | bytes 9830408 | tf_op jit(solution)/shard_map/ppermute | solution.py:33
  97.9 5.7 %copy-start.2 = (bf16[768,2560]{1,0:T(8,128)(2,1)S(1)}, bf16[768,2560]{1,0:T(8,128)(2,1)}, u32[]{:S(2)}) copy-start(bf16[768,2560]{1,0:T(8,128)(2,1)} %copy-done.1) | copy-start | bytes 11796484
  97.9 5.7 %copy-start.4 = (bf16[320,768]{1,0:T(8,128)(2,1)S(1)}, bf16[320,768]{1,0:T(8,128)(2,1)}, u32[]{:S(2)}) copy-start(bf16[320,768]{1,0:T(8,128)(2,1)} %copy-done.3) | copy-start | bytes 1474564
  97.9 5.7 %copy-start.6 = (bf16[320,768]{1,0:T(8,128)(2,1)S(1)}, bf16[320,768]{1,0:T(8,128)(2,1)}, u32[]{:S(2)}) copy-start(bf16[320,768]{1,0:T(8,128)(2,1)} %copy-done.5) | copy-start | bytes 1474564
  111.0 93.2 %copy-start.8 = (bf16[160,2560]{1,0:T(8,128)(2,1)S(1)}, bf16[160,2560]{1,0:T(8,128)(2,1)}, u32[]{:S(2)}) copy-start(bf16[160,2560]{1,0:T(8,128)(2,1)} %param.10) | copy-start | bytes 2457604
  111.0 26.5 %collective-permute-start.10 = (bf16[8,100,128]{2,1,0:T(8,128)(2,1)S(1)}, bf16[8,100,128]{2,1,0:T(8,128)(2,1)S(1)}, u32[]{:S(2)}, u32[]{:S(2)}) collective-permute-start(bf16[8,100,128]{2,1,0:T(8,128)(2,1)S(1)} %get-tuple-element.13), channel_id=1, source_target_pairs={{0,32},{16,48},{32,64},{48,80},{64,96},{80,112},{96,0},{112,16},{1... | collective-permute-start | bytes 614408 | tf_op jit(solution)/shard_map/ppermute | solution.py:33
  117.0 34.6 %collective-permute-start.11 = (bf16[8,100,128]{2,1,0:T(8,128)(2,1)S(1)}, bf16[8,100,128]{2,1,0:T(8,128)(2,1)S(1)}, u32[]{:S(2)}, u32[]{:S(2)}) collective-permute-start(bf16[8,100,128]{2,1,0:T(8,128)(2,1)S(1)} %get-tuple-element.12), channel_id=1, source_target_pairs={{0,48},{16,64},{32,80},{48,96},{64,112},{80,0},{96,16},{112,32},{1... | collective-permute-start | bytes 614408 | tf_op jit(solution)/shard_map/ppermute | solution.py:33
  124.9 29.0 %collective-permute-start.12 = (bf16[8,100,128]{2,1,0:T(8,128)(2,1)S(1)}, bf16[8,100,128]{2,1,0:T(8,128)(2,1)S(1)}, u32[]{:S(2)}, u32[]{:S(2)}) collective-permute-start(bf16[8,100,128]{2,1,0:T(8,128)(2,1)S(1)} %get-tuple-element.11), channel_id=1, source_target_pairs={{0,64},{16,80},{32,96},{48,112},{64,0},{80,16},{96,32},{112,48},{1... | collective-permute-start | bytes 614408 | tf_op jit(solution)/shard_map/ppermute | solution.py:33
  128.7 25.2 %collective-permute-start.13 = (bf16[8,100,128]{2,1,0:T(8,128)(2,1)S(1)}, bf16[8,100,128]{2,1,0:T(8,128)(2,1)S(1)}, u32[]{:S(2)}, u32[]{:S(2)}) collective-permute-start(bf16[8,100,128]{2,1,0:T(8,128)(2,1)S(1)} %get-tuple-element.10), channel_id=1, source_target_pairs={{0,80},{16,96},{32,112},{48,0},{64,16},{80,32},{96,48},{112,64},{1... | collective-permute-start | bytes 614408 | tf_op jit(solution)/shard_map/ppermute | solution.py:33
  134.2 30.1 %collective-permute-start.14 = (bf16[8,100,128]{2,1,0:T(8,128)(2,1)S(1)}, bf16[8,100,128]{2,1,0:T(8,128)(2,1)S(1)}, u32[]{:S(2)}, u32[]{:S(2)}) collective-permute-start(bf16[8,100,128]{2,1,0:T(8,128)(2,1)S(1)} %get-tuple-element.15), channel_id=1, source_target_pairs={{0,96},{16,112},{32,0},{48,16},{64,32},{80,48},{96,64},{112,80},{1... | collective-permute-start | bytes 614408 | tf_op jit(solution)/shard_map/ppermute | solution.py:33
  137.6 28.3 %collective-permute-start.15 = (bf16[8,100,128]{2,1,0:T(8,128)(2,1)S(1)}, bf16[8,100,128]{2,1,0:T(8,128)(2,1)S(1)}, u32[]{:S(2)}, u32[]{:S(2)}) collective-permute-start(bf16[8,100,128]{2,1,0:T(8,128)(2,1)S(1)} %get-tuple-element.14), channel_id=1, source_target_pairs={{0,112},{16,0},{32,16},{48,32},{64,48},{80,64},{96,80},{112,96},{1... | collective-permute-start | bytes 614408 | tf_op jit(solution)/shard_map/ppermute | solution.py:33
  151.5 14.3 %collective-permute-start.9 = (bf16[8,100,128]{2,1,0:T(8,128)(2,1)S(1)}, bf16[8,100,128]{2,1,0:T(8,128)(2,1)S(1)}, u32[]{:S(2)}, u32[]{:S(2)}) collective-permute-start(bf16[8,100,128]{2,1,0:T(8,128)(2,1)S(1)} %get-tuple-element.9), channel_id=1, source_target_pairs={{0,16},{16,32},{32,48},{48,64},{64,80},{80,96},{96,112},{112,0},{1... | collective-permute-start | bytes 614408 | tf_op jit(solution)/shard_map/ppermute | solution.py:33
  167.1 20.6 %collective-permute-start.16 = (f32[100,128]{1,0:T(8,128)S(1)}, f32[100,128]{1,0:T(8,128)S(1)}, u32[]{:S(2)}, u32[]{:S(2)}) collective-permute-start(f32[100,128]{1,0:T(8,128)S(1)} %get-tuple-element.32), channel_id=1, source_target_pairs={{0,128},{128,256},{256,384},{384,4},{4,132},{132,260},{260,388},{3... | collective-permute-start | bytes 153608 | tf_op jit(solution)/shard_map/ppermute | solution.py:32
  170.7 22.3 %collective-permute-start.17 = (f32[100,128]{1,0:T(8,128)S(1)}, f32[100,128]{1,0:T(8,128)S(1)}, u32[]{:S(2)}, u32[]{:S(2)}) collective-permute-start(f32[100,128]{1,0:T(8,128)S(1)} %get-tuple-element.38), channel_id=1, source_target_pairs={{0,256},{128,384},{256,4},{384,132},{4,260},{132,388},{260,0},{388... | collective-permute-start | bytes 153608 | tf_op jit(solution)/shard_map/ppermute | solution.py:32
  173.9 22.4 %collective-permute-start.18 = (f32[100,128]{1,0:T(8,128)S(1)}, f32[100,128]{1,0:T(8,128)S(1)}, u32[]{:S(2)}, u32[]{:S(2)}) collective-permute-start(f32[100,128]{1,0:T(8,128)S(1)} %get-tuple-element.37), channel_id=1, source_target_pairs={{0,384},{128,4},{256,132},{384,260},{4,388},{132,0},{260,128},{388... | collective-permute-start | bytes 153608 | tf_op jit(solution)/shard_map/ppermute | solution.py:32
  179.4 16.9 %collective-permute-start.19 = (f32[100,128]{1,0:T(8,128)S(1)}, f32[100,128]{1,0:T(8,128)S(1)}, u32[]{:S(2)}, u32[]{:S(2)}) collective-permute-start(f32[100,128]{1,0:T(8,128)S(1)} %get-tuple-element.36), channel_id=1, source_target_pairs={{0,4},{128,132},{256,260},{384,388},{4,0},{132,128},{260,256},{388... | collective-permute-start | bytes 153608 | tf_op jit(solution)/shard_map/ppermute | solution.py:32
  183.4 13.0 %collective-permute-start.20 = (f32[100,128]{1,0:T(8,128)S(1)}, f32[100,128]{1,0:T(8,128)S(1)}, u32[]{:S(2)}, u32[]{:S(2)}) collective-permute-start(f32[100,128]{1,0:T(8,128)S(1)} %get-tuple-element.35), channel_id=1, source_target_pairs={{0,132},{128,260},{256,388},{384,0},{4,128},{132,256},{260,384},{3... | collective-permute-start | bytes 153608 | tf_op jit(solution)/shard_map/ppermute | solution.py:32
  187.7 8.6 %collective-permute-start.21 = (f32[100,128]{1,0:T(8,128)S(1)}, f32[100,128]{1,0:T(8,128)S(1)}, u32[]{:S(2)}, u32[]{:S(2)}) collective-permute-start(f32[100,128]{1,0:T(8,128)S(1)} %get-tuple-element.34), channel_id=1, source_target_pairs={{0,260},{128,388},{256,0},{384,128},{4,256},{132,384},{260,4},{388... | collective-permute-start | bytes 153608 | tf_op jit(solution)/shard_map/ppermute | solution.py:32
  193.0 5.0 %collective-permute-start.22 = (f32[100,128]{1,0:T(8,128)S(1)}, f32[100,128]{1,0:T(8,128)S(1)}, u32[]{:S(2)}, u32[]{:S(2)}) collective-permute-start(f32[100,128]{1,0:T(8,128)S(1)} %get-tuple-element.33), channel_id=1, source_target_pairs={{0,388},{128,0},{256,128},{384,256},{4,384},{132,4},{260,132},{388... | collective-permute-start | bytes 153608 | tf_op jit(solution)/shard_map/ppermute | solution.py:32
  198.0 8.6 %collective-permute-start.23 = (f32[50,128]{1,0:T(8,128)S(1)}, f32[50,128]{1,0:T(8,128)S(1)}, u32[]{:S(2)}, u32[]{:S(2)}) collective-permute-start(f32[50,128]{1,0:T(8,128)S(1)} %constant_dynamic-slice_fusion.2), channel_id=1, source_target_pairs={{0,8},{8,0},{1,9},{9,1},{2,10},{10,2},{3,11},{11,3},{4,12},{12,4},... | collective-permute-start | bytes 76808 | tf_op jit(solution)/shard_map/ppermute | solution.py:33
  206.4 0.8 copy-start.12
  206.5 0.8 copy-start.13
  208.6 7.2 %collective-permute-start.24 = (bf16[50,128]{1,0:T(8,128)(2,1)S(1)}, bf16[50,128]{1,0:T(8,128)(2,1)S(1)}, u32[]{:S(2)}, u32[]{:S(2)}) collective-permute-start(bf16[50,128]{1,0:T(8,128)(2,1)S(1)} %get-tuple-element.6), channel_id=1, source_target_pairs={{0,384},{128,0},{256,128},{384,256},{1,385},{129,1},{257,129},{385... | collective-permute-start | bytes 38408 | tf_op jit(solution)/shard_map/ppermute | solution.py:33
  210.6 5.4 %collective-permute-start.25 = (bf16[50,128]{1,0:T(8,128)(2,1)S(1)}, bf16[50,128]{1,0:T(8,128)(2,1)S(1)}, u32[]{:S(2)}, u32[]{:S(2)}) collective-permute-start(bf16[50,128]{1,0:T(8,128)(2,1)S(1)} %get-tuple-element.6), channel_id=1, source_target_pairs={{0,256},{128,384},{256,0},{384,128},{1,257},{129,385},{257,1},{385... | collective-permute-start | bytes 38408 | tf_op jit(solution)/shard_map/ppermute | solution.py:33
  213.0 6.3 %collective-permute-start.26 = (bf16[50,128]{1,0:T(8,128)(2,1)S(1)}, bf16[50,128]{1,0:T(8,128)(2,1)S(1)}, u32[]{:S(2)}, u32[]{:S(2)}) collective-permute-start(bf16[50,128]{1,0:T(8,128)(2,1)S(1)} %get-tuple-element.6), channel_id=1, source_target_pairs={{0,128},{128,256},{256,384},{384,0},{1,129},{129,257},{257,385},{3... | collective-permute-start | bytes 38408 | tf_op jit(solution)/shard_map/ppermute | solution.py:33
  219.4 19.9 %collective-permute-start.27 = (bf16[4,50,128]{2,1,0:T(8,128)(2,1)S(1)}, bf16[4,50,128]{2,1,0:T(8,128)(2,1)S(1)}, u32[]{:S(2)}, u32[]{:S(2)}) collective-permute-start(bf16[4,50,128]{2,1,0:T(8,128)(2,1)S(1)} %get-tuple-element.4), channel_id=1, source_target_pairs={{0,112},{16,0},{32,16},{48,32},{64,48},{80,64},{96,80},{112,96},{1... | collective-permute-start | bytes 153608 | tf_op jit(solution)/shard_map/ppermute | solution.py:33
  223.7 20.6 %collective-permute-start.28 = (bf16[4,50,128]{2,1,0:T(8,128)(2,1)S(1)}, bf16[4,50,128]{2,1,0:T(8,128)(2,1)S(1)}, u32[]{:S(2)}, u32[]{:S(2)}) collective-permute-start(bf16[4,50,128]{2,1,0:T(8,128)(2,1)S(1)} %get-tuple-element.4), channel_id=1, source_target_pairs={{0,96},{16,112},{32,0},{48,16},{64,32},{80,48},{96,64},{112,80},{1... | collective-permute-start | bytes 153608 | tf_op jit(solution)/shard_map/ppermute | solution.py:33
  226.8 19.4 %collective-permute-start.29 = (bf16[4,50,128]{2,1,0:T(8,128)(2,1)S(1)}, bf16[4,50,128]{2,1,0:T(8,128)(2,1)S(1)}, u32[]{:S(2)}, u32[]{:S(2)}) collective-permute-start(bf16[4,50,128]{2,1,0:T(8,128)(2,1)S(1)} %get-tuple-element.4), channel_id=1, source_target_pairs={{0,80},{16,96},{32,112},{48,0},{64,16},{80,32},{96,48},{112,64},{1... | collective-permute-start | bytes 153608 | tf_op jit(solution)/shard_map/ppermute | solution.py:33
  231.7 14.6 %collective-permute-start.30 = (bf16[4,50,128]{2,1,0:T(8,128)(2,1)S(1)}, bf16[4,50,128]{2,1,0:T(8,128)(2,1)S(1)}, u32[]{:S(2)}, u32[]{:S(2)}) collective-permute-start(bf16[4,50,128]{2,1,0:T(8,128)(2,1)S(1)} %get-tuple-element.4), channel_id=1, source_target_pairs={{0,64},{16,80},{32,96},{48,112},{64,0},{80,16},{96,32},{112,48},{1... | collective-permute-start | bytes 153608 | tf_op jit(solution)/shard_map/ppermute | solution.py:33
  235.2 11.1 %collective-permute-start.31 = (bf16[4,50,128]{2,1,0:T(8,128)(2,1)S(1)}, bf16[4,50,128]{2,1,0:T(8,128)(2,1)S(1)}, u32[]{:S(2)}, u32[]{:S(2)}) collective-permute-start(bf16[4,50,128]{2,1,0:T(8,128)(2,1)S(1)} %get-tuple-element.4), channel_id=1, source_target_pairs={{0,48},{16,64},{32,80},{48,96},{64,112},{80,0},{96,16},{112,32},{1... | collective-permute-start | bytes 153608 | tf_op jit(solution)/shard_map/ppermute | solution.py:33
  239.3 9.2 %collective-permute-start.32 = (bf16[4,50,128]{2,1,0:T(8,128)(2,1)S(1)}, bf16[4,50,128]{2,1,0:T(8,128)(2,1)S(1)}, u32[]{:S(2)}, u32[]{:S(2)}) collective-permute-start(bf16[4,50,128]{2,1,0:T(8,128)(2,1)S(1)} %get-tuple-element.4), channel_id=1, source_target_pairs={{0,32},{16,48},{32,64},{48,80},{64,96},{80,112},{96,0},{112,16},{1... | collective-permute-start | bytes 153608 | tf_op jit(solution)/shard_map/ppermute | solution.py:33
  244.3 7.1 %collective-permute-start.33 = (bf16[4,50,128]{2,1,0:T(8,128)(2,1)S(1)}, bf16[4,50,128]{2,1,0:T(8,128)(2,1)S(1)}, u32[]{:S(2)}, u32[]{:S(2)}) collective-permute-start(bf16[4,50,128]{2,1,0:T(8,128)(2,1)S(1)} %get-tuple-element.4), channel_id=1, source_target_pairs={{0,16},{16,32},{32,48},{48,64},{64,80},{80,96},{96,112},{112,0},{1... | collective-permute-start | bytes 153608 | tf_op jit(solution)/shard_map/ppermute | solution.py:33
  251.6 6.9 %collective-permute-start.34 = (bf16[8,4,50,128]{3,2,1,0:T(8,128)(2,1)S(1)}, bf16[8,4,50,128]{3,2,1,0:T(8,128)(2,1)S(1)}, u32[]{:S(2)}, u32[]{:S(2)}) collective-permute-start(bf16[8,4,50,128]{3,2,1,0:T(8,128)(2,1)S(1)} %constant_dynamic-slice_fusion), channel_id=1, source_target_pairs={{0,8},{8,0},{1,9},{9,1},{2,10},{10,2},{3,11},{11,3},{4,12},{12,4},... | collective-permute-start | bytes 1228808 | tf_op jit(solution)/shard_map/ppermute | solution.py:33

commit v2 on v1

v2 whole, which is shorter than its diff:
```python
import math

import jax
import jax.numpy as jnp
from jax import lax
from jax.sharding import Mesh, PartitionSpec as P


OPT_STEP = 10


beta_one = 0.9
beta_two = 0.999
learn_rate = 0.15
epsilon = 0.0001


def size(axis):
    return 8 if axis == "y" else lax.axis_size(axis)


def shift(value, axis, by):
    n = size(axis)
    hops = [(i, (i + by) % n) for i in range(n)]
    if axis == "y":
        at = [2 * (y % 4) + y // 4 for y in range(n)]
        return lax.ppermute(value, ("yl", "yh"), [(at[i], at[j]) for i, j in hops])
    return lax.ppermute(value, axis, hops)


def unpack_signs(signs):
    shifts = jnp.arange(32, dtype=jnp.int32)
    bit_values = jnp.bitwise_and(jnp.right_shift(signs[:, None, :], shifts[None, :, None]), 1)
    return (1 - 2 * bit_values).reshape(signs.shape[0] * 32, signs.shape[1]).astype(jnp.bfloat16)


def step(hidden, resid, target, w_out, signs, m_old, v_old):
    features, width = w_out.shape
    tokens = hidden.shape[0]
    group = tokens * lax.axis_size("x")
    half = lax.axis_index("yh")
    core = lax.axis_index("c")
    col = lax.axis_index("x")
    odd = lax.axis_index("z") % 2

    from_left = shift(hidden, "x", 1)
    from_right = shift(hidden, "x", -1)

    quarter = features // 4
    piece = lax.dynamic_slice_in_dim(w_out, (core * 2 + odd) * quarter, quarter, 0)
    piece = shift(piece, "yh", 1)
    other_signs = shift(signs, "yh", 1)
    pair = jnp.stack([resid, target])
    other_pair = shift(lax.dynamic_slice_in_dim(pair, (1 - half) * group, group, 2), "yh", 1)
    beside = lax.ppermute(piece, "z", [(i, i ^ 1) for i in range(8)])
    part = jnp.concatenate(
        [jnp.where(odd == 0, piece, beside), jnp.where(odd == 0, beside, piece)], axis=0
    )
    twin = shift(part, "c", 1)
    other_w = jnp.concatenate(
        [jnp.where(core == 0, part, twin), jnp.where(core == 0, twin, part)], axis=0
    )
    far_top = shift(from_left[: tokens // 2], "x", 1)
    far_low = shift(from_right[tokens // 2 :], "x", -1)

    probes = unpack_signs(signs)
    other_probes = unpack_signs(other_signs)
    own_pair = lax.dynamic_slice_in_dim(pair, half * group, group, 2)

    def in_order(own, other):
        first = jnp.where(half == 0, own, other)
        second = jnp.where(half == 0, other, own)
        return jnp.concatenate([first, second], axis=0)

    stacked = jnp.concatenate([in_order(w_out, other_w), in_order(probes, other_probes)], axis=0)
    pair_all = jnp.concatenate(
        [jnp.where(half == 0, own_pair, other_pair), jnp.where(half == 0, other_pair, own_pair)], axis=1
    )
    count = 2 * features

    each = m_old.shape[0]
    row_start = (
        (lax.axis_index("yl") * lax.axis_size("z") + lax.axis_index("z")) * 2 + core
    ) * each
    my_probes = lax.dynamic_slice_in_dim(probes.reshape(-1, 128), row_start, each, 0)
    own_rows = lax.dynamic_slice_in_dim(w_out.reshape(-1, 128), row_start, each, 0)

    def run(block, places):
        cols = [lax.dynamic_slice_in_dim(pair_all, ((col + k) % 4) * tokens, tokens, 2) for k in places]
        here = jnp.concatenate(cols, axis=2) if len(cols) > 1 else cols[0]
        forward = lax.dot_general(
            stacked, block, (((1,), (1,)), ((), ())), preferred_element_type=jnp.float32
        )
        misfit = here[0].astype(jnp.float32) + forward[:count] - here[1].astype(jnp.float32)
        spread = 1.0 + misfit * misfit
        rooted = jnp.sqrt(spread)
        slopes = (misfit / rooted).astype(jnp.bfloat16)
        bends = (forward[count:] / (spread * rooted)).astype(jnp.bfloat16)
        away = jnp.where(core == 0, bends, slopes)
        kept = jnp.where(core == 0, slopes, bends)
        return away, kept

    near = jnp.concatenate([hidden, from_left, from_right], axis=0)
    away_near, kept_near = run(near, (0, 3, 1))
    sum_away = jnp.dot(away_near, near, preferred_element_type=jnp.float32)
    sum_kept = jnp.dot(kept_near, near, preferred_element_type=jnp.float32)
    sum_away, sum_kept, far_top, far_low, my_probes, own_rows = lax.optimization_barrier(
        (sum_away, sum_kept, far_top, far_low, my_probes, own_rows)
    )
    far = jnp.concatenate([far_top, far_low], axis=0)
    away_far, kept_far = run(far, (2,))
    sum_away = sum_away + jnp.dot(away_far, far, preferred_element_type=jnp.float32)
    got = shift(sum_away, "c", 1)
    sum_kept = sum_kept + jnp.dot(kept_far, far, preferred_element_type=jnp.float32)
    mine = (sum_kept + got).astype(jnp.bfloat16)

    plane = 64
    pieces = mine.reshape(plane, count * width // (plane * 128), 128)
    terms = lax.all_to_all(pieces, ("yh", "yl", "z"), 0, 0, tiled=True)
    total = jnp.sum(terms.astype(jnp.float32), axis=0)
    keep_rows = lax.dynamic_slice_in_dim(total, core * each, each, 0)
    send_rows = lax.dynamic_slice_in_dim(total, (1 - core) * each, each, 0)
    got_rows = shift(send_rows, "c", 1)
    grad_mine = jnp.where(core == 0, keep_rows, got_rows)
    curve_mine = jnp.where(core == 0, got_rows, keep_rows)

    scaling = 1.0 / math.sqrt(tokens * 512)
    gradient = grad_mine * scaling
    curvature = curve_mine * scaling
    diag_est = my_probes.astype(jnp.float32) * curvature
    new_m = beta_one * m_old + (1.0 - beta_one) * gradient
    new_v = beta_two * v_old + (1.0 - beta_two) * diag_est * diag_est
    first_fix = 1.0 - beta_one**OPT_STEP
    second_fix = 1.0 - beta_two**OPT_STEP
    update = new_m / first_fix / (jnp.sqrt(new_v / second_fix) + epsilon)
    fresh = (own_rows.astype(jnp.float32) - learn_rate * update).astype(jnp.bfloat16)

    spread_rows = jnp.broadcast_to(fresh[None], (32, *fresh.shape))
    mine_rows = lax.all_to_all(spread_rows, ("yl", "z"), 0, 0, tiled=True)
    twin_rows = shift(mine_rows, "c", 1)
    both = jnp.stack(
        [jnp.where(core == 0, mine_rows, twin_rows), jnp.where(core == 0, twin_rows, mine_rows)], axis=1
    )
    new_w = both.reshape(w_out.shape)
    return (new_w, new_m, new_v)


def solution(mesh):
    fine = Mesh(mesh.devices.reshape(4, 8, 2, 2, 4), ("yl", "z", "c", "yh", "x"))
    dp, shard = ("yl", "z", "c"), ("yh", "x")
    return jax.shard_map(
        step,
        mesh=fine,
        in_specs=(
            P(dp + shard, None),
            P(shard, dp),
            P(shard, dp),
            P(shard, None),
            P(shard, None),
            P(shard + dp, None),
            P(shard + dp, None),
        ),
        out_specs=(P(shard, None), P(shard + dp, None), P(shard + dp, None)),
        check_vma=False,
    )
```

time: 262 us -> 192 us (0.73)
  starting transfers between devices: 153 us -> 79.3 us
  blocking collectives: 0 us -> 21.7 us
  waiting for transfers between devices: 70.9 us -> 53 us
  local copies, waits for them, and re-layouts: 13 us -> 16.9 us
  matrix products: 11.6 us -> 7.83 us
    ppermute x28 -> x11, starting transfers between devices: 124 us -> 61.4 us  [shift(): return lax.ppermute(value, axis, hops)]
    ppermute x28 -> x11, waiting for transfers between devices: 69.3 us -> 12.1 us  [shift(): return lax.ppermute(value, axis, hops)]
    all_to_all x0 -> x1, waiting for transfers between devices: none -> 40.9 us  [step(): terms = lax.all_to_all(pieces, ('yh', 'yl', 'z'), 0, 0, tiled=True)]
    ppermute x7 -> x1, starting transfers between devices: 29.1 us -> 3.99 us  [step(): beside = lax.ppermute(piece, 'z', [(i, i ^ 1) for i in range(8)])]
    all_to_all x0 -> x1, blocking collectives: none -> 21.7 us  [step(): mine_rows = lax.all_to_all(spread_rows, ('yl', 'z'), 0, 0, tiled=True)]
    all_to_all x0 -> x1, starting transfers between devices: none -> 13.9 us  [step(): terms = lax.all_to_all(pieces, ('yh', 'yl', 'z'), 0, 0, tiled=True)]
    dot_general x4, matrix products: 7.81 us -> 4.06 us  [the longest x1 1.43 us: step(): sum_away = jnp.dot(away_near, near, preferred_element_type=jnp.float32)]
  transfers between devices with their start and end apart: 35 -> 13, of which waited for: 13 -> 7; matrix products, arithmetic and copies ran while one was open for 6% -> 14% of each run, Pallas kernels for 0% -> 0%
where the time goes in v2:
time: 192 us; the launch traced here: 191 us
  starting transfers between devices  79.3 us (41%)
  waiting for transfers between devices  53 us (28%)
  blocking collectives  21.7 us (11%)
  local copies, waits for them, and re-layouts  16.9 us (9%)
  other arithmetic  11.3 us (6%)
  matrix products  7.83 us (4%)
    ppermute x11, starting transfers between devices, shift(): return lax.ppermute(value, axis, hops)  61.4 us
    all_to_all x1, waiting for transfers between devices, step(): terms = lax.all_to_all(pieces, ('yh', 'yl', 'z'), 0, 0, tiled=True)  40.9 us
    all_to_all x1, blocking collectives, step(): mine_rows = lax.all_to_all(spread_rows, ('yl', 'z'), 0, 0, tiled=True)  21.7 us
    all_to_all x1, starting transfers between devices, step(): terms = lax.all_to_all(pieces, ('yh', 'yl', 'z'), 0, 0, tiled=True)  13.9 us
    ppermute x11, waiting for transfers between devices, shift(): return lax.ppermute(value, axis, hops)  12.1 us
    ppermute x1, starting transfers between devices, step(): beside = lax.ppermute(piece, 'z', [(i, i ^ 1) for i in range(8)])  3.99 us
  transfers between devices with their start and end apart: 13, of which 7 were waited for; matrix products, arithmetic and copies ran while one was open for 14% of the time, Pallas kernels for 0%

profile of v2, /device:TPU:1, one launch (start us, length us, event | category | flops | bytes accessed | tf_op | source)
XLA Modules:
  0.0 191.2 jit_solution(8453890139324700311)
XLA Ops:
  0.6 4.1 %collective-permute-start.4 = (bf16[256,2560]{1,0:T(8,128)(2,1)}, bf16[256,2560]{1,0:T(8,128)(2,1)S(1)}, u32[]{:S(2)}, u32[]{:S(2)}) collective-permute-start(bf16[256,2560]{1,0:T(8,128)(2,1)} %param.7), channel_id=1, source_target_pairs={{0,1},{1,2},{2,3},{3,0},{4,5},{5,6},{6,7},{7,4},{8,9},{9,10},{10,1... | collective-permute-start | bytes 3932168 | tf_op jit(solution)/shard_map/ppermute | solution.py:28
  4.7 3.2 %collective-permute-start.5 = (bf16[256,2560]{1,0:T(8,128)(2,1)}, bf16[256,2560]{1,0:T(8,128)(2,1)}, u32[]{:S(2)}, u32[]{:S(2)}) collective-permute-start(bf16[256,2560]{1,0:T(8,128)(2,1)} %param.7), channel_id=1, source_target_pairs={{0,3},{1,0},{2,1},{3,2},{4,7},{5,4},{6,5},{7,6},{8,11},{9,8},{10,9... | collective-permute-start | bytes 3932168 | tf_op jit(solution)/shard_map/ppermute | solution.py:28
  7.9 7.6 %collective-permute-start.3 = (s32[5,2560]{1,0:T(8,128)}, s32[5,2560]{1,0:T(8,128)}, u32[]{:S(2)}, u32[]{:S(2)}) collective-permute-start(s32[5,2560]{1,0:T(8,128)} %param.11), channel_id=1, source_target_pairs={{0,4},{4,0},{1,5},{5,1},{2,6},{6,2},{3,7},{7,3},{8,12},{12,8},{9,1... | collective-permute-start | bytes 153608 | tf_op jit(solution)/shard_map/ppermute | solution.py:28
  15.6 0.9 constant_dynamic-slice_fusion.2
  16.5 1.9 %collective-permute-start = (bf16[40,2560]{1,0:T(8,128)(2,1)S(1)}, bf16[40,2560]{1,0:T(8,128)(2,1)}, u32[]{:S(2)}, u32[]{:S(2)}) collective-permute-start(bf16[40,2560]{1,0:T(8,128)(2,1)S(1)} %constant_dynamic-slice_fusion.2), channel_id=1, source_target_pairs={{0,4},{4,0},{1,5},{5,1},{2,6},{6,2},{3,7},{7,3},{8,12},{12,8},{9,1... | collective-permute-start | bytes 614408 | tf_op jit(solution)/shard_map/ppermute | solution.py:28
  18.5 1.9 %fusion.14 = bf16[2,160,1024]{2,1,0:T(8,128)(2,1)} fusion(s32[]{:T(128)S(6)} %select_n.175, bf16[1,160,2048]{2,1,0:T(8,128)(2,1)} %bitcast.78, bf16[1,160,2048]{2,1,0:T(8,128)(2,1)} %bitcast.80), kind=kLoop, calls=%fused_computation.40 | loop fusion | flops 1310720 | bytes 1966084 | tf_op jit(solution)/shard_map/stack | solution.py:53
  20.4 7.3 %collective-permute-start.6 = (bf16[2,160,1024]{2,1,0:T(8,128)(2,1)}, bf16[2,160,1024]{2,1,0:T(8,128)(2,1)}, u32[]{:S(2)}, u32[]{:S(2)}) collective-permute-start(bf16[2,160,1024]{2,1,0:T(8,128)(2,1)} %fusion.14), channel_id=1, source_target_pairs={{0,4},{4,0},{1,5},{5,1},{2,6},{6,2},{3,7},{7,3},{8,12},{12,8},{9,1... | collective-permute-start | bytes 1966088 | tf_op jit(solution)/shard_map/ppermute | solution.py:28
  27.7 0.6 shift_right_arithmetic.58
  28.4 0.8 shift_right_arithmetic.65
  29.1 0.1 shift_right_arithmetic.66
  29.2 0.2 shift_right_arithmetic.55
  29.4 1.3 shift_right_arithmetic.64
  30.7 0.1 dynamic-slice
  30.8 2.5 %constant_dynamic-update-slice_fusion.2 = bf16[768,2560]{1,0:T(8,128)(2,1)} fusion(bf16[256,2560]{1,0:T(8,128)(2,1)} %param.7), kind=kLoop, calls=%fused_computation.92 | loop fusion | bytes 2621440
  33.3 4.0 %collective-permute-start.1 = (bf16[40,2560]{1,0:T(8,128)(2,1)}, bf16[40,2560]{1,0:T(8,128)(2,1)}, u32[]{:S(2)}, u32[]{:S(2)}) collective-permute-start(bf16[40,2560]{1,0:T(8,128)(2,1)} %collective-permute-done), channel_id=1, source_target_pairs={{0,16},{16,0},{32,48},{48,32},{64,80},{80,64},{96,112},{112,96},{1... | collective-permute-start | bytes 614408 | tf_op jit(solution)/shard_map/ppermute | solution.py:55
  37.3 0.8 fusion.42
  38.2 1.9 reshape.35
  40.1 0.8 constant_dynamic-slice_fusion.1
  40.9 0.0 collective-permute-done.3
  40.9 1.6 fusion.13
  42.6 0.0 collective-permute-done.1
  42.6 1.1 broadcast_select_fusion.7
  43.7 15.6 %collective-permute-start.2 = (bf16[80,2560]{1,0:T(8,128)(2,1)S(1)}, bf16[80,2560]{1,0:T(8,128)(2,1)S(1)}, u32[]{:S(2)}, u32[]{:S(2)}) collective-permute-start(bf16[80,2560]{1,0:T(8,128)(2,1)S(1)} %pad_maximum_fusion.6), channel_id=1, source_target_pairs={{0,8},{8,0},{1,9},{9,1},{2,10},{10,2},{3,11},{11,3},{4,12},{12,4},... | collective-permute-start | bytes 1228808 | tf_op jit(solution)/shard_map/ppermute | solution.py:28
  59.3 1.2 collective-permute-done.6
  60.5 1.4 broadcast_select_fusion.2
  61.9 0.2 fusion.27
  62.1 0.1 pad_maximum_fusion.1
  62.1 0.0 collective-permute-done.2
  62.1 0.1 broadcast_select_fusion.5
  62.3 0.3 broadcast_select_fusion.1
  62.6 0.0 collective-permute-done.4
  62.6 2.5 %collective-permute-start.7 = (bf16[128,2560]{1,0:T(8,128)(2,1)S(1)}, bf16[128,2560]{1,0:T(8,128)(2,1)S(1)}, u32[]{:S(2)}, u32[]{:S(2)}) collective-permute-start(bf16[128,2560]{1,0:T(8,128)(2,1)S(1)} %slice.44), channel_id=1, source_target_pairs={{0,1},{1,2},{2,3},{3,0},{4,5},{5,6},{6,7},{7,4},{8,9},{9,10},{10,1... | collective-permute-start | bytes 1966088 | tf_op jit(solution)/shard_map/ppermute | solution.py:28
  65.1 1.1 slice.45
  66.2 4.3 %collective-permute-start.8 = (bf16[128,2560]{1,0:T(8,128)(2,1)S(1)}, bf16[128,2560]{1,0:T(8,128)(2,1)S(1)}, u32[]{:S(2)}, u32[]{:S(2)}) collective-permute-start(bf16[128,2560]{1,0:T(8,128)(2,1)S(1)} %slice.45), channel_id=1, source_target_pairs={{0,3},{1,0},{2,1},{3,2},{4,7},{5,4},{6,5},{7,6},{8,11},{9,8},{10,9... | collective-permute-start | bytes 1966088 | tf_op jit(solution)/shard_map/ppermute | solution.py:28
  70.6 0.1 constant_dynamic-update-slice_fusion.1
  70.7 1.4 constant_dynamic-update-slice_fusion
  72.1 2.7 %fusion.17 = f32[640,768]{1,0:T(8,128)S(1)} fusion(bf16[768,2560]{1,0:T(8,128)(2,1)S(1)} %constant_dynamic-update-slice_fusion, bf16[160,2560]{1,0:T(8,128)(2,1)S(1)} %get-tuple-element.37, bf16[160,2560]{1,0:T(8,128)(2,1)S(1)} %get-tuple-element.36, bf16[160,2560]{1,0:T(8,128)(2,1)S(1)} %get-tuple-element.23, bf16[160,2560]{1,0:T(8,128)(2,1)S(1)} %get-tuple-element.22), kind=kOutput, calls=%fused_computation.45 | convolution fusion | flops 2529689600 | bytes 9175040 | tf_op jit(solution)/shard_map/dot_general | solution.py:91
  74.8 0.7 fusion.10
  75.5 1.4 fusion.18
  76.9 1.4 fusion.20
  78.4 1.9 %collective-permute-done.7 = bf16[128,2560]{1,0:T(8,128)(2,1)S(1)} collective-permute-done((bf16[128,2560]{1,0:T(8,128)(2,1)S(1)}, bf16[128,2560]{1,0:T(8,128)(2,1)S(1)}, u32[]{:S(2)}, u32[]{:S(2)}) %collective-permute-start.7) | collective-permute-done | bytes 655392 | tf_op jit(solution)/shard_map/ppermute | solution.py:28
  80.3 2.0 %collective-permute-done.8 = bf16[128,2560]{1,0:T(8,128)(2,1)S(1)} collective-permute-done((bf16[128,2560]{1,0:T(8,128)(2,1)S(1)}, bf16[128,2560]{1,0:T(8,128)(2,1)S(1)}, u32[]{:S(2)}, u32[]{:S(2)}) %collective-permute-start.8) | collective-permute-done | bytes 655392 | tf_op jit(solution)/shard_map/ppermute | solution.py:28
  82.5 1.0 fusion.16
  83.5 0.2 fusion.24
  83.7 0.6 fusion.32
  84.3 0.6 add.130
  84.9 5.2 %collective-permute-start.9 = (f32[320,2560]{1,0:T(8,128)S(1)}, f32[320,2560]{1,0:T(8,128)S(1)}, u32[]{:S(2)}, u32[]{:S(2)}) collective-permute-start(f32[320,2560]{1,0:T(8,128)S(1)} %add.130), channel_id=1, source_target_pairs={{0,8},{8,0},{1,9},{9,1},{2,10},{10,2},{3,11},{11,3},{4,12},{12,4},... | collective-permute-start | bytes 9830408 | tf_op jit(solution)/shard_map/ppermute | solution.py:28
  90.1 0.6 fusion.34
  90.7 4.7 %collective-permute-done.9 = f32[320,2560]{1,0:T(8,128)S(1)} collective-permute-done((f32[320,2560]{1,0:T(8,128)S(1)}, f32[320,2560]{1,0:T(8,128)S(1)}, u32[]{:S(2)}, u32[]{:S(2)}) %collective-permute-start.9) | collective-permute-done | bytes 3276832 | tf_op jit(solution)/shard_map/ppermute | solution.py:28
  95.4 1.0 add_convert_fusion
  96.5 3.0 %reshape.36 = bf16[64,100,128]{2,1,0:T(8,128)(2,1)} reshape(bf16[320,2560]{1,0:T(8,128)(2,1)S(1)} %add_convert_fusion) | data formatting | bytes 3276800 | tf_op jit(solution)/shard_map/reshape | solution.py:118
  99.5 13.9 %all-to-all-start = ((bf16[64,100,128]{2,1,0:T(8,128)(2,1)}), bf16[64,100,128]{2,1,0:T(8,128)(2,1)S(1)}, u32[]{:S(2)}, u32[]{:S(2)}) async-start(bf16[64,100,128]{2,1,0:T(8,128)(2,1)} %reshape.36), calls=%async_computation | async-start | bytes 3407872 | tf_op jit(solution)/shard_map/all_to_all | solution.py:119
  113.4 40.9 %all-to-all-done = bf16[64,100,128]{2,1,0:T(8,128)(2,1)S(1)} async-done(((bf16[64,100,128]{2,1,0:T(8,128)(2,1)}), bf16[64,100,128]{2,1,0:T(8,128)(2,1)S(1)}, u32[]{:S(2)}, u32[]{:S(2)}) %all-to-all-start) | async-done | bytes 1638432 | tf_op jit(solution)/shard_map/all_to_all | solution.py:119
  154.3 0.3 convert_reduce_fusion
  154.7 5.5 %collective-permute-start.10 = (f32[50,128]{1,0:T(8,128)S(1)}, f32[50,128]{1,0:T(8,128)S(1)}, u32[]{:S(2)}, u32[]{:S(2)}) collective-permute-start(f32[50,128]{1,0:T(8,128)S(1)} %constant_dynamic-slice_fusion), channel_id=1, source_target_pairs={{0,8},{8,0},{1,9},{9,1},{2,10},{10,2},{3,11},{11,3},{4,12},{12,4},... | collective-permute-start | bytes 76808 | tf_op jit(solution)/shard_map/ppermute | solution.py:28
  160.2 0.8 collective-permute-done.10
  161.0 0.6 subtract_convert_fusion
  161.7 0.1 broadcast_in_dim.2
  161.7 21.7 %all_to_all.10 = bf16[32,50,128]{2,1,0:T(8,128)(2,1)S(1)} all-to-all(bf16[32,50,128]{2,1,0:T(8,128)(2,1)S(1)} %broadcast_in_dim.2), channel_id=1, replica_groups=mesh['yl'=4,'z'=8,'c'=2,'yh'=2,'x'=4] {'yl','z'}, dimensions={0} | all-to-all | bytes 819200 | tf_op jit(solution)/shard_map/all_to_all | solution.py:139
  183.5 4.3 %collective-permute-start.11 = (bf16[32,50,128]{2,1,0:T(8,128)(2,1)S(1)}, bf16[32,50,128]{2,1,0:T(8,128)(2,1)S(1)}, u32[]{:S(2)}, u32[]{:S(2)}) collective-permute-start(bf16[32,50,128]{2,1,0:T(8,128)(2,1)S(1)} %all_to_all.10), channel_id=1, source_target_pairs={{0,8},{8,0},{1,9},{9,1},{2,10},{10,2},{3,11},{11,3},{4,12},{12,4},... | collective-permute-start | bytes 1228808 | tf_op jit(solution)/shard_map/ppermute | solution.py:28
  187.8 1.4 collective-permute-done.11
  189.2 0.1 select_bitcast_fusion.1
  189.3 0.1 pad_maximum_fusion.2
  189.4 1.8 reshape.37
  (22 shorter events, 0.2 us)
Async XLA Ops:
  0.6 28.6 %copy-start.4 = (s32[5,2560]{1,0:T(8,128)S(1)}, s32[5,2560]{1,0:T(8,128)}, u32[]{:S(2)}) copy-start(s32[5,2560]{1,0:T(8,128)} %param.11) | copy-start | bytes 153604
  0.6 61.9 %collective-permute-start.4 = (bf16[256,2560]{1,0:T(8,128)(2,1)}, bf16[256,2560]{1,0:T(8,128)(2,1)S(1)}, u32[]{:S(2)}, u32[]{:S(2)}) collective-permute-start(bf16[256,2560]{1,0:T(8,128)(2,1)} %param.7), channel_id=1, source_target_pairs={{0,1},{1,2},{2,3},{3,0},{4,5},{5,6},{6,7},{7,4},{8,9},{9,10},{10,1... | collective-permute-start | bytes 3932168 | tf_op jit(solution)/shard_map/ppermute | solution.py:28
  4.7 60.4 %collective-permute-start.5 = (bf16[256,2560]{1,0:T(8,128)(2,1)}, bf16[256,2560]{1,0:T(8,128)(2,1)}, u32[]{:S(2)}, u32[]{:S(2)}) collective-permute-start(bf16[256,2560]{1,0:T(8,128)(2,1)} %param.7), channel_id=1, source_target_pairs={{0,3},{1,0},{2,1},{3,2},{4,7},{5,4},{6,5},{7,6},{8,11},{9,8},{10,9... | collective-permute-start | bytes 3932168 | tf_op jit(solution)/shard_map/ppermute | solution.py:28
  7.9 33.0 %collective-permute-start.3 = (s32[5,2560]{1,0:T(8,128)}, s32[5,2560]{1,0:T(8,128)}, u32[]{:S(2)}, u32[]{:S(2)}) collective-permute-start(s32[5,2560]{1,0:T(8,128)} %param.11), channel_id=1, source_target_pairs={{0,4},{4,0},{1,5},{5,1},{2,6},{6,2},{3,7},{7,3},{8,12},{12,8},{9,1... | collective-permute-start | bytes 153608 | tf_op jit(solution)/shard_map/ppermute | solution.py:28
  16.5 16.8 %collective-permute-start = (bf16[40,2560]{1,0:T(8,128)(2,1)S(1)}, bf16[40,2560]{1,0:T(8,128)(2,1)}, u32[]{:S(2)}, u32[]{:S(2)}) collective-permute-start(bf16[40,2560]{1,0:T(8,128)(2,1)S(1)} %constant_dynamic-slice_fusion.2), channel_id=1, source_target_pairs={{0,4},{4,0},{1,5},{5,1},{2,6},{6,2},{3,7},{7,3},{8,12},{12,8},{9,1... | collective-permute-start | bytes 614408 | tf_op jit(solution)/shard_map/ppermute | solution.py:28
  20.4 40.0 %collective-permute-start.6 = (bf16[2,160,1024]{2,1,0:T(8,128)(2,1)}, bf16[2,160,1024]{2,1,0:T(8,128)(2,1)}, u32[]{:S(2)}, u32[]{:S(2)}) collective-permute-start(bf16[2,160,1024]{2,1,0:T(8,128)(2,1)} %fusion.14), channel_id=1, source_target_pairs={{0,4},{4,0},{1,5},{5,1},{2,6},{6,2},{3,7},{7,3},{8,12},{12,8},{9,1... | collective-permute-start | bytes 1966088 | tf_op jit(solution)/shard_map/ppermute | solution.py:28
  30.7 7.5 %copy-start.1 = (bf16[160,2560]{1,0:T(8,128)(2,1)S(1)}, bf16[160,2560]{1,0:T(8,128)(2,1)}, u32[]{:S(2)}) copy-start(bf16[160,2560]{1,0:T(8,128)(2,1)} %param.10) | copy-start | bytes 2457604
  33.3 9.2 %collective-permute-start.1 = (bf16[40,2560]{1,0:T(8,128)(2,1)}, bf16[40,2560]{1,0:T(8,128)(2,1)}, u32[]{:S(2)}, u32[]{:S(2)}) collective-permute-start(bf16[40,2560]{1,0:T(8,128)(2,1)} %collective-permute-done), channel_id=1, source_target_pairs={{0,16},{16,0},{32,48},{48,32},{64,80},{80,64},{96,112},{112,96},{1... | collective-permute-start | bytes 614408 | tf_op jit(solution)/shard_map/ppermute | solution.py:55
  40.1 20.4 %copy-start.2 = (bf16[160,2048]{1,0:T(8,128)(2,1)S(1)}, bf16[160,2048]{1,0:T(8,128)(2,1)}, u32[]{:S(2)}) copy-start(bf16[160,2048]{1,0:T(8,128)(2,1)} %param.8) | copy-start | bytes 1966084
  40.1 20.4 %copy-start.3 = (bf16[160,2048]{1,0:T(8,128)(2,1)S(1)}, bf16[160,2048]{1,0:T(8,128)(2,1)}, u32[]{:S(2)}) copy-start(bf16[160,2048]{1,0:T(8,128)(2,1)} %param.9) | copy-start | bytes 1966084
  43.7 18.5 %collective-permute-start.2 = (bf16[80,2560]{1,0:T(8,128)(2,1)S(1)}, bf16[80,2560]{1,0:T(8,128)(2,1)S(1)}, u32[]{:S(2)}, u32[]{:S(2)}) collective-permute-start(bf16[80,2560]{1,0:T(8,128)(2,1)S(1)} %pad_maximum_fusion.6), channel_id=1, source_target_pairs={{0,8},{8,0},{1,9},{9,1},{2,10},{10,2},{3,11},{11,3},{4,12},{12,4},... | collective-permute-start | bytes 1228808 | tf_op jit(solution)/shard_map/ppermute | solution.py:28
  62.3 8.3 %copy-start = (bf16[768,2560]{1,0:T(8,128)(2,1)S(1)}, bf16[768,2560]{1,0:T(8,128)(2,1)}, u32[]{:S(2)}) copy-start(bf16[768,2560]{1,0:T(8,128)(2,1)} %constant_dynamic-update-slice_fusion.2) | copy-start | bytes 11796484
  62.6 17.7 %collective-permute-start.7 = (bf16[128,2560]{1,0:T(8,128)(2,1)S(1)}, bf16[128,2560]{1,0:T(8,128)(2,1)S(1)}, u32[]{:S(2)}, u32[]{:S(2)}) collective-permute-start(bf16[128,2560]{1,0:T(8,128)(2,1)S(1)} %slice.44), channel_id=1, source_target_pairs={{0,1},{1,2},{2,3},{3,0},{4,5},{5,6},{6,7},{7,4},{8,9},{9,10},{10,1... | collective-permute-start | bytes 1966088 | tf_op jit(solution)/shard_map/ppermute | solution.py:28
  66.2 16.1 %collective-permute-start.8 = (bf16[128,2560]{1,0:T(8,128)(2,1)S(1)}, bf16[128,2560]{1,0:T(8,128)(2,1)S(1)}, u32[]{:S(2)}, u32[]{:S(2)}) collective-permute-start(bf16[128,2560]{1,0:T(8,128)(2,1)S(1)} %slice.45), channel_id=1, source_target_pairs={{0,3},{1,0},{2,1},{3,2},{4,7},{5,4},{6,5},{7,6},{8,11},{9,8},{10,9... | collective-permute-start | bytes 1966088 | tf_op jit(solution)/shard_map/ppermute | solution.py:28
  84.9 10.5 %collective-permute-start.9 = (f32[320,2560]{1,0:T(8,128)S(1)}, f32[320,2560]{1,0:T(8,128)S(1)}, u32[]{:S(2)}, u32[]{:S(2)}) collective-permute-start(f32[320,2560]{1,0:T(8,128)S(1)} %add.130), channel_id=1, source_target_pairs={{0,8},{8,0},{1,9},{9,1},{2,10},{10,2},{3,11},{11,3},{4,12},{12,4},... | collective-permute-start | bytes 9830408 | tf_op jit(solution)/shard_map/ppermute | solution.py:28
  99.5 61.5 %copy-start.5 = (f32[50,128]{1,0:T(8,128)S(1)}, f32[50,128]{1,0:T(8,128)}, u32[]{:S(2)}) copy-start(f32[50,128]{1,0:T(8,128)} %param.12) | copy-start | bytes 76804
  99.5 61.5 %copy-start.6 = (f32[50,128]{1,0:T(8,128)S(1)}, f32[50,128]{1,0:T(8,128)}, u32[]{:S(2)}) copy-start(f32[50,128]{1,0:T(8,128)} %param.13) | copy-start | bytes 76804
  99.5 54.8 %all-to-all-start = ((bf16[64,100,128]{2,1,0:T(8,128)(2,1)}), bf16[64,100,128]{2,1,0:T(8,128)(2,1)S(1)}, u32[]{:S(2)}, u32[]{:S(2)}) async-start(bf16[64,100,128]{2,1,0:T(8,128)(2,1)} %reshape.36), calls=%async_computation | async-start | bytes 3407872 | tf_op jit(solution)/shard_map/all_to_all | solution.py:119
  154.7 6.4 %collective-permute-start.10 = (f32[50,128]{1,0:T(8,128)S(1)}, f32[50,128]{1,0:T(8,128)S(1)}, u32[]{:S(2)}, u32[]{:S(2)}) collective-permute-start(f32[50,128]{1,0:T(8,128)S(1)} %constant_dynamic-slice_fusion), channel_id=1, source_target_pairs={{0,8},{8,0},{1,9},{9,1},{2,10},{10,2},{3,11},{11,3},{4,12},{12,4},... | collective-permute-start | bytes 76808 | tf_op jit(solution)/shard_map/ppermute | solution.py:28
  183.5 5.7 %collective-permute-start.11 = (bf16[32,50,128]{2,1,0:T(8,128)(2,1)S(1)}, bf16[32,50,128]{2,1,0:T(8,128)(2,1)S(1)}, u32[]{:S(2)}, u32[]{:S(2)}) collective-permute-start(bf16[32,50,128]{2,1,0:T(8,128)(2,1)S(1)} %all_to_all.10), channel_id=1, source_target_pairs={{0,8},{8,0},{1,9},{9,1},{2,10},{10,2},{3,11},{11,3},{4,12},{12,4},... | collective-permute-start | bytes 1228808 | tf_op jit(solution)/shard_map/ppermute | solution.py:28

commit v3 on v2

--- a/solution.py
+++ b/solution.py
@@ -50,33 +50,22 @@
     piece = lax.dynamic_slice_in_dim(w_out, (core * 2 + odd) * quarter, quarter, 0)
     piece = shift(piece, "yh", 1)
     other_signs = shift(signs, "yh", 1)
-    pair = jnp.stack([resid, target])
-    other_pair = shift(lax.dynamic_slice_in_dim(pair, (1 - half) * group, group, 2), "yh", 1)
+    pair = jnp.stack(
+        [lax.dynamic_slice_in_dim(part, (1 - half) * group, group, 1) for part in (resid, target)]
+    )
+    other_pair = shift(pair, "yh", 1)
+    twin = shift(piece, "c", 1)
     beside = lax.ppermute(piece, "z", [(i, i ^ 1) for i in range(8)])
-    part = jnp.concatenate(
-        [jnp.where(odd == 0, piece, beside), jnp.where(odd == 0, beside, piece)], axis=0
-    )
-    twin = shift(part, "c", 1)
-    other_w = jnp.concatenate(
-        [jnp.where(core == 0, part, twin), jnp.where(core == 0, twin, part)], axis=0
-    )
+    across = lax.ppermute(piece, ("z", "c"), [(i, i ^ 3) for i in range(16)])
     far_top = shift(from_left[: tokens // 2], "x", 1)
     far_low = shift(from_right[tokens // 2 :], "x", -1)
-
+    spot = core * 2 + odd
+    other_w = jnp.zeros_like(w_out)
+    for flip, rows in enumerate((piece, beside, twin, across)):
+        other_w = lax.dynamic_update_slice_in_dim(other_w, rows, (spot ^ flip) * quarter, 0)
+    other_stack = jnp.concatenate([other_w, unpack_signs(other_signs)], axis=0)
     probes = unpack_signs(signs)
-    other_probes = unpack_signs(other_signs)
-    own_pair = lax.dynamic_slice_in_dim(pair, half * group, group, 2)
-
-    def in_order(own, other):
-        first = jnp.where(half == 0, own, other)
-        second = jnp.where(half == 0, other, own)
-        return jnp.concatenate([first, second], axis=0)
-
-    stacked = jnp.concatenate([in_order(w_out, other_w), in_order(probes, other_probes)], axis=0)
-    pair_all = jnp.concatenate(
-        [jnp.where(half == 0, own_pair, other_pair), jnp.where(half == 0, other_pair, own_pair)], axis=1
-    )
-    count = 2 * features
+    own_stack = jnp.concatenate([w_out, probes], axis=0)
 
     each = m_old.shape[0]
     row_start = (
@@ -85,37 +74,57 @@
     my_probes = lax.dynamic_slice_in_dim(probes.reshape(-1, 128), row_start, each, 0)
     own_rows = lax.dynamic_slice_in_dim(w_out.reshape(-1, 128), row_start, each, 0)
 
-    def run(block, places):
-        cols = [lax.dynamic_slice_in_dim(pair_all, ((col + k) % 4) * tokens, tokens, 2) for k in places]
-        here = jnp.concatenate(cols, axis=2) if len(cols) > 1 else cols[0]
+    def run(stack, block, residual, wanted):
         forward = lax.dot_general(
-            stacked, block, (((1,), (1,)), ((), ())), preferred_element_type=jnp.float32
+            stack, block, (((1,), (1,)), ((), ())), preferred_element_type=jnp.float32
         )
-        misfit = here[0].astype(jnp.float32) + forward[:count] - here[1].astype(jnp.float32)
+        misfit = residual.astype(jnp.float32) + forward[:features] - wanted.astype(jnp.float32)
         spread = 1.0 + misfit * misfit
         rooted = jnp.sqrt(spread)
         slopes = (misfit / rooted).astype(jnp.bfloat16)
-        bends = (forward[count:] / (spread * rooted)).astype(jnp.bfloat16)
+        bends = (forward[features:] / (spread * rooted)).astype(jnp.bfloat16)
         away = jnp.where(core == 0, bends, slopes)
         kept = jnp.where(core == 0, slopes, bends)
         return away, kept
 
-    near = jnp.concatenate([hidden, from_left, from_right], axis=0)
-    away_near, kept_near = run(near, (0, 3, 1))
-    sum_away = jnp.dot(away_near, near, preferred_element_type=jnp.float32)
-    sum_kept = jnp.dot(kept_near, near, preferred_element_type=jnp.float32)
-    sum_away, sum_kept, far_top, far_low, my_probes, own_rows = lax.optimization_barrier(
-        (sum_away, sum_kept, far_top, far_low, my_probes, own_rows)
+    def columns(part, k, base):
+        return lax.dynamic_slice_in_dim(part, base + ((col + k) % 4) * tokens, tokens, 1)
+
+    def own_run(block, k):
+        base = half * group
+        return run(own_stack, block, columns(resid, k, base), columns(target, k, base))
+
+    def other_run(block, k):
+        return run(other_stack, block, columns(other_pair[0], k, 0), columns(other_pair[1], k, 0))
+
+    def products(rows, block):
+        return jnp.dot(rows, block, preferred_element_type=jnp.float32)
+
+    near = ((hidden, 0), (from_left, 3), (from_right, 1))
+    runs = [own_run(block, k) for block, k in near]
+    away_own = sum(products(r[0], b) for r, (b, _) in zip(runs, near))
+    kept_own = sum(products(r[1], b) for r, (b, _) in zip(runs, near))
+    runs = [other_run(block, k) for block, k in near]
+    away_other = sum(products(r[0], b) for r, (b, _) in zip(runs, near))
+    kept_other = sum(products(r[1], b) for r, (b, _) in zip(runs, near))
+    away_own, kept_own, away_other, kept_other, far_top, far_low, my_probes, own_rows = (
+        lax.optimization_barrier(
+            (away_own, kept_own, away_other, kept_other, far_top, far_low, my_probes, own_rows)
+        )
     )
     far = jnp.concatenate([far_top, far_low], axis=0)
-    away_far, kept_far = run(far, (2,))
-    sum_away = sum_away + jnp.dot(away_far, far, preferred_element_type=jnp.float32)
-    got = shift(sum_away, "c", 1)
-    sum_kept = sum_kept + jnp.dot(kept_far, far, preferred_element_type=jnp.float32)
-    mine = (sum_kept + got).astype(jnp.bfloat16)
+    own_far = own_run(far, 2)
+    other_far = other_run(far, 2)
+    got_own = shift(away_own + products(own_far[0], far), "c", 1)
+    got_other = shift(away_other + products(other_far[0], far), "c", 1)
+    mine_own = kept_own + products(own_far[1], far) + got_own
+    mine_other = kept_other + products(other_far[1], far) + got_other
+    mine = jnp.concatenate(
+        [jnp.where(half == 0, mine_own, mine_other), jnp.where(half == 0, mine_other, mine_own)], axis=0
+    ).astype(jnp.bfloat16)
 
     plane = 64
-    pieces = mine.reshape(plane, count * width // (plane * 128), 128)
+    pieces = mine.reshape(plane, 2 * features * width // (plane * 128), 128)
     terms = lax.all_to_all(pieces, ("yh", "yl", "z"), 0, 0, tiled=True)
     total = jnp.sum(terms.astype(jnp.float32), axis=0)
     keep_rows = lax.dynamic_slice_in_dim(total, core * each, each, 0)

time: 192 us -> 221 us (1.15)
  waiting for transfers between devices: 53 us -> 73.8 us
  matrix products: 7.83 us -> 13.6 us
    ppermute x11 -> x12, waiting for transfers between devices: 12.1 us -> 27.3 us  [shift(): return lax.ppermute(value, axis, hops)]
    dot_general x6 -> x24, matrix products: 7.83 us -> 13.6 us  [the longest x16 8.65 us: products(): return jnp.dot(rows, block, preferred_element_type=jnp.float32)]
    ppermute x11 -> x12, starting transfers between devices: 61.4 us -> 56.1 us  [shift(): return lax.ppermute(value, axis, hops)]
    ppermute x0 -> x1, waiting for transfers between devices: none -> 5.19 us  [step(): across = lax.ppermute(piece, ('z', 'c'), [(i, i ^ 3) for i in range(16)])]
    select_n x5 -> x0, other arithmetic: 4.52 us -> none  [the longest x2 1.92 us: in_order(): first = jnp.where(half == 0, own, other)]
    ppermute x0 -> x1, starting transfers between devices: none -> 4.5 us  [step(): across = lax.ppermute(piece, ('z', 'c'), [(i, i ^ 3) for i in range(16)])]
    reshape x1 -> x0, local copies, waits for them, and re-layouts: 3.03 us -> none  [step(): pieces = mine.reshape(plane, count * width // (plane * 128), 128)]
    convert_element_type x0 -> x1, local copies, waits for them, and re-layouts: none -> 3.03 us  [step(): mine = jnp.concatenate([jnp.where(half == 0, mine_own, mine_other), jnp.w...]
  transfers between devices with their start and end apart: 13 -> 15, of which waited for: 7 -> 8; matrix products, arithmetic and copies ran while one was open for 14% -> 12% of each run, Pallas kernels for 0% -> 0%
where the time goes in v3:
time: 221 us; the launch traced here: 220 us
  starting transfers between devices  78 us (35%)
  waiting for transfers between devices  73.8 us (33%)
  blocking collectives  23.7 us (11%)
  local copies, waits for them, and re-layouts  18.1 us (8%)
  matrix products  13.6 us (6%)
  other arithmetic  11.5 us (5%)
    ppermute x12, starting transfers between devices, shift(): return lax.ppermute(value, axis, hops)  56.1 us
    all_to_all x1, waiting for transfers between devices, step(): terms = lax.all_to_all(pieces, ('yh', 'yl', 'z'), 0, 0, tiled=True)  41.3 us
    ppermute x12, waiting for transfers between devices, shift(): return lax.ppermute(value, axis, hops)  27.3 us
    all_to_all x1, blocking collectives, step(): mine_rows = lax.all_to_all(spread_rows, ('yl', 'z'), 0, 0, tiled=True)  23.7 us
    all_to_all x1, starting transfers between devices, step(): terms = lax.all_to_all(pieces, ('yh', 'yl', 'z'), 0, 0, tiled=True)  13.4 us
    dot_general x16, matrix products, products(): return jnp.dot(rows, block, preferred_element_type=jnp.float32)  8.65 us
    shift_right_arithmetic x6, local copies, waits for them, and re-layouts, unpack_signs(): jnp.right_shift(signs[:, None, :], shifts[None, :, None])  5.65 us
    ppermute x1, waiting for transfers between devices, step(): across = lax.ppermute(piece, ('z', 'c'), [(i, i ^ 3) for i in range(16)])  5.19 us
  transfers between devices with their start and end apart: 15, of which 8 were waited for; matrix products, arithmetic and copies ran while one was open for 12% of the time, Pallas kernels for 0%

profile of v3, /device:TPU:1, one launch (start us, length us, event | category | flops | bytes accessed | tf_op | source)
XLA Modules:
  0.0 219.8 jit_solution(10139755918111269986)
XLA Ops:
  0.6 5.3 %collective-permute-start.1 = (bf16[256,2560]{1,0:T(8,128)(2,1)}, bf16[256,2560]{1,0:T(8,128)(2,1)S(1)}, u32[]{:S(2)}, u32[]{:S(2)}) collective-permute-start(bf16[256,2560]{1,0:T(8,128)(2,1)} %param.7), channel_id=1, source_target_pairs={{0,3},{1,0},{2,1},{3,2},{4,7},{5,4},{6,5},{7,6},{8,11},{9,8},{10,9... | collective-permute-start | bytes 3932168 | tf_op jit(solution)/shard_map/ppermute | solution.py:28
  6.0 1.9 collective-permute-start
  7.9 7.5 %collective-permute-start.6 = (s32[5,2560]{1,0:T(8,128)}, s32[5,2560]{1,0:T(8,128)}, u32[]{:S(2)}, u32[]{:S(2)}) collective-permute-start(s32[5,2560]{1,0:T(8,128)} %param.11), channel_id=1, source_target_pairs={{0,4},{4,0},{1,5},{5,1},{2,6},{6,2},{3,7},{7,3},{8,12},{12,8},{9,1... | collective-permute-start | bytes 153608 | tf_op jit(solution)/shard_map/ppermute | solution.py:28
  15.4 1.1 dynamic-slice_bitcast_fusion
  16.5 0.9 pad_maximum_fusion.4
  17.4 1.9 collective-permute-start.7
  19.4 0.7 constant_dynamic-slice_fusion.1
  20.1 7.3 %collective-permute-start.2 = (bf16[40,2560]{1,0:T(8,128)(2,1)}, bf16[40,2560]{1,0:T(8,128)(2,1)}, u32[]{:S(2)}, u32[]{:S(2)}) collective-permute-start(bf16[40,2560]{1,0:T(8,128)(2,1)} %constant_dynamic-slice_fusion.1), channel_id=1, source_target_pairs={{0,4},{4,0},{1,5},{5,1},{2,6},{6,2},{3,7},{7,3},{8,12},{12,8},{9,1... | collective-permute-start | bytes 614408 | tf_op jit(solution)/shard_map/ppermute | solution.py:28
  27.4 1.9 reshape.51
  29.3 1.3 shift_right_arithmetic.55
  30.7 2.5 %shift_right_arithmetic.64 = s32[3200,128]{1,0:T(8,128)} reshape(s32[5,32,2560]{2,1,0:T(8,128)} %shift_right_arithmetic.55) | data formatting | bytes 3276800 | tf_op jit(solution)/shard_map/shift_right_arithmetic | solution.py:33
  33.2 0.7 shift_right_arithmetic.65
  33.9 1.0 shift_right_arithmetic.66
  35.0 0.8 fusion.84
  35.8 0.7 constant_dynamic-slice_fusion
  36.6 1.6 fusion.3
  38.2 0.6 fusion.92
  38.8 14.0 %collective-permute-done.2 = bf16[40,2560]{1,0:T(8,128)(2,1)} collective-permute-done((bf16[40,2560]{1,0:T(8,128)(2,1)}, bf16[40,2560]{1,0:T(8,128)(2,1)}, u32[]{:S(2)}, u32[]{:S(2)}) %collective-permute-start.2) | collective-permute-done | bytes 204832 | tf_op jit(solution)/shard_map/ppermute | solution.py:28
  52.8 4.0 %collective-permute-start.3 = (bf16[40,2560]{1,0:T(8,128)(2,1)}, bf16[40,2560]{1,0:T(8,128)(2,1)S(1)}, u32[]{:S(2)}, u32[]{:S(2)}) collective-permute-start(bf16[40,2560]{1,0:T(8,128)(2,1)} %collective-permute-done.2), channel_id=1, source_target_pairs={{0,16},{16,0},{32,48},{48,32},{64,80},{80,64},{96,112},{112,96},{1... | collective-permute-start | bytes 614408 | tf_op jit(solution)/shard_map/ppermute | solution.py:58
  56.8 11.6 %collective-permute-start.4 = (bf16[40,2560]{1,0:T(8,128)(2,1)}, bf16[40,2560]{1,0:T(8,128)(2,1)S(1)}, u32[]{:S(2)}, u32[]{:S(2)}) collective-permute-start(bf16[40,2560]{1,0:T(8,128)(2,1)} %collective-permute-done.2), channel_id=1, source_target_pairs={{0,8},{8,0},{1,9},{9,1},{2,10},{10,2},{3,11},{11,3},{4,12},{12,4},... | collective-permute-start | bytes 614408 | tf_op jit(solution)/shard_map/ppermute | solution.py:28
  68.5 1.0 constant_dynamic-update-slice_fusion.3
  69.4 4.5 %collective-permute-start.5 = (bf16[40,2560]{1,0:T(8,128)(2,1)}, bf16[40,2560]{1,0:T(8,128)(2,1)S(1)}, u32[]{:S(2)}, u32[]{:S(2)}) collective-permute-start(bf16[40,2560]{1,0:T(8,128)(2,1)} %collective-permute-done.2), channel_id=1, source_target_pairs={{0,24},{8,16},{16,8},{24,0},{32,56},{40,48},{48,40},{56,32},{64,88... | collective-permute-start | bytes 614408 | tf_op jit(solution)/shard_map/ppermute | solution.py:59
  74.0 5.2 %collective-permute-done.5 = bf16[40,2560]{1,0:T(8,128)(2,1)S(1)} collective-permute-done((bf16[40,2560]{1,0:T(8,128)(2,1)}, bf16[40,2560]{1,0:T(8,128)(2,1)S(1)}, u32[]{:S(2)}, u32[]{:S(2)}) %collective-permute-start.5) | collective-permute-done | bytes 204832 | tf_op jit(solution)/shard_map/ppermute | solution.py:59
  79.2 0.6 fusion.88
  79.9 1.1 fusion.94
  81.0 0.6 fusion.90
  81.7 0.6 fusion.91
  82.3 0.4 copy-done.4
  83.7 0.4 fusion.58
  84.1 0.6 fusion.86
  84.7 0.6 fusion.87
  85.3 0.4 fusion.25
  86.1 0.4 fusion.50
  86.5 2.1 collective-permute-start.8
  88.7 4.4 %collective-permute-start.9 = (bf16[128,2560]{1,0:T(8,128)(2,1)S(1)}, bf16[128,2560]{1,0:T(8,128)(2,1)S(1)}, u32[]{:S(2)}, u32[]{:S(2)}) collective-permute-start(bf16[128,2560]{1,0:T(8,128)(2,1)S(1)} %slice.101), channel_id=1, source_target_pairs={{0,3},{1,0},{2,1},{3,2},{4,7},{5,4},{6,5},{7,6},{8,11},{9,8},{10,9... | collective-permute-start | bytes 1966088 | tf_op jit(solution)/shard_map/ppermute | solution.py:28
  93.1 0.4 convolution_add_fusion.7
  93.5 0.4 convolution_add_fusion.5
  93.9 0.4 convolution_add_fusion.6
  94.3 1.6 convolution_add_fusion.4
  95.9 0.4 convolution_add_fusion.3
  96.3 0.4 convolution_add_fusion.1
  96.7 0.4 convolution_add_fusion.2
  97.1 1.6 convolution_add_fusion
  98.7 7.1 %collective-permute-done.8 = bf16[128,2560]{1,0:T(8,128)(2,1)S(1)} collective-permute-done((bf16[128,2560]{1,0:T(8,128)(2,1)S(1)}, bf16[128,2560]{1,0:T(8,128)(2,1)S(1)}, u32[]{:S(2)}, u32[]{:S(2)}) %collective-permute-start.8) | collective-permute-done | bytes 655392 | tf_op jit(solution)/shard_map/ppermute | solution.py:28
  105.8 1.0 collective-permute-done.9
  106.9 0.6 fusion.89
  107.5 0.6 fusion.85
  108.6 1.4 add.284
  110.0 3.3 %collective-permute-start.10 = (f32[160,2560]{1,0:T(8,128)}, f32[160,2560]{1,0:T(8,128)}, u32[]{:S(2)}, u32[]{:S(2)}) collective-permute-start(f32[160,2560]{1,0:T(8,128)} %add.284), channel_id=1, source_target_pairs={{0,8},{8,0},{1,9},{9,1},{2,10},{10,2},{3,11},{11,3},{4,12},{12,4},... | collective-permute-start | bytes 4915208 | tf_op jit(solution)/shard_map/ppermute | solution.py:28
  113.9 1.5 add.290
  115.4 1.9 collective-permute-start.11
  117.7 0.4 fusion.42
  118.1 3.0 %collective-permute-done.11 = f32[160,2560]{1,0:T(8,128)} collective-permute-done((f32[160,2560]{1,0:T(8,128)}, f32[160,2560]{1,0:T(8,128)}, u32[]{:S(2)}, u32[]{:S(2)}) %collective-permute-start.11) | collective-permute-done | bytes 1638432 | tf_op jit(solution)/shard_map/ppermute | solution.py:28
  121.1 3.0 %select_convert_fusion.1 = (bf16[160,2560]{1,0:T(8,128)(2,1)S(1)}, bf16[160,2560]{1,0:T(8,128)(2,1)S(1)}) fusion(pred[]{:T(512)S(6)} %eq.23, f32[160,2560]{1,0:T(8,128)} %collective-permute-done.10, f32[160,2560]{1,0:T(8,128)S(1)} %copy-done.1, f32[160,2560]{1,0:T(8,128)S(1)} %fusion.46, f32[160,2560]{1,0:T(8,128)} %collective-permute-done.11, ...), kind=kLoop, calls=%fused_computation.23 | loop fusion | flops 3276800 | bytes 11468801 | tf_op jit(solution)/shard_map/convert.8
  124.2 3.0 %convert_element_type.190 = bf16[64,100,128]{2,1,0:T(8,128)(2,1)} reshape(bf16[320,2560]{1,0:T(8,128)(2,1)S(1)} %pad_maximum_fusion.2) | data formatting | bytes 3276800 | tf_op jit(solution)/shard_map/convert_element_type | solution.py:124
  127.2 13.4 %all-to-all-start = ((bf16[64,100,128]{2,1,0:T(8,128)(2,1)}), bf16[64,100,128]{2,1,0:T(8,128)(2,1)S(1)}, u32[]{:S(2)}, u32[]{:S(2)}) async-start(bf16[64,100,128]{2,1,0:T(8,128)(2,1)} %convert_element_type.190), calls=%async_computation | async-start | bytes 3407872 | tf_op jit(solution)/shard_map/all_to_all | solution.py:128
  140.7 41.3 %all-to-all-done = bf16[64,100,128]{2,1,0:T(8,128)(2,1)S(1)} async-done(((bf16[64,100,128]{2,1,0:T(8,128)(2,1)}), bf16[64,100,128]{2,1,0:T(8,128)(2,1)S(1)}, u32[]{:S(2)}, u32[]{:S(2)}) %all-to-all-start) | async-done | bytes 1638432 | tf_op jit(solution)/shard_map/all_to_all | solution.py:128
  182.3 4.6 %collective-permute-start.12 = (f32[50,128]{1,0:T(8,128)S(1)}, f32[50,128]{1,0:T(8,128)S(1)}, u32[]{:S(2)}, u32[]{:S(2)}) collective-permute-start(f32[50,128]{1,0:T(8,128)S(1)} %constant_dynamic-slice_fusion.2), channel_id=1, source_target_pairs={{0,8},{8,0},{1,9},{9,1},{2,10},{10,2},{3,11},{11,3},{4,12},{12,4},... | collective-permute-start | bytes 76808 | tf_op jit(solution)/shard_map/ppermute | solution.py:28
  187.0 0.8 collective-permute-done.12
  187.8 0.6 subtract_convert_fusion
  188.5 23.7 %all_to_all.10 = bf16[32,50,128]{2,1,0:T(8,128)(2,1)S(1)} all-to-all(bf16[32,50,128]{2,1,0:T(8,128)(2,1)S(1)} %broadcast_in_dim.5), channel_id=1, replica_groups=mesh['yl'=4,'z'=8,'c'=2,'yh'=2,'x'=4] {'yl','z'}, dimensions={0} | all-to-all | bytes 819200 | tf_op jit(solution)/shard_map/all_to_all | solution.py:148
  212.2 4.3 %collective-permute-start.13 = (bf16[32,50,128]{2,1,0:T(8,128)(2,1)S(1)}, bf16[32,50,128]{2,1,0:T(8,128)(2,1)S(1)}, u32[]{:S(2)}, u32[]{:S(2)}) collective-permute-start(bf16[32,50,128]{2,1,0:T(8,128)(2,1)S(1)} %all_to_all.10), channel_id=1, source_target_pairs={{0,8},{8,0},{1,9},{9,1},{2,10},{10,2},{3,11},{11,3},{4,12},{12,4},... | collective-permute-start | bytes 1228808 | tf_op jit(solution)/shard_map/ppermute | solution.py:28
  216.5 1.4 collective-permute-done.13
  218.0 1.8 reshape.52
  (51 shorter events, 3.9 us)
Async XLA Ops:
  0.6 18.7 %copy-start.3 = (bf16[160,2560]{1,0:T(8,128)(2,1)S(1)}, bf16[160,2560]{1,0:T(8,128)(2,1)}, u32[]{:S(2)}) copy-start(bf16[160,2560]{1,0:T(8,128)(2,1)} %param.10) | copy-start | bytes 2457604
  0.6 80.3 %collective-permute-start.1 = (bf16[256,2560]{1,0:T(8,128)(2,1)}, bf16[256,2560]{1,0:T(8,128)(2,1)S(1)}, u32[]{:S(2)}, u32[]{:S(2)}) collective-permute-start(bf16[256,2560]{1,0:T(8,128)(2,1)} %param.7), channel_id=1, source_target_pairs={{0,3},{1,0},{2,1},{3,2},{4,7},{5,4},{6,5},{7,6},{8,11},{9,8},{10,9... | collective-permute-start | bytes 3932168 | tf_op jit(solution)/shard_map/ppermute | solution.py:28
  6.0 75.7 %collective-permute-start = (bf16[256,2560]{1,0:T(8,128)(2,1)}, bf16[256,2560]{1,0:T(8,128)(2,1)S(1)}, u32[]{:S(2)}, u32[]{:S(2)}) collective-permute-start(bf16[256,2560]{1,0:T(8,128)(2,1)} %param.7), channel_id=1, source_target_pairs={{0,1},{1,2},{2,3},{3,0},{4,5},{5,6},{6,7},{7,4},{8,9},{9,10},{10,1... | collective-permute-start | bytes 3932168 | tf_op jit(solution)/shard_map/ppermute | solution.py:28
  7.9 28.6 %collective-permute-start.6 = (s32[5,2560]{1,0:T(8,128)}, s32[5,2560]{1,0:T(8,128)}, u32[]{:S(2)}, u32[]{:S(2)}) collective-permute-start(s32[5,2560]{1,0:T(8,128)} %param.11), channel_id=1, source_target_pairs={{0,4},{4,0},{1,5},{5,1},{2,6},{6,2},{3,7},{7,3},{8,12},{12,8},{9,1... | collective-permute-start | bytes 153608 | tf_op jit(solution)/shard_map/ppermute | solution.py:28
  16.5 12.8 %copy-start.6 = (s32[5,2560]{1,0:T(8,128)S(1)}, s32[5,2560]{1,0:T(8,128)}, u32[]{:S(2)}) copy-start(s32[5,2560]{1,0:T(8,128)} %param.11) | copy-start | bytes 153604
  17.4 62.4 %collective-permute-start.7 = (bf16[2,160,1024]{2,1,0:T(8,128)(2,1)}, bf16[2,160,1024]{2,1,0:T(8,128)(2,1)}, u32[]{:S(2)}, u32[]{:S(2)}) collective-permute-start(bf16[2,160,1024]{2,1,0:T(8,128)(2,1)} %pad_maximum_fusion.4), channel_id=1, source_target_pairs={{0,4},{4,0},{1,5},{5,1},{2,6},{6,2},{3,7},{7,3},{8,12},{12,8},{9,1... | collective-permute-start | bytes 1966088 | tf_op jit(solution)/shard_map/ppermute | solution.py:28
  20.1 32.8 %collective-permute-start.2 = (bf16[40,2560]{1,0:T(8,128)(2,1)}, bf16[40,2560]{1,0:T(8,128)(2,1)}, u32[]{:S(2)}, u32[]{:S(2)}) collective-permute-start(bf16[40,2560]{1,0:T(8,128)(2,1)} %constant_dynamic-slice_fusion.1), channel_id=1, source_target_pairs={{0,4},{4,0},{1,5},{5,1},{2,6},{6,2},{3,7},{7,3},{8,12},{12,8},{9,1... | collective-permute-start | bytes 614408 | tf_op jit(solution)/shard_map/ppermute | solution.py:28
  29.3 3.9 %copy-start.9 = (s32[160]{0:T(256)}, s32[160]{0:T(256)S(1)}, u32[]{:S(2)}) copy-start(s32[160]{0:T(256)S(1)} %shift_right_arithmetic.58) | copy-start | bytes 1924
  36.5 1.7 copy-start
  52.8 16.6 %collective-permute-start.3 = (bf16[40,2560]{1,0:T(8,128)(2,1)}, bf16[40,2560]{1,0:T(8,128)(2,1)S(1)}, u32[]{:S(2)}, u32[]{:S(2)}) collective-permute-start(bf16[40,2560]{1,0:T(8,128)(2,1)} %collective-permute-done.2), channel_id=1, source_target_pairs={{0,16},{16,0},{32,48},{48,32},{64,80},{80,64},{96,112},{112,96},{1... | collective-permute-start | bytes 614408 | tf_op jit(solution)/shard_map/ppermute | solution.py:58
  56.8 17.1 %collective-permute-start.4 = (bf16[40,2560]{1,0:T(8,128)(2,1)}, bf16[40,2560]{1,0:T(8,128)(2,1)S(1)}, u32[]{:S(2)}, u32[]{:S(2)}) collective-permute-start(bf16[40,2560]{1,0:T(8,128)(2,1)} %collective-permute-done.2), channel_id=1, source_target_pairs={{0,8},{8,0},{1,9},{9,1},{2,10},{10,2},{3,11},{11,3},{4,12},{12,4},... | collective-permute-start | bytes 614408 | tf_op jit(solution)/shard_map/ppermute | solution.py:28
  69.4 9.8 %collective-permute-start.5 = (bf16[40,2560]{1,0:T(8,128)(2,1)}, bf16[40,2560]{1,0:T(8,128)(2,1)S(1)}, u32[]{:S(2)}, u32[]{:S(2)}) collective-permute-start(bf16[40,2560]{1,0:T(8,128)(2,1)} %collective-permute-done.2), channel_id=1, source_target_pairs={{0,24},{8,16},{16,8},{24,0},{32,56},{40,48},{48,40},{56,32},{64,88... | collective-permute-start | bytes 614408 | tf_op jit(solution)/shard_map/ppermute | solution.py:59
  81.6 1.1 copy-start.4
  81.6 1.3 copy-start.5
  86.5 19.3 %collective-permute-start.8 = (bf16[128,2560]{1,0:T(8,128)(2,1)S(1)}, bf16[128,2560]{1,0:T(8,128)(2,1)S(1)}, u32[]{:S(2)}, u32[]{:S(2)}) collective-permute-start(bf16[128,2560]{1,0:T(8,128)(2,1)S(1)} %slice.100), channel_id=1, source_target_pairs={{0,1},{1,2},{2,3},{3,0},{4,5},{5,6},{6,7},{7,4},{8,9},{9,10},{10,1... | collective-permute-start | bytes 1966088 | tf_op jit(solution)/shard_map/ppermute | solution.py:28
  88.7 18.1 %collective-permute-start.9 = (bf16[128,2560]{1,0:T(8,128)(2,1)S(1)}, bf16[128,2560]{1,0:T(8,128)(2,1)S(1)}, u32[]{:S(2)}, u32[]{:S(2)}) collective-permute-start(bf16[128,2560]{1,0:T(8,128)(2,1)S(1)} %slice.101), channel_id=1, source_target_pairs={{0,3},{1,0},{2,1},{3,2},{4,7},{5,4},{6,5},{7,6},{8,11},{9,8},{10,9... | collective-permute-start | bytes 1966088 | tf_op jit(solution)/shard_map/ppermute | solution.py:28
  110.0 8.0 %collective-permute-start.10 = (f32[160,2560]{1,0:T(8,128)}, f32[160,2560]{1,0:T(8,128)}, u32[]{:S(2)}, u32[]{:S(2)}) collective-permute-start(f32[160,2560]{1,0:T(8,128)} %add.284), channel_id=1, source_target_pairs={{0,8},{8,0},{1,9},{9,1},{2,10},{10,2},{3,11},{11,3},{4,12},{12,4},... | collective-permute-start | bytes 4915208 | tf_op jit(solution)/shard_map/ppermute | solution.py:28
  115.4 5.7 %collective-permute-start.11 = (f32[160,2560]{1,0:T(8,128)}, f32[160,2560]{1,0:T(8,128)}, u32[]{:S(2)}, u32[]{:S(2)}) collective-permute-start(f32[160,2560]{1,0:T(8,128)} %add.290), channel_id=1, source_target_pairs={{0,8},{8,0},{1,9},{9,1},{2,10},{10,2},{3,11},{11,3},{4,12},{12,4},... | collective-permute-start | bytes 4915208 | tf_op jit(solution)/shard_map/ppermute | solution.py:28
  117.3 3.8 %copy-start.2 = (f32[160,2560]{1,0:T(8,128)S(1)}, f32[160,2560]{1,0:T(8,128)}, u32[]{:S(2)}) copy-start(f32[160,2560]{1,0:T(8,128)} %convolution_add_fusion) | copy-start | bytes 4915204
  117.7 3.4 %copy-start.1 = (f32[160,2560]{1,0:T(8,128)S(1)}, f32[160,2560]{1,0:T(8,128)}, u32[]{:S(2)}) copy-start(f32[160,2560]{1,0:T(8,128)} %convolution_add_fusion.4) | copy-start | bytes 4915204
  127.2 54.8 %all-to-all-start = ((bf16[64,100,128]{2,1,0:T(8,128)(2,1)}), bf16[64,100,128]{2,1,0:T(8,128)(2,1)S(1)}, u32[]{:S(2)}, u32[]{:S(2)}) async-start(bf16[64,100,128]{2,1,0:T(8,128)(2,1)} %convert_element_type.190), calls=%async_computation | async-start | bytes 3407872 | tf_op jit(solution)/shard_map/all_to_all | solution.py:128
  140.6 47.2 %copy-start.7 = (f32[50,128]{1,0:T(8,128)S(1)}, f32[50,128]{1,0:T(8,128)}, u32[]{:S(2)}) copy-start(f32[50,128]{1,0:T(8,128)} %param.12) | copy-start | bytes 76804
  140.6 47.1 %copy-start.8 = (f32[50,128]{1,0:T(8,128)S(1)}, f32[50,128]{1,0:T(8,128)}, u32[]{:S(2)}) copy-start(f32[50,128]{1,0:T(8,128)} %param.13) | copy-start | bytes 76804
  182.3 5.5 %collective-permute-start.12 = (f32[50,128]{1,0:T(8,128)S(1)}, f32[50,128]{1,0:T(8,128)S(1)}, u32[]{:S(2)}, u32[]{:S(2)}) collective-permute-start(f32[50,128]{1,0:T(8,128)S(1)} %constant_dynamic-slice_fusion.2), channel_id=1, source_target_pairs={{0,8},{8,0},{1,9},{9,1},{2,10},{10,2},{3,11},{11,3},{4,12},{12,4},... | collective-permute-start | bytes 76808 | tf_op jit(solution)/shard_map/ppermute | solution.py:28
  212.2 5.7 %collective-permute-start.13 = (bf16[32,50,128]{2,1,0:T(8,128)(2,1)S(1)}, bf16[32,50,128]{2,1,0:T(8,128)(2,1)S(1)}, u32[]{:S(2)}, u32[]{:S(2)}) collective-permute-start(bf16[32,50,128]{2,1,0:T(8,128)(2,1)S(1)} %all_to_all.10), channel_id=1, source_target_pairs={{0,8},{8,0},{1,9},{9,1},{2,10},{10,2},{3,11},{11,3},{4,12},{12,4},... | collective-permute-start | bytes 1228808 | tf_op jit(solution)/shard_map/ppermute | solution.py:28

commit v4 on v2

--- a/solution.py
+++ b/solution.py
@@ -41,57 +41,47 @@
     half = lax.axis_index("yh")
     core = lax.axis_index("c")
     col = lax.axis_index("x")
-    odd = lax.axis_index("z") % 2
 
     from_left = shift(hidden, "x", 1)
     from_right = shift(hidden, "x", -1)
 
-    quarter = features // 4
-    piece = lax.dynamic_slice_in_dim(w_out, (core * 2 + odd) * quarter, quarter, 0)
-    piece = shift(piece, "yh", 1)
+    rows = features // 2
+    part = shift(lax.dynamic_slice_in_dim(w_out, core * rows, rows, 0), "yh", 1)
     other_signs = shift(signs, "yh", 1)
-    pair = jnp.stack([resid, target])
-    other_pair = shift(lax.dynamic_slice_in_dim(pair, (1 - half) * group, group, 2), "yh", 1)
-    beside = lax.ppermute(piece, "z", [(i, i ^ 1) for i in range(8)])
-    part = jnp.concatenate(
-        [jnp.where(odd == 0, piece, beside), jnp.where(odd == 0, beside, piece)], axis=0
-    )
+
+    def gap(at):
+        first = lax.dynamic_slice_in_dim(resid, at * group, group, 1)
+        return first.astype(jnp.float32) - lax.dynamic_slice_in_dim(
+            target, at * group, group, 1
+        ).astype(jnp.float32)
+
+    other_gap = shift(gap(1 - half).astype(jnp.bfloat16), "yh", 1)
+    far_top = shift(from_left[: tokens // 2], "x", 1)
+    far_low = shift(from_right[tokens // 2 :], "x", -1)
     twin = shift(part, "c", 1)
+
+    def in_order(own, other):
+        return jnp.concatenate(
+            [jnp.where(half == 0, own, other), jnp.where(half == 0, other, own)], axis=0
+        )
+
+    probes = unpack_signs(signs)
     other_w = jnp.concatenate(
         [jnp.where(core == 0, part, twin), jnp.where(core == 0, twin, part)], axis=0
     )
-    far_top = shift(from_left[: tokens // 2], "x", 1)
-    far_low = shift(from_right[tokens // 2 :], "x", -1)
-
-    probes = unpack_signs(signs)
-    other_probes = unpack_signs(other_signs)
-    own_pair = lax.dynamic_slice_in_dim(pair, half * group, group, 2)
-
-    def in_order(own, other):
-        first = jnp.where(half == 0, own, other)
-        second = jnp.where(half == 0, other, own)
-        return jnp.concatenate([first, second], axis=0)
-
-    stacked = jnp.concatenate([in_order(w_out, other_w), in_order(probes, other_probes)], axis=0)
-    pair_all = jnp.concatenate(
-        [jnp.where(half == 0, own_pair, other_pair), jnp.where(half == 0, other_pair, own_pair)], axis=1
+    stacked = jnp.concatenate(
+        [in_order(w_out, other_w), in_order(probes, unpack_signs(other_signs))], axis=0
     )
+    gaps = in_order(gap(half), other_gap.astype(jnp.float32))
+    gaps = jnp.concatenate([gaps, gaps], axis=1)
     count = 2 * features
 
-    each = m_old.shape[0]
-    row_start = (
-        (lax.axis_index("yl") * lax.axis_size("z") + lax.axis_index("z")) * 2 + core
-    ) * each
-    my_probes = lax.dynamic_slice_in_dim(probes.reshape(-1, 128), row_start, each, 0)
-    own_rows = lax.dynamic_slice_in_dim(w_out.reshape(-1, 128), row_start, each, 0)
-
-    def run(block, places):
-        cols = [lax.dynamic_slice_in_dim(pair_all, ((col + k) % 4) * tokens, tokens, 2) for k in places]
-        here = jnp.concatenate(cols, axis=2) if len(cols) > 1 else cols[0]
+    def run(block, first):
+        here = lax.dynamic_slice_in_dim(gaps, ((col + first) % 4) * tokens, block.shape[0], 1)
         forward = lax.dot_general(
             stacked, block, (((1,), (1,)), ((), ())), preferred_element_type=jnp.float32
         )
-        misfit = here[0].astype(jnp.float32) + forward[:count] - here[1].astype(jnp.float32)
+        misfit = here + forward[:count]
         spread = 1.0 + misfit * misfit
         rooted = jnp.sqrt(spread)
         slopes = (misfit / rooted).astype(jnp.bfloat16)
@@ -100,23 +90,37 @@
         kept = jnp.where(core == 0, slopes, bends)
         return away, kept
 
-    near = jnp.concatenate([hidden, from_left, from_right], axis=0)
-    away_near, kept_near = run(near, (0, 3, 1))
-    sum_away = jnp.dot(away_near, near, preferred_element_type=jnp.float32)
-    sum_kept = jnp.dot(kept_near, near, preferred_element_type=jnp.float32)
-    sum_away, sum_kept, far_top, far_low, my_probes, own_rows = lax.optimization_barrier(
-        (sum_away, sum_kept, far_top, far_low, my_probes, own_rows)
+    def products(terms, block):
+        return jnp.dot(terms, block, preferred_element_type=jnp.float32)
+
+    near = jnp.concatenate([from_left, hidden, from_right], axis=0)
+    away, kept = run(near, 3)
+    away_near = products(away, near)
+    kept_near = products(kept, near)
+    away_near, kept_near, far_top, far_low = lax.optimization_barrier(
+        (away_near, kept_near, far_top, far_low)
     )
     far = jnp.concatenate([far_top, far_low], axis=0)
-    away_far, kept_far = run(far, (2,))
-    sum_away = sum_away + jnp.dot(away_far, far, preferred_element_type=jnp.float32)
-    got = shift(sum_away, "c", 1)
-    sum_kept = sum_kept + jnp.dot(kept_far, far, preferred_element_type=jnp.float32)
-    mine = (sum_kept + got).astype(jnp.bfloat16)
+    away, kept = run(far, 2)
+    got = [
+        shift(away_near[rows] + products(away[rows], far), "c", 1)
+        for rows in (slice(0, features), slice(features, None))
+    ]
+    kept_all = kept_near + products(kept, far)
+    mine = jnp.concatenate(
+        [kept_all[:features] + got[0], kept_all[features:] + got[1]], axis=0
+    ).astype(jnp.bfloat16)
 
+    each = m_old.shape[0]
+    row_start = (
+        (lax.axis_index("yl") * lax.axis_size("z") + lax.axis_index("z")) * 2 + core
+    ) * each
+    my_probes = lax.dynamic_slice_in_dim(unpack_signs(signs).reshape(-1, 128), row_start, each, 0)
+    own_rows = lax.dynamic_slice_in_dim(w_out.reshape(-1, 128), row_start, each, 0)
     plane = 64
     pieces = mine.reshape(plane, count * width // (plane * 128), 128)
     terms = lax.all_to_all(pieces, ("yh", "yl", "z"), 0, 0, tiled=True)
+    terms, my_probes, own_rows = lax.optimization_barrier((terms, my_probes, own_rows))
     total = jnp.sum(terms.astype(jnp.float32), axis=0)
     keep_rows = lax.dynamic_slice_in_dim(total, core * each, each, 0)
     send_rows = lax.dynamic_slice_in_dim(total, (1 - core) * each, each, 0)

time: 192 us -> 185 us (0.964)
  starting transfers between devices: 79.3 us -> 75.6 us
  local copies, waits for them, and re-layouts: 16.9 us -> 14.2 us
    ppermute x11 -> x12, waiting for transfers between devices: 12.1 us -> 18.5 us  [shift(): return lax.ppermute(value, axis, hops)]
    all_to_all x1, waiting for transfers between devices: 40.9 us -> 35.7 us  [step(): terms = lax.all_to_all(pieces, ('yh', 'yl', 'z'), 0, 0, tiled=True)]
    ppermute x1 -> x0, starting transfers between devices: 3.99 us -> none  [step(): beside = lax.ppermute(piece, 'z', [(i, i ^ 1) for i in range(8)])]
    all_to_all x1, starting transfers between devices: 13.9 us -> 17.1 us  [step(): terms = lax.all_to_all(pieces, ('yh', 'yl', 'z'), 0, 0, tiled=True)]
    convert_element_type x0 -> x1, local copies, waits for them, and re-layouts: none -> 3.04 us  [step(): mine = jnp.concatenate([kept_all[:features] + got[0], kept_all[features:]...]
    reshape x1 -> x0, local copies, waits for them, and re-layouts: 3.03 us -> none  [step(): pieces = mine.reshape(plane, count * width // (plane * 128), 128)]
    ppermute x11 -> x12, starting transfers between devices: 61.4 us -> 58.5 us  [shift(): return lax.ppermute(value, axis, hops)]
    dot_general x4 -> x5, matrix products: 4.06 us -> 4.23 us  [products(): return jnp.dot(terms, block, preferred_element_type=jnp.float32)]
  transfers between devices with their start and end apart: 13 -> 13, of which waited for: 7 -> 8; matrix products, arithmetic and copies ran while one was open for 14% -> 11% of each run, Pallas kernels for 0% -> 0%
where the time goes in v4:
time: 185 us; the launch traced here: 184 us
  starting transfers between devices  75.6 us (41%)
  waiting for transfers between devices  54.2 us (29%)
  blocking collectives  21.7 us (12%)
  local copies, waits for them, and re-layouts  14.2 us (8%)
  other arithmetic  9.41 us (5%)
  matrix products  8.02 us (4%)
    ppermute x12, starting transfers between devices, shift(): return lax.ppermute(value, axis, hops)  58.5 us
    all_to_all x1, waiting for transfers between devices, step(): terms = lax.all_to_all(pieces, ('yh', 'yl', 'z'), 0, 0, tiled=True)  35.7 us
    all_to_all x1, blocking collectives, step(): mine_rows = lax.all_to_all(spread_rows, ('yl', 'z'), 0, 0, tiled=True)  21.7 us
    ppermute x12, waiting for transfers between devices, shift(): return lax.ppermute(value, axis, hops)  18.5 us
    all_to_all x1, starting transfers between devices, step(): terms = lax.all_to_all(pieces, ('yh', 'yl', 'z'), 0, 0, tiled=True)  17.1 us
    dot_general x5, matrix products, products(): return jnp.dot(terms, block, preferred_element_type=jnp.float32)  4.23 us
    dot_general x2, matrix products, run(): lax.dot_general(stacked, block, (((1,), (1,)), ((), ())), preferred_eleme...  3.78 us
  transfers between devices with their start and end apart: 13, of which 8 were waited for; matrix products, arithmetic and copies ran while one was open for 11% of the time, Pallas kernels for 0%

profile of v4, /device:TPU:1, one launch (start us, length us, event | category | flops | bytes accessed | tf_op | source)
XLA Modules:
  0.0 184.2 jit_solution(563803771952774964)
XLA Ops:
  0.6 0.0 copy-start.2
  0.7 1.2 constant_dynamic-slice_fusion.2
  1.8 8.3 %collective-permute-start = (bf16[80,2560]{1,0:T(8,128)(2,1)S(1)}, bf16[80,2560]{1,0:T(8,128)(2,1)S(1)}, u32[]{:S(2)}, u32[]{:S(2)}) collective-permute-start(bf16[80,2560]{1,0:T(8,128)(2,1)S(1)} %constant_dynamic-slice_fusion.2), channel_id=1, source_target_pairs={{0,4},{4,0},{1,5},{5,1},{2,6},{6,2},{3,7},{7,3},{8,12},{12,8},{9,1... | collective-permute-start | bytes 1228808 | tf_op jit(solution)/shard_map/ppermute | solution.py:28
  10.1 1.9 %subtract_convert_fusion = bf16[160,1024]{1,0:T(8,128)(2,1)} fusion(bf16[160,2048]{1,0:T(8,128)(2,1)} %param.9, s32[]{:T(128)S(6)} %select_n.143, bf16[160,2048]{1,0:T(8,128)(2,1)} %param.8), kind=kLoop, calls=%fused_computation.35 | loop fusion | flops 655360 | bytes 983044 | tf_op jit(solution)/shard_map/convert_element_type | solution.py:58
  12.0 1.9 %collective-permute-start.5 = (bf16[160,1024]{1,0:T(8,128)(2,1)}, bf16[160,1024]{1,0:T(8,128)(2,1)}, u32[]{:S(2)}, u32[]{:S(2)}) collective-permute-start(bf16[160,1024]{1,0:T(8,128)(2,1)} %subtract_convert_fusion), channel_id=1, source_target_pairs={{0,4},{4,0},{1,5},{5,1},{2,6},{6,2},{3,7},{7,3},{8,12},{12,8},{9,1... | collective-permute-start | bytes 983048 | tf_op jit(solution)/shard_map/ppermute | solution.py:28
  13.9 7.3 %collective-permute-start.2 = (s32[5,2560]{1,0:T(8,128)}, s32[5,2560]{1,0:T(8,128)}, u32[]{:S(2)}, u32[]{:S(2)}) collective-permute-start(s32[5,2560]{1,0:T(8,128)} %param.11), channel_id=1, source_target_pairs={{0,4},{4,0},{1,5},{5,1},{2,6},{6,2},{3,7},{7,3},{8,12},{12,8},{9,1... | collective-permute-start | bytes 153608 | tf_op jit(solution)/shard_map/ppermute | solution.py:28
  21.2 3.1 %collective-permute-start.3 = (bf16[256,2560]{1,0:T(8,128)(2,1)}, bf16[256,2560]{1,0:T(8,128)(2,1)S(1)}, u32[]{:S(2)}, u32[]{:S(2)}) collective-permute-start(bf16[256,2560]{1,0:T(8,128)(2,1)} %param.7), channel_id=1, source_target_pairs={{0,1},{1,2},{2,3},{3,0},{4,5},{5,6},{6,7},{7,4},{8,9},{9,10},{10,1... | collective-permute-start | bytes 3932168 | tf_op jit(solution)/shard_map/ppermute | solution.py:28
  24.3 3.4 %collective-permute-start.4 = (bf16[256,2560]{1,0:T(8,128)(2,1)}, bf16[256,2560]{1,0:T(8,128)(2,1)}, u32[]{:S(2)}, u32[]{:S(2)}) collective-permute-start(bf16[256,2560]{1,0:T(8,128)(2,1)} %param.7), channel_id=1, source_target_pairs={{0,3},{1,0},{2,1},{3,2},{4,7},{5,4},{6,5},{7,6},{8,11},{9,8},{10,9... | collective-permute-start | bytes 3932168 | tf_op jit(solution)/shard_map/ppermute | solution.py:28
  27.8 0.1 shift_right_arithmetic.65
  27.9 9.0 %collective-permute-done.2 = s32[5,2560]{1,0:T(8,128)} collective-permute-done((s32[5,2560]{1,0:T(8,128)}, s32[5,2560]{1,0:T(8,128)}, u32[]{:S(2)}, u32[]{:S(2)}) %collective-permute-start.2) | collective-permute-done | bytes 51232 | tf_op jit(solution)/shard_map/ppermute | solution.py:28
  36.9 1.6 fusion.14
  38.6 11.3 %collective-permute-start.1 = (bf16[80,2560]{1,0:T(8,128)(2,1)S(1)}, bf16[80,2560]{1,0:T(8,128)(2,1)S(1)}, u32[]{:S(2)}, u32[]{:S(2)}) collective-permute-start(bf16[80,2560]{1,0:T(8,128)(2,1)S(1)} %collective-permute-done), channel_id=1, source_target_pairs={{0,8},{8,0},{1,9},{9,1},{2,10},{10,2},{3,11},{11,3},{4,12},{12,4},... | collective-permute-start | bytes 1228808 | tf_op jit(solution)/shard_map/ppermute | solution.py:28
  49.9 1.2 convert_select_fusion.1
  51.1 0.2 maximum_maximum_fusion
  51.3 0.1 broadcast_select_fusion.3
  51.3 0.9 copy-done
  52.2 0.3 broadcast_select_fusion.1
  52.5 0.9 collective-permute-done.3
  53.4 2.5 %collective-permute-start.6 = (bf16[128,2560]{1,0:T(8,128)(2,1)S(1)}, bf16[128,2560]{1,0:T(8,128)(2,1)S(1)}, u32[]{:S(2)}, u32[]{:S(2)}) collective-permute-start(bf16[128,2560]{1,0:T(8,128)(2,1)S(1)} %slice.50), channel_id=1, source_target_pairs={{0,1},{1,2},{2,3},{3,0},{4,5},{5,6},{6,7},{7,4},{8,9},{9,10},{10,1... | collective-permute-start | bytes 1966088 | tf_op jit(solution)/shard_map/ppermute | solution.py:28
  55.9 1.1 slice.51
  57.1 4.1 %collective-permute-start.7 = (bf16[128,2560]{1,0:T(8,128)(2,1)S(1)}, bf16[128,2560]{1,0:T(8,128)(2,1)S(1)}, u32[]{:S(2)}, u32[]{:S(2)}) collective-permute-start(bf16[128,2560]{1,0:T(8,128)(2,1)S(1)} %slice.51), channel_id=1, source_target_pairs={{0,3},{1,0},{2,1},{3,2},{4,7},{5,4},{6,5},{7,6},{8,11},{9,8},{10,9... | collective-permute-start | bytes 1966088 | tf_op jit(solution)/shard_map/ppermute | solution.py:28
  61.2 0.1 constant_dynamic-update-slice_fusion.2
  61.3 0.1 constant_dynamic-update-slice_fusion.1
  61.4 1.4 constant_dynamic-update-slice_fusion
  62.8 2.7 %fusion.16 = f32[640,768]{1,0:T(8,128)S(1)} fusion(bf16[768,2560]{1,0:T(8,128)(2,1)S(1)} %constant_dynamic-update-slice_fusion, bf16[160,2560]{1,0:T(8,128)(2,1)S(1)} %get-tuple-element.36, bf16[160,2560]{1,0:T(8,128)(2,1)S(1)} %get-tuple-element.35, bf16[160,2560]{1,0:T(8,128)(2,1)S(1)} %get-tuple-element.30, bf16[160,2560]{1,0:T(8,128)(2,1)S(1)} %get-tuple-element.29), kind=kOutput, calls=%fused_computation.38 | convolution fusion | flops 2529689600 | bytes 9175040 | tf_op jit(solution)/shard_map/dot_general | solution.py:81
  65.5 0.7 fusion.12
  66.2 1.4 fusion.17
  67.6 1.4 fusion.19
  69.1 1.5 collective-permute-done.6
  70.6 2.5 %collective-permute-done.7 = bf16[128,2560]{1,0:T(8,128)(2,1)S(1)} collective-permute-done((bf16[128,2560]{1,0:T(8,128)(2,1)S(1)}, bf16[128,2560]{1,0:T(8,128)(2,1)S(1)}, u32[]{:S(2)}, u32[]{:S(2)}) %collective-permute-start.7) | collective-permute-done | bytes 655392 | tf_op jit(solution)/shard_map/ppermute | solution.py:28
  73.2 1.1 fusion.15
  74.2 0.2 broadcast_select_fusion.4
  74.5 0.4 slice_add_fusion.2
  74.8 0.4 slice_add_fusion.3
  75.2 5.0 %collective-permute-start.8 = (f32[160,2560]{1,0:T(8,128)S(1)}, f32[160,2560]{1,0:T(8,128)S(1)}, u32[]{:S(2)}, u32[]{:S(2)}) collective-permute-start(f32[160,2560]{1,0:T(8,128)S(1)} %slice_add_fusion.3), channel_id=1, source_target_pairs={{0,8},{8,0},{1,9},{9,1},{2,10},{10,2},{3,11},{11,3},{4,12},{12,4},... | collective-permute-start | bytes 4915208 | tf_op jit(solution)/shard_map/ppermute | solution.py:28
  80.2 1.9 %collective-permute-start.9 = (f32[160,2560]{1,0:T(8,128)S(1)}, f32[160,2560]{1,0:T(8,128)S(1)}, u32[]{:S(2)}, u32[]{:S(2)}) collective-permute-start(f32[160,2560]{1,0:T(8,128)S(1)} %slice_add_fusion.2), channel_id=1, source_target_pairs={{0,8},{8,0},{1,9},{9,1},{2,10},{10,2},{3,11},{11,3},{4,12},{12,4},... | collective-permute-start | bytes 4915208 | tf_op jit(solution)/shard_map/ppermute | solution.py:28
  82.1 0.6 fusion.26
  82.7 0.6 add.106
  83.3 0.0 collective-permute-done.8
  83.3 2.3 %collective-permute-done.9 = f32[160,2560]{1,0:T(8,128)S(1)} collective-permute-done((f32[160,2560]{1,0:T(8,128)S(1)}, f32[160,2560]{1,0:T(8,128)S(1)}, u32[]{:S(2)}, u32[]{:S(2)}) %collective-permute-start.9) | collective-permute-done | bytes 1638432 | tf_op jit(solution)/shard_map/ppermute | solution.py:28
  85.7 0.6 fusion.1
  86.3 0.1 pad_maximum_fusion.1
  86.4 3.0 %convert_element_type.69 = bf16[64,100,128]{2,1,0:T(8,128)(2,1)} reshape(bf16[320,2560]{1,0:T(8,128)(2,1)S(1)} %pad_maximum_fusion.1) | data formatting | bytes 3276800 | tf_op jit(solution)/shard_map/convert_element_type | solution.py:112
  89.4 17.1 %all-to-all-start = ((bf16[64,100,128]{2,1,0:T(8,128)(2,1)}), bf16[64,100,128]{2,1,0:T(8,128)(2,1)S(1)}, u32[]{:S(2)}, u32[]{:S(2)}) async-start(bf16[64,100,128]{2,1,0:T(8,128)(2,1)} %convert_element_type.69), calls=%async_computation | async-start | bytes 3407872 | tf_op jit(solution)/shard_map/all_to_all | solution.py:122
  106.5 1.9 %reshape.28 = bf16[3200,128]{1,0:T(8,128)(2,1)} reshape(bf16[160,2560]{1,0:T(8,128)(2,1)S(1)} %copy-done) | data formatting | bytes 1638400 | tf_op jit(solution)/shard_map/reshape | solution.py:119
  108.4 0.1 shift_right_arithmetic.72
  108.5 0.1 shift_right_arithmetic.73
  108.6 0.2 shift_right_arithmetic.62
  108.8 1.3 shift_right_arithmetic.71
  110.0 0.1 dynamic-slice
  110.1 0.7 constant_dynamic-slice_fusion
  110.8 0.8 fusion.41
  111.7 35.7 %all-to-all-done = bf16[64,100,128]{2,1,0:T(8,128)(2,1)S(1)} async-done(((bf16[64,100,128]{2,1,0:T(8,128)(2,1)}), bf16[64,100,128]{2,1,0:T(8,128)(2,1)S(1)}, u32[]{:S(2)}, u32[]{:S(2)}) %all-to-all-start) | async-done | bytes 1638432 | tf_op jit(solution)/shard_map/all_to_all | solution.py:122
  147.4 0.3 convert_reduce_fusion
  147.8 5.5 %collective-permute-start.10 = (f32[50,128]{1,0:T(8,128)S(1)}, f32[50,128]{1,0:T(8,128)S(1)}, u32[]{:S(2)}, u32[]{:S(2)}) collective-permute-start(f32[50,128]{1,0:T(8,128)S(1)} %constant_dynamic-slice_fusion.1), channel_id=1, source_target_pairs={{0,8},{8,0},{1,9},{9,1},{2,10},{10,2},{3,11},{11,3},{4,12},{12,4},... | collective-permute-start | bytes 76808 | tf_op jit(solution)/shard_map/ppermute | solution.py:28
  153.3 0.8 collective-permute-done.10
  154.1 0.6 subtract_convert_fusion.1
  154.8 0.1 broadcast_in_dim.2
  154.8 21.7 %all_to_all.10 = bf16[32,50,128]{2,1,0:T(8,128)(2,1)S(1)} all-to-all(bf16[32,50,128]{2,1,0:T(8,128)(2,1)S(1)} %broadcast_in_dim.2), channel_id=1, replica_groups=mesh['yl'=4,'z'=8,'c'=2,'yh'=2,'x'=4] {'yl','z'}, dimensions={0} | all-to-all | bytes 819200 | tf_op jit(solution)/shard_map/all_to_all | solution.py:143
  176.6 4.3 %collective-permute-start.11 = (bf16[32,50,128]{2,1,0:T(8,128)(2,1)S(1)}, bf16[32,50,128]{2,1,0:T(8,128)(2,1)S(1)}, u32[]{:S(2)}, u32[]{:S(2)}) collective-permute-start(bf16[32,50,128]{2,1,0:T(8,128)(2,1)S(1)} %all_to_all.10), channel_id=1, source_target_pairs={{0,8},{8,0},{1,9},{9,1},{2,10},{10,2},{3,11},{11,3},{4,12},{12,4},... | collective-permute-start | bytes 1228808 | tf_op jit(solution)/shard_map/ppermute | solution.py:28
  180.9 1.4 collective-permute-done.11
  182.3 0.1 select_bitcast_fusion.1
  182.3 0.1 pad_maximum_fusion.2
  182.4 1.8 reshape.29
  (21 shorter events, 0.2 us)
Async XLA Ops:
  0.6 49.2 %copy-start.2 = (bf16[160,2048]{1,0:T(8,128)(2,1)S(1)}, bf16[160,2048]{1,0:T(8,128)(2,1)}, u32[]{:S(2)}) copy-start(bf16[160,2048]{1,0:T(8,128)(2,1)} %param.9) | copy-start | bytes 1966084
  0.6 49.2 %copy-start.3 = (bf16[160,2048]{1,0:T(8,128)(2,1)S(1)}, bf16[160,2048]{1,0:T(8,128)(2,1)}, u32[]{:S(2)}) copy-start(bf16[160,2048]{1,0:T(8,128)(2,1)} %param.8) | copy-start | bytes 1966084
  0.7 36.2 %copy-start.4 = (s32[5,2560]{1,0:T(8,128)S(1)}, s32[5,2560]{1,0:T(8,128)}, u32[]{:S(2)}) copy-start(s32[5,2560]{1,0:T(8,128)} %param.11) | copy-start | bytes 153604
  1.8 36.7 %collective-permute-start = (bf16[80,2560]{1,0:T(8,128)(2,1)S(1)}, bf16[80,2560]{1,0:T(8,128)(2,1)S(1)}, u32[]{:S(2)}, u32[]{:S(2)}) collective-permute-start(bf16[80,2560]{1,0:T(8,128)(2,1)S(1)} %constant_dynamic-slice_fusion.2), channel_id=1, source_target_pairs={{0,4},{4,0},{1,5},{5,1},{2,6},{6,2},{3,7},{7,3},{8,12},{12,8},{9,1... | collective-permute-start | bytes 1228808 | tf_op jit(solution)/shard_map/ppermute | solution.py:28
  12.0 37.8 %collective-permute-start.5 = (bf16[160,1024]{1,0:T(8,128)(2,1)}, bf16[160,1024]{1,0:T(8,128)(2,1)}, u32[]{:S(2)}, u32[]{:S(2)}) collective-permute-start(bf16[160,1024]{1,0:T(8,128)(2,1)} %subtract_convert_fusion), channel_id=1, source_target_pairs={{0,4},{4,0},{1,5},{5,1},{2,6},{6,2},{3,7},{7,3},{8,12},{12,8},{9,1... | collective-permute-start | bytes 983048 | tf_op jit(solution)/shard_map/ppermute | solution.py:28
  13.9 23.0 %collective-permute-start.2 = (s32[5,2560]{1,0:T(8,128)}, s32[5,2560]{1,0:T(8,128)}, u32[]{:S(2)}, u32[]{:S(2)}) collective-permute-start(s32[5,2560]{1,0:T(8,128)} %param.11), channel_id=1, source_target_pairs={{0,4},{4,0},{1,5},{5,1},{2,6},{6,2},{3,7},{7,3},{8,12},{12,8},{9,1... | collective-permute-start | bytes 153608 | tf_op jit(solution)/shard_map/ppermute | solution.py:28
  21.2 32.1 %collective-permute-start.3 = (bf16[256,2560]{1,0:T(8,128)(2,1)}, bf16[256,2560]{1,0:T(8,128)(2,1)S(1)}, u32[]{:S(2)}, u32[]{:S(2)}) collective-permute-start(bf16[256,2560]{1,0:T(8,128)(2,1)} %param.7), channel_id=1, source_target_pairs={{0,1},{1,2},{2,3},{3,0},{4,5},{5,6},{6,7},{7,4},{8,9},{9,10},{10,1... | collective-permute-start | bytes 3932168 | tf_op jit(solution)/shard_map/ppermute | solution.py:28
  24.3 31.6 %collective-permute-start.4 = (bf16[256,2560]{1,0:T(8,128)(2,1)}, bf16[256,2560]{1,0:T(8,128)(2,1)}, u32[]{:S(2)}, u32[]{:S(2)}) collective-permute-start(bf16[256,2560]{1,0:T(8,128)(2,1)} %param.7), channel_id=1, source_target_pairs={{0,3},{1,0},{2,1},{3,2},{4,7},{5,4},{6,5},{7,6},{8,11},{9,8},{10,9... | collective-permute-start | bytes 3932168 | tf_op jit(solution)/shard_map/ppermute | solution.py:28
  38.6 12.7 %collective-permute-start.1 = (bf16[80,2560]{1,0:T(8,128)(2,1)S(1)}, bf16[80,2560]{1,0:T(8,128)(2,1)S(1)}, u32[]{:S(2)}, u32[]{:S(2)}) collective-permute-start(bf16[80,2560]{1,0:T(8,128)(2,1)S(1)} %collective-permute-done), channel_id=1, source_target_pairs={{0,8},{8,0},{1,9},{9,1},{2,10},{10,2},{3,11},{11,3},{4,12},{12,4},... | collective-permute-start | bytes 1228808 | tf_op jit(solution)/shard_map/ppermute | solution.py:28
  51.0 1.2 copy-start
  53.4 7.9 %copy-start.1 = (bf16[256,2560]{1,0:T(8,128)(2,1)S(1)}, bf16[256,2560]{1,0:T(8,128)(2,1)}, u32[]{:S(2)}) copy-start(bf16[256,2560]{1,0:T(8,128)(2,1)} %param.7) | copy-start | bytes 3932164
  53.4 17.2 %collective-permute-start.6 = (bf16[128,2560]{1,0:T(8,128)(2,1)S(1)}, bf16[128,2560]{1,0:T(8,128)(2,1)S(1)}, u32[]{:S(2)}, u32[]{:S(2)}) collective-permute-start(bf16[128,2560]{1,0:T(8,128)(2,1)S(1)} %slice.50), channel_id=1, source_target_pairs={{0,1},{1,2},{2,3},{3,0},{4,5},{5,6},{6,7},{7,4},{8,9},{9,10},{10,1... | collective-permute-start | bytes 1966088 | tf_op jit(solution)/shard_map/ppermute | solution.py:28
  57.1 16.0 %collective-permute-start.7 = (bf16[128,2560]{1,0:T(8,128)(2,1)S(1)}, bf16[128,2560]{1,0:T(8,128)(2,1)S(1)}, u32[]{:S(2)}, u32[]{:S(2)}) collective-permute-start(bf16[128,2560]{1,0:T(8,128)(2,1)S(1)} %slice.51), channel_id=1, source_target_pairs={{0,3},{1,0},{2,1},{3,2},{4,7},{5,4},{6,5},{7,6},{8,11},{9,8},{10,9... | collective-permute-start | bytes 1966088 | tf_op jit(solution)/shard_map/ppermute | solution.py:28
  75.2 8.1 %collective-permute-start.8 = (f32[160,2560]{1,0:T(8,128)S(1)}, f32[160,2560]{1,0:T(8,128)S(1)}, u32[]{:S(2)}, u32[]{:S(2)}) collective-permute-start(f32[160,2560]{1,0:T(8,128)S(1)} %slice_add_fusion.3), channel_id=1, source_target_pairs={{0,8},{8,0},{1,9},{9,1},{2,10},{10,2},{3,11},{11,3},{4,12},{12,4},... | collective-permute-start | bytes 4915208 | tf_op jit(solution)/shard_map/ppermute | solution.py:28
  80.2 5.5 %collective-permute-start.9 = (f32[160,2560]{1,0:T(8,128)S(1)}, f32[160,2560]{1,0:T(8,128)S(1)}, u32[]{:S(2)}, u32[]{:S(2)}) collective-permute-start(f32[160,2560]{1,0:T(8,128)S(1)} %slice_add_fusion.2), channel_id=1, source_target_pairs={{0,8},{8,0},{1,9},{9,1},{2,10},{10,2},{3,11},{11,3},{4,12},{12,4},... | collective-permute-start | bytes 4915208 | tf_op jit(solution)/shard_map/ppermute | solution.py:28
  89.4 58.0 %all-to-all-start = ((bf16[64,100,128]{2,1,0:T(8,128)(2,1)}), bf16[64,100,128]{2,1,0:T(8,128)(2,1)S(1)}, u32[]{:S(2)}, u32[]{:S(2)}) async-start(bf16[64,100,128]{2,1,0:T(8,128)(2,1)} %convert_element_type.69), calls=%async_computation | async-start | bytes 3407872 | tf_op jit(solution)/shard_map/all_to_all | solution.py:122
  108.7 45.4 %copy-start.5 = (f32[50,128]{1,0:T(8,128)S(1)}, f32[50,128]{1,0:T(8,128)}, u32[]{:S(2)}) copy-start(f32[50,128]{1,0:T(8,128)} %param.12) | copy-start | bytes 76804
  108.7 45.4 %copy-start.6 = (f32[50,128]{1,0:T(8,128)S(1)}, f32[50,128]{1,0:T(8,128)}, u32[]{:S(2)}) copy-start(f32[50,128]{1,0:T(8,128)} %param.13) | copy-start | bytes 76804
  147.8 6.4 %collective-permute-start.10 = (f32[50,128]{1,0:T(8,128)S(1)}, f32[50,128]{1,0:T(8,128)S(1)}, u32[]{:S(2)}, u32[]{:S(2)}) collective-permute-start(f32[50,128]{1,0:T(8,128)S(1)} %constant_dynamic-slice_fusion.1), channel_id=1, source_target_pairs={{0,8},{8,0},{1,9},{9,1},{2,10},{10,2},{3,11},{11,3},{4,12},{12,4},... | collective-permute-start | bytes 76808 | tf_op jit(solution)/shard_map/ppermute | solution.py:28
  176.6 5.7 %collective-permute-start.11 = (bf16[32,50,128]{2,1,0:T(8,128)(2,1)S(1)}, bf16[32,50,128]{2,1,0:T(8,128)(2,1)S(1)}, u32[]{:S(2)}, u32[]{:S(2)}) collective-permute-start(bf16[32,50,128]{2,1,0:T(8,128)(2,1)S(1)} %all_to_all.10), channel_id=1, source_target_pairs={{0,8},{8,0},{1,9},{9,1},{2,10},{10,2},{3,11},{11,3},{4,12},{12,4},... | collective-permute-start | bytes 1228808 | tf_op jit(solution)/shard_map/ppermute | solution.py:28

commit v5 on v4

v5 whole, which is shorter than its diff:
```python
import math

import jax
import jax.numpy as jnp
from jax import lax
from jax.experimental import pallas as pl
from jax.experimental.pallas import tpu as pltpu
from jax.sharding import Mesh, PartitionSpec as P


OPT_STEP = 10


beta_one = 0.9
beta_two = 0.999
learn_rate = 0.15
epsilon = 0.0001


def size(axis):
    return 8 if axis == "y" else lax.axis_size(axis)


def shift(value, axis, by):
    n = size(axis)
    hops = [(i, (i + by) % n) for i in range(n)]
    if axis == "y":
        at = [2 * (y % 4) + y // 4 for y in range(n)]
        return lax.ppermute(value, ("yl", "yh"), [(at[i], at[j]) for i, j in hops])
    return lax.ppermute(value, axis, hops)


def unpack_signs(signs):
    shifts = jnp.arange(32, dtype=jnp.int32)
    bit_values = jnp.bitwise_and(jnp.right_shift(signs[:, None, :], shifts[None, :, None]), 1)
    return (1 - 2 * bit_values).reshape(signs.shape[0] * 32, signs.shape[1]).astype(jnp.bfloat16)


def cut_kernel(half_ref, *refs):
    out_ref, lines = refs[6:]
    piece = out_ref.shape[1]
    per_row = refs[0].shape[1] // 128
    block = 8 * piece // per_row
    steps = refs[0].shape[0] // block

    for part in range(2):
        near_ref, far_ref, got_ref = refs[3 * part : 3 * part + 3]
        side = half_ref[0] if part == 0 else 1 - half_ref[0]

        @pl.loop(0, steps)
        def _(step):
            base = pl.multiple_of(step * block, 8)
            for group in range(0, block, 8):
                at = pl.ds(base + group, 8)
                rows = near_ref[at, :] + far_ref[at, :] + got_ref[at, :]
                for lane in range(per_row):
                    lines[pl.ds(group * per_row + lane, 8, stride=per_row), :] = rows[
                        :, lane * 128 : (lane + 1) * 128
                    ]
            for i in range(8):
                out_ref[(side * steps + step) * 8 + i] = lines[i * piece : (i + 1) * piece, :].astype(
                    jnp.bfloat16
                )


def cut(half, terms, plane):
    cells = 2 * terms[0].size
    piece = cells // (plane * 128)
    whole = pl.BlockSpec(memory_space=pltpu.VMEM)
    return pl.pallas_call(
        cut_kernel,
        out_shape=jax.ShapeDtypeStruct((plane, piece, 128), jnp.bfloat16),
        in_specs=[pl.BlockSpec(memory_space=pltpu.SMEM)] + [whole] * 6,
        out_specs=whole,
        scratch_shapes=[pltpu.VMEM((8 * piece, 128), jnp.float32)],
        compiler_params=pltpu.CompilerParams(vmem_limit_bytes=20 << 20),
        cost_estimate=pl.CostEstimate(flops=2 * cells, bytes_accessed=14 * cells, transcendentals=0),
        name="cut",
    )(half.reshape(1).astype(jnp.int32), *terms)


def step(hidden, resid, target, w_out, signs, m_old, v_old):
    features, _ = w_out.shape
    tokens = hidden.shape[0]
    group = tokens * lax.axis_size("x")
    half = lax.axis_index("yh")
    core = lax.axis_index("c")
    col = lax.axis_index("x")

    cutoff = tokens // 2
    top, low = hidden[:cutoff], hidden[cutoff:]
    left_top = shift(top, "x", 1)
    right_low = shift(low, "x", -1)
    left_low = shift(low, "x", 1)
    right_top = shift(top, "x", -1)
    far_top = shift(left_top, "x", 1)
    far_low = shift(right_low, "x", -1)

    rows = features // 2
    part = shift(lax.dynamic_slice_in_dim(w_out, core * rows, rows, 0), "yh", 1)
    other_signs = shift(signs, "yh", 1)

    def gap(at, kind):
        def part(whole):
            return lax.dynamic_slice_in_dim(whole, at * group, group, 1).astype(jnp.float32)

        gaps = (part(resid) - part(target)).astype(kind)
        gaps = jnp.concatenate([gaps, gaps], axis=1)
        return lax.dynamic_slice_in_dim(gaps, ((col + 3) % 4) * tokens, group, 1)

    other_gaps = shift(gap(1 - half, jnp.bfloat16), "yh", 1)
    twin = shift(part, "c", 1)
    probes = unpack_signs(signs)
    own_stack = jnp.concatenate([w_out, probes], axis=0)
    own_gaps = gap(half, jnp.float32)
    left_top, left_low, right_top, right_low, twin = lax.optimization_barrier(
        (left_top, left_low, right_top, right_low, twin)
    )
    other_signs, _ = lax.optimization_barrier((other_signs, probes))
    other_stack = jnp.concatenate(
        [
            jnp.where(core == 0, part, twin),
            jnp.where(core == 0, twin, part),
            unpack_signs(other_signs),
        ],
        axis=0,
    )

    def run(stacked, gaps, block):
        here = gaps[:, : block.shape[0]] if block.shape[0] > tokens else gaps[:, -tokens:]
        forward = lax.dot_general(
            stacked, block, (((1,), (1,)), ((), ())), preferred_element_type=jnp.float32
        )
        misfit = here.astype(jnp.float32) + forward[:features]
        spread = 1.0 + misfit * misfit
        rooted = jnp.sqrt(spread)
        slopes = (misfit / rooted).astype(jnp.bfloat16)
        bends = (forward[features:] / (spread * rooted)).astype(jnp.bfloat16)
        away = jnp.where(core == 0, bends, slopes)
        kept = jnp.where(core == 0, slopes, bends)
        return [jnp.dot(terms, block, preferred_element_type=jnp.float32) for terms in (away, kept)]

    near = jnp.concatenate([left_top, left_low, hidden, right_top, right_low], axis=0)
    own_away, own_kept = run(own_stack, own_gaps, near)
    other_away, other_kept = run(other_stack, other_gaps, near)
    own_away, own_kept, other_away, other_kept, far_top, far_low = lax.optimization_barrier(
        (own_away, own_kept, other_away, other_kept, far_top, far_low)
    )
    far = jnp.concatenate([far_top, far_low], axis=0)
    own_far = run(own_stack, own_gaps, far)
    own_got = shift(own_away + own_far[0], "c", 1)
    other_far = run(other_stack, other_gaps, far)
    other_got = shift(other_away + other_far[0], "c", 1)
    pieces = cut(half, (own_kept, own_far[1], own_got, other_kept, other_far[1], other_got), 64)

    each = m_old.shape[0]
    row_start = (
        (lax.axis_index("yl") * lax.axis_size("z") + lax.axis_index("z")) * 2 + core
    ) * each
    my_probes = lax.dynamic_slice_in_dim(unpack_signs(signs).reshape(-1, 128), row_start, each, 0)
    own_rows = lax.dynamic_slice_in_dim(w_out.reshape(-1, 128), row_start, each, 0)
    terms = lax.all_to_all(pieces, ("yh", "yl", "z"), 0, 0, tiled=True)
    terms, my_probes, own_rows = lax.optimization_barrier((terms, my_probes, own_rows))
    total = jnp.sum(terms.astype(jnp.float32), axis=0)
    keep_rows = lax.dynamic_slice_in_dim(total, core * each, each, 0)
    send_rows = lax.dynamic_slice_in_dim(total, (1 - core) * each, each, 0)
    got_rows = shift(send_rows, "c", 1)
    grad_mine = jnp.where(core == 0, keep_rows, got_rows)
    curve_mine = jnp.where(core == 0, got_rows, keep_rows)

    scaling = 1.0 / math.sqrt(tokens * 512)
    gradient = grad_mine * scaling
    curvature = curve_mine * scaling
    diag_est = my_probes.astype(jnp.float32) * curvature
    new_m = beta_one * m_old + (1.0 - beta_one) * gradient
    new_v = beta_two * v_old + (1.0 - beta_two) * diag_est * diag_est
    first_fix = 1.0 - beta_one**OPT_STEP
    second_fix = 1.0 - beta_two**OPT_STEP
    update = new_m / first_fix / (jnp.sqrt(new_v / second_fix) + epsilon)
    fresh = (own_rows.astype(jnp.float32) - learn_rate * update).astype(jnp.bfloat16)

    spread_rows = jnp.broadcast_to(fresh[None], (32, *fresh.shape))
    mine_rows = lax.all_to_all(spread_rows, ("yl", "z"), 0, 0, tiled=True)
    twin_rows = shift(mine_rows, "c", 1)
    both = jnp.stack([jnp.where(core == 0, mine_rows, twin_rows), jnp.where(core == 0, twin_rows, mine_rows)], axis=1)
    new_w = both.reshape(w_out.shape)
    return (new_w, new_m, new_v)


def solution(mesh):
    fine = Mesh(mesh.devices.reshape(4, 8, 2, 2, 4), ("yl", "z", "c", "yh", "x"))
    dp, shard = ("yl", "z", "c"), ("yh", "x")
    return jax.shard_map(
        step,
        mesh=fine,
        in_specs=(
            P(dp + shard, None),
            P(shard, dp),
            P(shard, dp),
            P(shard, None),
            P(shard, None),
            P(shard + dp, None),
            P(shard + dp, None),
        ),
        out_specs=(P(shard, None), P(shard + dp, None), P(shard + dp, None)),
        check_vma=False,
    )
```

time: 185 us -> 176 us (0.951)
  waiting for transfers between devices: 54.2 us -> 43.9 us
  other arithmetic: 9.41 us -> 6.45 us
  blocking collectives: 21.7 us -> 23.7 us
  Pallas kernels: 0 us -> 1.91 us
    ppermute x12 -> x14, waiting for transfers between devices: 18.5 us -> 7.92 us  [shift(): return lax.ppermute(value, axis, hops)]
    all_to_all x1, starting transfers between devices: 17.1 us -> 13.2 us  [step(): terms = lax.all_to_all(pieces, ('yh', 'yl', 'z'), 0, 0, tiled=True)]
    ppermute x12 -> x14, starting transfers between devices: 58.5 us -> 62.2 us  [shift(): return lax.ppermute(value, axis, hops)]
    select_n x4 -> x0, other arithmetic: 3.36 us -> none  [the longest x3 3.12 us: in_order(): jnp.where(half == 0, own, other)]
    convert_element_type x1 -> x0, local copies, waits for them, and re-layouts: 3.04 us -> none  [step(): mine = jnp.concatenate([kept_all[:features] + got[0], kept_all[features:]...]
    unnamed x17, local copies, waits for them, and re-layouts: 1.13 us -> 3.63 us
    all_to_all x1, blocking collectives: 21.7 us -> 23.7 us  [step(): mine_rows = lax.all_to_all(spread_rows, ('yl', 'z'), 0, 0, tiled=True)]
    pallas_call x0 -> x1, Pallas kernels: none -> 1.91 us  [cut(): pl.pallas_call(cut_kernel, out_shape=jax.ShapeDtypeStruct((plane, piece,...]
  transfers between devices with their start and end apart: 13 -> 15, of which waited for: 8 -> 6; matrix products, arithmetic and copies ran while one was open for 11% -> 13% of each run, Pallas kernels for 0% -> 0%
where the time goes in v5:
time: 176 us; the launch traced here: 175 us
  starting transfers between devices  75.4 us (43%)
  waiting for transfers between devices  43.9 us (25%)
  blocking collectives  23.7 us (13%)
  local copies, waits for them, and re-layouts  13.5 us (8%)
  matrix products  9.3 us (5%)
  other arithmetic  6.45 us (4%)
  Pallas kernels  1.91 us (1%)
    ppermute x14, starting transfers between devices, shift(): return lax.ppermute(value, axis, hops)  62.2 us
    all_to_all x1, waiting for transfers between devices, step(): terms = lax.all_to_all(pieces, ('yh', 'yl', 'z'), 0, 0, tiled=True)  36 us
    all_to_all x1, blocking collectives, step(): mine_rows = lax.all_to_all(spread_rows, ('yl', 'z'), 0, 0, tiled=True)  23.7 us
    all_to_all x1, starting transfers between devices, step(): terms = lax.all_to_all(pieces, ('yh', 'yl', 'z'), 0, 0, tiled=True)  13.2 us
    ppermute x14, waiting for transfers between devices, shift(): return lax.ppermute(value, axis, hops)  7.92 us
    dot_general x8, matrix products, run(): jnp.dot(terms, block, preferred_element_type=jnp.float32)  5.14 us
    dot_general x4, matrix products, run(): lax.dot_general(stacked, block, (((1,), (1,)), ((), ())), preferred_eleme...  4.16 us
    unnamed x17, local copies, waits for them, and re-layouts  3.63 us
  transfers between devices with their start and end apart: 15, of which 6 were waited for; matrix products, arithmetic and copies ran while one was open for 13% of the time, Pallas kernels for 0%

profile of v5, /device:TPU:1, one launch (start us, length us, event | category | flops | bytes accessed | tf_op | source)
XLA Modules:
  0.0 175.3 jit_solution(7355484344814705055)
XLA Ops:
  0.6 1.1 constant_dynamic-slice_fusion.2
  1.7 8.4 %collective-permute-start.4 = (bf16[80,2560]{1,0:T(8,128)(2,1)S(1)}, bf16[80,2560]{1,0:T(8,128)(2,1)S(1)}, u32[]{:S(2)}, u32[]{:S(2)}) collective-permute-start(bf16[80,2560]{1,0:T(8,128)(2,1)S(1)} %constant_dynamic-slice_fusion.2), channel_id=1, source_target_pairs={{0,4},{4,0},{1,5},{5,1},{2,6},{6,2},{3,7},{7,3},{8,12},{12,8},{9,1... | collective-permute-start | bytes 1228808 | tf_op jit(solution)/shard_map/ppermute | solution.py:30
  10.1 1.9 %collective-permute-start.6 = (s32[5,2560]{1,0:T(8,128)}, s32[5,2560]{1,0:T(8,128)S(1)}, u32[]{:S(2)}, u32[]{:S(2)}) collective-permute-start(s32[5,2560]{1,0:T(8,128)} %param.11), channel_id=1, source_target_pairs={{0,4},{4,0},{1,5},{5,1},{2,6},{6,2},{3,7},{7,3},{8,12},{12,8},{9,1... | collective-permute-start | bytes 153608 | tf_op jit(solution)/shard_map/ppermute | solution.py:30
  12.1 1.4 fusion.64
  13.4 3.1 %collective-permute-start = (bf16[128,2560]{1,0:T(8,128)(2,1)S(1)}, bf16[128,2560]{1,0:T(8,128)(2,1)}, u32[]{:S(2)}, u32[]{:S(2)}) collective-permute-start(bf16[128,2560]{1,0:T(8,128)(2,1)S(1)} %get-tuple-element.41), channel_id=1, source_target_pairs={{0,1},{1,2},{2,3},{3,0},{4,5},{5,6},{6,7},{7,4},{8,9},{9,10},{10,1... | collective-permute-start | bytes 1966088 | tf_op jit(solution)/shard_map/ppermute | solution.py:30
  16.6 3.4 %collective-permute-start.3 = (bf16[128,2560]{1,0:T(8,128)(2,1)S(1)}, bf16[128,2560]{1,0:T(8,128)(2,1)}, u32[]{:S(2)}, u32[]{:S(2)}) collective-permute-start(bf16[128,2560]{1,0:T(8,128)(2,1)S(1)} %get-tuple-element.40), channel_id=1, source_target_pairs={{0,3},{1,0},{2,1},{3,2},{4,7},{5,4},{6,5},{7,6},{8,11},{9,8},{10,9... | collective-permute-start | bytes 1966088 | tf_op jit(solution)/shard_map/ppermute | solution.py:30
  20.0 1.9 %collective-permute-start.1 = (bf16[128,2560]{1,0:T(8,128)(2,1)S(1)}, bf16[128,2560]{1,0:T(8,128)(2,1)}, u32[]{:S(2)}, u32[]{:S(2)}) collective-permute-start(bf16[128,2560]{1,0:T(8,128)(2,1)S(1)} %get-tuple-element.40), channel_id=1, source_target_pairs={{0,1},{1,2},{2,3},{3,0},{4,5},{5,6},{6,7},{7,4},{8,9},{9,10},{10,1... | collective-permute-start | bytes 1966088 | tf_op jit(solution)/shard_map/ppermute | solution.py:30
  21.9 2.1 %collective-permute-done.6 = s32[5,2560]{1,0:T(8,128)S(1)} collective-permute-done((s32[5,2560]{1,0:T(8,128)}, s32[5,2560]{1,0:T(8,128)S(1)}, u32[]{:S(2)}, u32[]{:S(2)}) %collective-permute-start.6) | collective-permute-done | bytes 51232 | tf_op jit(solution)/shard_map/ppermute | solution.py:30
  24.0 4.9 %collective-permute-start.2 = (bf16[128,2560]{1,0:T(8,128)(2,1)S(1)}, bf16[128,2560]{1,0:T(8,128)(2,1)}, u32[]{:S(2)}, u32[]{:S(2)}) collective-permute-start(bf16[128,2560]{1,0:T(8,128)(2,1)S(1)} %get-tuple-element.41), channel_id=1, source_target_pairs={{0,3},{1,0},{2,1},{3,2},{4,7},{5,4},{6,5},{7,6},{8,11},{9,8},{10,9... | collective-permute-start | bytes 1966088 | tf_op jit(solution)/shard_map/ppermute | solution.py:30
  28.9 9.9 %collective-permute-start.5 = (bf16[80,2560]{1,0:T(8,128)(2,1)S(1)}, bf16[80,2560]{1,0:T(8,128)(2,1)}, u32[]{:S(2)}, u32[]{:S(2)}) collective-permute-start(bf16[80,2560]{1,0:T(8,128)(2,1)S(1)} %collective-permute-done.4), channel_id=1, source_target_pairs={{0,8},{8,0},{1,9},{9,1},{2,10},{10,2},{3,11},{11,3},{4,12},{12,4},... | collective-permute-start | bytes 1228808 | tf_op jit(solution)/shard_map/ppermute | solution.py:30
  38.9 0.4 fusion.7
  39.3 1.3 subtract_convert_fusion
  40.6 0.2 fusion.19
  40.8 0.1 fusion.12
  41.0 0.4 fusion.3
  41.4 7.9 %collective-permute-start.7 = (bf16[160,1024]{1,0:T(8,128)(2,1)S(1)}, bf16[160,1024]{1,0:T(8,128)(2,1)S(1)}, u32[]{:S(2)}, u32[]{:S(2)}) collective-permute-start(bf16[160,1024]{1,0:T(8,128)(2,1)S(1)} %fusion.19), channel_id=1, source_target_pairs={{0,4},{4,0},{1,5},{5,1},{2,6},{6,2},{3,7},{7,3},{8,12},{12,8},{9,1... | collective-permute-start | bytes 983048 | tf_op jit(solution)/shard_map/ppermute | solution.py:30
  49.3 1.9 %collective-permute-start.8 = (bf16[128,2560]{1,0:T(8,128)(2,1)}, bf16[128,2560]{1,0:T(8,128)(2,1)S(1)}, u32[]{:S(2)}, u32[]{:S(2)}) collective-permute-start(bf16[128,2560]{1,0:T(8,128)(2,1)} %collective-permute-done), channel_id=1, source_target_pairs={{0,1},{1,2},{2,3},{3,0},{4,5},{5,6},{6,7},{7,4},{8,9},{9,10},{10,1... | collective-permute-start | bytes 1966088 | tf_op jit(solution)/shard_map/ppermute | solution.py:30
  51.3 4.6 %collective-permute-start.9 = (bf16[128,2560]{1,0:T(8,128)(2,1)}, bf16[128,2560]{1,0:T(8,128)(2,1)S(1)}, u32[]{:S(2)}, u32[]{:S(2)}) collective-permute-start(bf16[128,2560]{1,0:T(8,128)(2,1)} %collective-permute-done.3), channel_id=1, source_target_pairs={{0,3},{1,0},{2,1},{3,2},{4,7},{5,4},{6,5},{7,6},{8,11},{9,8},{10,9... | collective-permute-start | bytes 1966088 | tf_op jit(solution)/shard_map/ppermute | solution.py:30
  55.9 1.1 constant_dynamic-update-slice_fusion.4
  57.0 1.1 constant_dynamic-update-slice_fusion.3
  58.1 0.1 constant_dynamic-update-slice_fusion.2
  58.2 1.2 constant_dynamic-update-slice_fusion.1
  59.4 1.1 constant_dynamic-update-slice_fusion
  60.6 1.5 fusion.9
  62.1 0.3 fusion.15
  62.4 1.1 broadcast_select_fusion.1
  63.4 1.5 fusion.11
  64.9 0.8 fusion.24.refs_0_
  65.7 0.2 fusion.17
  66.0 1.0 fusion.20.refs_3_
  67.0 0.8 fusion.26
  67.8 1.0 fusion.22
  68.7 0.9 collective-permute-done.9
  69.7 0.6 fusion.10
  70.4 0.6 fusion.8
  71.0 0.1 fusion.37
  71.1 0.4 fusion.38
  71.5 0.2 add.97
  71.7 3.3 %collective-permute-start.11 = (f32[160,2560]{1,0:T(8,128)S(1)}, f32[160,2560]{1,0:T(8,128)S(1)}, u32[]{:S(2)}, u32[]{:S(2)}) collective-permute-start(f32[160,2560]{1,0:T(8,128)S(1)} %add.97), channel_id=1, source_target_pairs={{0,8},{8,0},{1,9},{9,1},{2,10},{10,2},{3,11},{11,3},{4,12},{12,4},... | collective-permute-start | bytes 4915208 | tf_op jit(solution)/shard_map/ppermute | solution.py:30
  75.0 0.1 fusion.34
  75.2 0.4 fusion.42
  75.5 0.2 add.94
  75.7 1.9 %collective-permute-start.10 = (f32[160,2560]{1,0:T(8,128)S(1)}, f32[160,2560]{1,0:T(8,128)S(1)}, u32[]{:S(2)}, u32[]{:S(2)}) collective-permute-start(f32[160,2560]{1,0:T(8,128)S(1)} %add.94), channel_id=1, source_target_pairs={{0,8},{8,0},{1,9},{9,1},{2,10},{10,2},{3,11},{11,3},{4,12},{12,4},... | collective-permute-start | bytes 4915208 | tf_op jit(solution)/shard_map/ppermute | solution.py:30
  77.6 0.4 fusion.44.refs_1_
  78.0 0.4 fusion.40.refs_4_
  78.5 2.6 %collective-permute-done.10.refs_2_ = f32[160,2560]{1,0:T(8,128)S(1)} collective-permute-done((f32[160,2560]{1,0:T(8,128)S(1)}, f32[160,2560]{1,0:T(8,128)S(1)}, u32[]{:S(2)}, u32[]{:S(2)}) %collective-permute-start.10) | collective-permute-done | bytes 1638432 | tf_op jit(solution)/shard_map/ppermute | solution.py:30
  81.1 1.9 %cut.1 = bf16[64,100,128]{2,1,0:T(8,128)(2,1)} custom-call(s32[1]{0:T(128)} %bitcast.half_ref, f32[160,2560]{1,0:T(8,128)S(1)} %fusion.24.refs_0_, f32[160,2560]{1,0:T(8,128)S(1)} %fusion.44.refs_1_, f32[160,2560]{1,0:T(8,128)S(1)} %collective-permute-done.10.refs_2_, f32[160,2560]{1,0:T(8,128)S(1)} %fusion.20.refs_3_, f32[160,2560]{1,0:T(8,128)S(1)} %fusion.40.refs_4_, ...), custom_call_target="tpu_custom_call" | custom-call | flops 1638400 | bytes 11468800 | tf_op jit(solution)/shard_map/cut/pallas_call | solution.py:70
  83.0 13.2 %all-to-all-start = ((bf16[64,100,128]{2,1,0:T(8,128)(2,1)}), bf16[64,100,128]{2,1,0:T(8,128)(2,1)S(1)}, u32[]{:S(2)}, u32[]{:S(2)}) async-start(bf16[64,100,128]{2,1,0:T(8,128)(2,1)} %cut.1), calls=%async_computation | async-start | bytes 3407872 | tf_op jit(solution)/shard_map/all_to_all | solution.py:162
  96.2 1.9 %reshape.29 = bf16[3200,128]{1,0:T(8,128)(2,1)} reshape(bf16[160,2560]{1,0:T(8,128)(2,1)S(1)} %copy-done.1) | data formatting | bytes 1638400 | tf_op jit(solution)/shard_map/reshape | solution.py:161
  98.2 0.1 shift_right_arithmetic.73
  98.3 0.2 shift_right_arithmetic.62
  98.5 1.3 shift_right_arithmetic.71
  99.8 0.7 constant_dynamic-slice_fusion
  100.6 0.8 fusion.54
  101.4 36.0 %all-to-all-done = bf16[64,100,128]{2,1,0:T(8,128)(2,1)S(1)} async-done(((bf16[64,100,128]{2,1,0:T(8,128)(2,1)}), bf16[64,100,128]{2,1,0:T(8,128)(2,1)S(1)}, u32[]{:S(2)}, u32[]{:S(2)}) %all-to-all-start) | async-done | bytes 1638432 | tf_op jit(solution)/shard_map/all_to_all | solution.py:162
  137.4 0.3 convert_reduce_fusion
  137.7 4.7 %collective-permute-start.12 = (f32[50,128]{1,0:T(8,128)S(1)}, f32[50,128]{1,0:T(8,128)S(1)}, u32[]{:S(2)}, u32[]{:S(2)}) collective-permute-start(f32[50,128]{1,0:T(8,128)S(1)} %constant_dynamic-slice_fusion.1), channel_id=1, source_target_pairs={{0,8},{8,0},{1,9},{9,1},{2,10},{10,2},{3,11},{11,3},{4,12},{12,4},... | collective-permute-start | bytes 76808 | tf_op jit(solution)/shard_map/ppermute | solution.py:30
  142.4 0.8 collective-permute-done.12
  143.2 0.6 subtract_convert_fusion.1
  143.9 23.7 %all_to_all.10 = bf16[32,50,128]{2,1,0:T(8,128)(2,1)S(1)} all-to-all(bf16[32,50,128]{2,1,0:T(8,128)(2,1)S(1)} %broadcast_in_dim.2), channel_id=1, replica_groups=mesh['yl'=4,'z'=8,'c'=2,'yh'=2,'x'=4] {'yl','z'}, dimensions={0} | all-to-all | bytes 819200 | tf_op jit(solution)/shard_map/all_to_all | solution.py:183
  167.6 4.3 %collective-permute-start.13 = (bf16[32,50,128]{2,1,0:T(8,128)(2,1)S(1)}, bf16[32,50,128]{2,1,0:T(8,128)(2,1)S(1)}, u32[]{:S(2)}, u32[]{:S(2)}) collective-permute-start(bf16[32,50,128]{2,1,0:T(8,128)(2,1)S(1)} %all_to_all.10), channel_id=1, source_target_pairs={{0,8},{8,0},{1,9},{9,1},{2,10},{10,2},{3,11},{11,3},{4,12},{12,4},... | collective-permute-start | bytes 1228808 | tf_op jit(solution)/shard_map/ppermute | solution.py:30
  171.9 1.4 collective-permute-done.13
  173.4 0.1 pad_maximum_fusion.4
  173.5 1.8 %reshape.30 = bf16[160,2560]{1,0:T(8,128)(2,1)} reshape(bf16[32,2,50,128]{3,2,1,0:T(8,128)(2,1)S(1)} %pad_maximum_fusion.4) | data formatting | bytes 1638400 | tf_op jit(solution)/shard_map/reshape | solution.py:186
  (30 shorter events, 0.5 us)
Async XLA Ops:
  0.6 38.3 %copy-start.3 = (s32[5,2560]{1,0:T(8,128)S(1)}, s32[5,2560]{1,0:T(8,128)}, u32[]{:S(2)}) copy-start(s32[5,2560]{1,0:T(8,128)} %param.11) | copy-start | bytes 153604
  1.7 37.6 %copy-start.2 = (bf16[160,2048]{1,0:T(8,128)(2,1)S(1)}, bf16[160,2048]{1,0:T(8,128)(2,1)}, u32[]{:S(2)}) copy-start(bf16[160,2048]{1,0:T(8,128)(2,1)} %param.9) | copy-start | bytes 1966084
  1.7 27.2 %collective-permute-start.4 = (bf16[80,2560]{1,0:T(8,128)(2,1)S(1)}, bf16[80,2560]{1,0:T(8,128)(2,1)S(1)}, u32[]{:S(2)}, u32[]{:S(2)}) collective-permute-start(bf16[80,2560]{1,0:T(8,128)(2,1)S(1)} %constant_dynamic-slice_fusion.2), channel_id=1, source_target_pairs={{0,4},{4,0},{1,5},{5,1},{2,6},{6,2},{3,7},{7,3},{8,12},{12,8},{9,1... | collective-permute-start | bytes 1228808 | tf_op jit(solution)/shard_map/ppermute | solution.py:30
  10.1 13.8 %collective-permute-start.6 = (s32[5,2560]{1,0:T(8,128)}, s32[5,2560]{1,0:T(8,128)S(1)}, u32[]{:S(2)}, u32[]{:S(2)}) collective-permute-start(s32[5,2560]{1,0:T(8,128)} %param.11), channel_id=1, source_target_pairs={{0,4},{4,0},{1,5},{5,1},{2,6},{6,2},{3,7},{7,3},{8,12},{12,8},{9,1... | collective-permute-start | bytes 153608 | tf_op jit(solution)/shard_map/ppermute | solution.py:30
  13.4 27.9 %collective-permute-start = (bf16[128,2560]{1,0:T(8,128)(2,1)S(1)}, bf16[128,2560]{1,0:T(8,128)(2,1)}, u32[]{:S(2)}, u32[]{:S(2)}) collective-permute-start(bf16[128,2560]{1,0:T(8,128)(2,1)S(1)} %get-tuple-element.41), channel_id=1, source_target_pairs={{0,1},{1,2},{2,3},{3,0},{4,5},{5,6},{6,7},{7,4},{8,9},{9,10},{10,1... | collective-permute-start | bytes 1966088 | tf_op jit(solution)/shard_map/ppermute | solution.py:30
  16.6 32.7 %collective-permute-start.3 = (bf16[128,2560]{1,0:T(8,128)(2,1)S(1)}, bf16[128,2560]{1,0:T(8,128)(2,1)}, u32[]{:S(2)}, u32[]{:S(2)}) collective-permute-start(bf16[128,2560]{1,0:T(8,128)(2,1)S(1)} %get-tuple-element.40), channel_id=1, source_target_pairs={{0,3},{1,0},{2,1},{3,2},{4,7},{5,4},{6,5},{7,6},{8,11},{9,8},{10,9... | collective-permute-start | bytes 1966088 | tf_op jit(solution)/shard_map/ppermute | solution.py:30
  20.0 31.3 %collective-permute-start.1 = (bf16[128,2560]{1,0:T(8,128)(2,1)S(1)}, bf16[128,2560]{1,0:T(8,128)(2,1)}, u32[]{:S(2)}, u32[]{:S(2)}) collective-permute-start(bf16[128,2560]{1,0:T(8,128)(2,1)S(1)} %get-tuple-element.40), channel_id=1, source_target_pairs={{0,1},{1,2},{2,3},{3,0},{4,5},{5,6},{6,7},{7,4},{8,9},{9,10},{10,1... | collective-permute-start | bytes 1966088 | tf_op jit(solution)/shard_map/ppermute | solution.py:30
  24.0 31.9 %collective-permute-start.2 = (bf16[128,2560]{1,0:T(8,128)(2,1)S(1)}, bf16[128,2560]{1,0:T(8,128)(2,1)}, u32[]{:S(2)}, u32[]{:S(2)}) collective-permute-start(bf16[128,2560]{1,0:T(8,128)(2,1)S(1)} %get-tuple-element.41), channel_id=1, source_target_pairs={{0,3},{1,0},{2,1},{3,2},{4,7},{5,4},{6,5},{7,6},{8,11},{9,8},{10,9... | collective-permute-start | bytes 1966088 | tf_op jit(solution)/shard_map/ppermute | solution.py:30
  28.9 27.0 %collective-permute-start.5 = (bf16[80,2560]{1,0:T(8,128)(2,1)S(1)}, bf16[80,2560]{1,0:T(8,128)(2,1)}, u32[]{:S(2)}, u32[]{:S(2)}) collective-permute-start(bf16[80,2560]{1,0:T(8,128)(2,1)S(1)} %collective-permute-done.4), channel_id=1, source_target_pairs={{0,8},{8,0},{1,9},{9,1},{2,10},{10,2},{3,11},{11,3},{4,12},{12,4},... | collective-permute-start | bytes 1228808 | tf_op jit(solution)/shard_map/ppermute | solution.py:30
  41.0 17.2 %copy-start = (bf16[256,2560]{1,0:T(8,128)(2,1)S(1)}, bf16[256,2560]{1,0:T(8,128)(2,1)}, u32[]{:S(2)}) copy-start(bf16[256,2560]{1,0:T(8,128)(2,1)} %param.7) | copy-start | bytes 3932164
  41.4 24.4 %collective-permute-start.7 = (bf16[160,1024]{1,0:T(8,128)(2,1)S(1)}, bf16[160,1024]{1,0:T(8,128)(2,1)S(1)}, u32[]{:S(2)}, u32[]{:S(2)}) collective-permute-start(bf16[160,1024]{1,0:T(8,128)(2,1)S(1)} %fusion.19), channel_id=1, source_target_pairs={{0,4},{4,0},{1,5},{5,1},{2,6},{6,2},{3,7},{7,3},{8,12},{12,8},{9,1... | collective-permute-start | bytes 983048 | tf_op jit(solution)/shard_map/ppermute | solution.py:30
  49.3 19.4 %collective-permute-start.8 = (bf16[128,2560]{1,0:T(8,128)(2,1)}, bf16[128,2560]{1,0:T(8,128)(2,1)S(1)}, u32[]{:S(2)}, u32[]{:S(2)}) collective-permute-start(bf16[128,2560]{1,0:T(8,128)(2,1)} %collective-permute-done), channel_id=1, source_target_pairs={{0,1},{1,2},{2,3},{3,0},{4,5},{5,6},{6,7},{7,4},{8,9},{9,10},{10,1... | collective-permute-start | bytes 1966088 | tf_op jit(solution)/shard_map/ppermute | solution.py:30
  51.3 18.4 %collective-permute-start.9 = (bf16[128,2560]{1,0:T(8,128)(2,1)}, bf16[128,2560]{1,0:T(8,128)(2,1)S(1)}, u32[]{:S(2)}, u32[]{:S(2)}) collective-permute-start(bf16[128,2560]{1,0:T(8,128)(2,1)} %collective-permute-done.3), channel_id=1, source_target_pairs={{0,3},{1,0},{2,1},{3,2},{4,7},{5,4},{6,5},{7,6},{8,11},{9,8},{10,9... | collective-permute-start | bytes 1966088 | tf_op jit(solution)/shard_map/ppermute | solution.py:30
  58.2 2.4 %copy-start.1 = (bf16[160,2560]{1,0:T(8,128)(2,1)S(1)}, bf16[160,2560]{1,0:T(8,128)(2,1)}, u32[]{:S(2)}) copy-start(bf16[160,2560]{1,0:T(8,128)(2,1)} %param.10) | copy-start | bytes 2457604
  71.7 6.8 %collective-permute-start.11 = (f32[160,2560]{1,0:T(8,128)S(1)}, f32[160,2560]{1,0:T(8,128)S(1)}, u32[]{:S(2)}, u32[]{:S(2)}) collective-permute-start(f32[160,2560]{1,0:T(8,128)S(1)} %add.97), channel_id=1, source_target_pairs={{0,8},{8,0},{1,9},{9,1},{2,10},{10,2},{3,11},{11,3},{4,12},{12,4},... | collective-permute-start | bytes 4915208 | tf_op jit(solution)/shard_map/ppermute | solution.py:30
  75.7 5.4 %collective-permute-start.10 = (f32[160,2560]{1,0:T(8,128)S(1)}, f32[160,2560]{1,0:T(8,128)S(1)}, u32[]{:S(2)}, u32[]{:S(2)}) collective-permute-start(f32[160,2560]{1,0:T(8,128)S(1)} %add.94), channel_id=1, source_target_pairs={{0,8},{8,0},{1,9},{9,1},{2,10},{10,2},{3,11},{11,3},{4,12},{12,4},... | collective-permute-start | bytes 4915208 | tf_op jit(solution)/shard_map/ppermute | solution.py:30
  83.0 54.3 %all-to-all-start = ((bf16[64,100,128]{2,1,0:T(8,128)(2,1)}), bf16[64,100,128]{2,1,0:T(8,128)(2,1)S(1)}, u32[]{:S(2)}, u32[]{:S(2)}) async-start(bf16[64,100,128]{2,1,0:T(8,128)(2,1)} %cut.1), calls=%async_computation | async-start | bytes 3407872 | tf_op jit(solution)/shard_map/all_to_all | solution.py:162
  99.8 43.5 %copy-start.4 = (f32[50,128]{1,0:T(8,128)S(1)}, f32[50,128]{1,0:T(8,128)}, u32[]{:S(2)}) copy-start(f32[50,128]{1,0:T(8,128)} %param.12) | copy-start | bytes 76804
  99.8 43.5 %copy-start.5 = (f32[50,128]{1,0:T(8,128)S(1)}, f32[50,128]{1,0:T(8,128)}, u32[]{:S(2)}) copy-start(f32[50,128]{1,0:T(8,128)} %param.13) | copy-start | bytes 76804
  137.7 5.5 %collective-permute-start.12 = (f32[50,128]{1,0:T(8,128)S(1)}, f32[50,128]{1,0:T(8,128)S(1)}, u32[]{:S(2)}, u32[]{:S(2)}) collective-permute-start(f32[50,128]{1,0:T(8,128)S(1)} %constant_dynamic-slice_fusion.1), channel_id=1, source_target_pairs={{0,8},{8,0},{1,9},{9,1},{2,10},{10,2},{3,11},{11,3},{4,12},{12,4},... | collective-permute-start | bytes 76808 | tf_op jit(solution)/shard_map/ppermute | solution.py:30
  167.6 5.7 %collective-permute-start.13 = (bf16[32,50,128]{2,1,0:T(8,128)(2,1)S(1)}, bf16[32,50,128]{2,1,0:T(8,128)(2,1)S(1)}, u32[]{:S(2)}, u32[]{:S(2)}) collective-permute-start(bf16[32,50,128]{2,1,0:T(8,128)(2,1)S(1)} %all_to_all.10), channel_id=1, source_target_pairs={{0,8},{8,0},{1,9},{9,1},{2,10},{10,2},{3,11},{11,3},{4,12},{12,4},... | collective-permute-start | bytes 1228808 | tf_op jit(solution)/shard_map/ppermute | solution.py:30

commit v6 on v5

--- a/solution.py
+++ b/solution.py
@@ -79,8 +79,39 @@
     )(half.reshape(1).astype(jnp.int32), *terms)
 
 
+def join_kernel(*refs):
+    count = len(refs) - 2
+    blocks, out_ref, arrived = refs[:count], refs[count], refs[count + 1]
+    copies, at = [], 0
+    for i, block in enumerate(blocks):
+        size_here = block.shape[0]
+        copies.append(
+            pltpu.make_async_copy(block, out_ref.at[pl.ds(at, size_here), :], arrived.at[i])
+        )
+        copies[-1].start()
+        at += size_here
+    for copy in copies:
+        copy.wait()
+
+
+def join(blocks):
+    rows, width = sum(b.shape[0] for b in blocks), blocks[0].shape[1]
+    return pl.pallas_call(
+        join_kernel,
+        out_shape=jax.ShapeDtypeStruct((rows, width), blocks[0].dtype),
+        in_specs=[pl.BlockSpec(memory_space=pl.ANY)] * len(blocks),
+        out_specs=pl.BlockSpec(memory_space=pltpu.VMEM),
+        scratch_shapes=[pltpu.SemaphoreType.DMA((len(blocks),))],
+        compiler_params=pltpu.CompilerParams(vmem_limit_bytes=8 << 20),
+        cost_estimate=pl.CostEstimate(
+            flops=rows * width, bytes_accessed=4 * rows * width, transcendentals=0
+        ),
+        name="join",
+    )(*blocks)
+
+
 def step(hidden, resid, target, w_out, signs, m_old, v_old):
-    features, _ = w_out.shape
+    features, width = w_out.shape
     tokens = hidden.shape[0]
     group = tokens * lax.axis_size("x")
     half = lax.axis_index("yh")
@@ -97,8 +128,15 @@
     far_low = shift(right_low, "x", -1)
 
     rows = features // 2
-    part = shift(lax.dynamic_slice_in_dim(w_out, core * rows, rows, 0), "yh", 1)
-    other_signs = shift(signs, "yh", 1)
+    octets = jnp.stack([(signs >> (16 * core + 8 * p)) & 255 for p in range(2)])
+    part = jnp.concatenate(
+        [
+            lax.dynamic_slice_in_dim(w_out, core * rows, rows, 0),
+            octets.reshape(-1, width).astype(jnp.bfloat16),
+        ],
+        axis=0,
+    )
+    part = shift(part, "yh", 1)
 
     def gap(at, kind):
         def part(whole):
@@ -113,17 +151,13 @@
     probes = unpack_signs(signs)
     own_stack = jnp.concatenate([w_out, probes], axis=0)
     own_gaps = gap(half, jnp.float32)
-    left_top, left_low, right_top, right_low, twin = lax.optimization_barrier(
-        (left_top, left_low, right_top, right_low, twin)
-    )
-    other_signs, _ = lax.optimization_barrier((other_signs, probes))
+    first = jnp.where(core == 0, part, twin)
+    second = jnp.where(core == 0, twin, part)
+    octets = jnp.stack([first[rows:], second[rows:]]).astype(jnp.int32)
+    octets = octets.reshape(4, -1, 1, width).transpose(1, 0, 2, 3)
+    bits = (octets >> jnp.arange(8, dtype=jnp.int32)[None, None, :, None]) & 1
     other_stack = jnp.concatenate(
-        [
-            jnp.where(core == 0, part, twin),
-            jnp.where(core == 0, twin, part),
-            unpack_signs(other_signs),
-        ],
-        axis=0,
+        [first[:rows], second[:rows], (1 - 2 * bits).reshape(-1, width).astype(jnp.bfloat16)], axis=0
     )
 
     def run(stacked, gaps, block):
@@ -140,13 +174,13 @@
         kept = jnp.where(core == 0, slopes, bends)
         return [jnp.dot(terms, block, preferred_element_type=jnp.float32) for terms in (away, kept)]
 
-    near = jnp.concatenate([left_top, left_low, hidden, right_top, right_low], axis=0)
+    near = join((left_top, left_low, hidden, right_top, right_low))
     own_away, own_kept = run(own_stack, own_gaps, near)
     other_away, other_kept = run(other_stack, other_gaps, near)
     own_away, own_kept, other_away, other_kept, far_top, far_low = lax.optimization_barrier(
         (own_away, own_kept, other_away, other_kept, far_top, far_low)
     )
-    far = jnp.concatenate([far_top, far_low], axis=0)
+    far = join((far_top, far_low))
     own_far = run(own_stack, own_gaps, far)
     own_got = shift(own_away + own_far[0], "c", 1)
     other_far = run(other_stack, other_gaps, far)

time: 176 us -> 194 us (1.10)
  matrix products: 9.3 us -> 16.7 us
  waiting for transfers between devices: 43.9 us -> 49.8 us
  other arithmetic: 6.45 us -> 11.4 us
  starting transfers between devices: 75.4 us -> 71.4 us
  Pallas kernels: 1.91 us -> 4.02 us
    ppermute x14 -> x13, waiting for transfers between devices: 7.92 us -> 13.6 us  [shift(): return lax.ppermute(value, axis, hops)]
    dot_general x8, matrix products: 5.14 us -> 10 us  [run(): jnp.dot(terms, block, preferred_element_type=jnp.float32)]
    convert_element_type x3, other arithmetic: 0.45 us -> 3.19 us  [run(): bends = (forward[features:] / (spread * rooted)).astype(jnp.bfloat16)]
    dot_general x4, matrix products: 4.16 us -> 6.66 us  [run(): lax.dot_general(stacked, block, (((1,), (1,)), ((), ())), preferred_eleme...]
    pallas_call x0 -> x2, Pallas kernels: none -> 2.11 us  [join(): pl.pallas_call(join_kernel, out_shape=jax.ShapeDtypeStruct((rows, width),...]
    all_to_all x1, starting transfers between devices: 13.2 us -> 11.1 us  [step(): terms = lax.all_to_all(pieces, ('yh', 'yl', 'z'), 0, 0, tiled=True)]
    shift_right_arithmetic x0 -> x4, local copies, waits for them, and re-layouts: none -> 1.96 us  [step(): bits = octets >> jnp.arange(8, dtype=jnp.int32)[None, None, :, None] & 1]
    ppermute x14 -> x13, starting transfers between devices: 62.2 us -> 60.3 us  [shift(): return lax.ppermute(value, axis, hops)]
  transfers between devices with their start and end apart: 15 -> 14, of which waited for: 6 -> 5; matrix products, arithmetic and copies ran while one was open for 13% -> 16% of each run, Pallas kernels for 0% -> 1%
where the time goes in v6:
time: 194 us; the launch traced here: 193 us
  starting transfers between devices  71.4 us (37%)
  waiting for transfers between devices  49.8 us (26%)
  blocking collectives  23.7 us (12%)
  matrix products  16.7 us (9%)
  local copies, waits for them, and re-layouts  15 us (8%)
  other arithmetic  11.4 us (6%)
  Pallas kernels  4.02 us (2%)
    ppermute x13, starting transfers between devices, shift(): return lax.ppermute(value, axis, hops)  60.3 us
    all_to_all x1, waiting for transfers between devices, step(): terms = lax.all_to_all(pieces, ('yh', 'yl', 'z'), 0, 0, tiled=True)  36.2 us
    all_to_all x1, blocking collectives, step(): mine_rows = lax.all_to_all(spread_rows, ('yl', 'z'), 0, 0, tiled=True)  23.7 us
    ppermute x13, waiting for transfers between devices, shift(): return lax.ppermute(value, axis, hops)  13.6 us
    all_to_all x1, starting transfers between devices, step(): terms = lax.all_to_all(pieces, ('yh', 'yl', 'z'), 0, 0, tiled=True)  11.1 us
    dot_general x8, matrix products, run(): jnp.dot(terms, block, preferred_element_type=jnp.float32)  10 us
    dot_general x4, matrix products, run(): lax.dot_general(stacked, block, (((1,), (1,)), ((), ())), preferred_eleme...  6.66 us
  transfers between devices with their start and end apart: 14, of which 5 were waited for; matrix products, arithmetic and copies ran while one was open for 16% of the time, Pallas kernels for 1%

profile of v6, /device:TPU:1, one launch (start us, length us, event | category | flops | bytes accessed | tf_op | source)
XLA Modules:
  0.0 193.2 jit_solution(351416842620362838)
XLA Ops:
  0.7 2.5 %fusion.66 = (bf16[128,2560]{1,0:T(8,128)(2,1)}, bf16[128,2560]{1,0:T(8,128)(2,1)}) fusion(bf16[256,2560]{1,0:T(8,128)(2,1)} %refs_2_.1), kind=kLoop, calls=%fused_computation.107 | loop fusion | bytes 2621440 | tf_op jit(solution)/shard_map/slice | solution.py:122
  3.2 5.2 %collective-permute-start.3 = (bf16[128,2560]{1,0:T(8,128)(2,1)}, bf16[128,2560]{1,0:T(8,128)(2,1)}, u32[]{:S(2)}, u32[]{:S(2)}) collective-permute-start(bf16[128,2560]{1,0:T(8,128)(2,1)} %get-tuple-element.28), channel_id=1, source_target_pairs={{0,3},{1,0},{2,1},{3,2},{4,7},{5,4},{6,5},{7,6},{8,11},{9,8},{10,9... | collective-permute-start | bytes 1966088 | tf_op jit(solution)/shard_map/ppermute | solution.py:30
  8.4 1.9 collective-permute-start.1
  10.3 2.1 %collective-permute-start = (bf16[128,2560]{1,0:T(8,128)(2,1)}, bf16[128,2560]{1,0:T(8,128)(2,1)}, u32[]{:S(2)}, u32[]{:S(2)}) collective-permute-start(bf16[128,2560]{1,0:T(8,128)(2,1)} %get-tuple-element.29), channel_id=1, source_target_pairs={{0,1},{1,2},{2,3},{3,0},{4,5},{5,6},{6,7},{7,4},{8,9},{9,10},{10,1... | collective-permute-start | bytes 1966088 | tf_op jit(solution)/shard_map/ppermute | solution.py:30
  12.4 4.4 %collective-permute-start.2 = (bf16[128,2560]{1,0:T(8,128)(2,1)}, bf16[128,2560]{1,0:T(8,128)(2,1)S(1)}, u32[]{:S(2)}, u32[]{:S(2)}) collective-permute-start(bf16[128,2560]{1,0:T(8,128)(2,1)} %get-tuple-element.29), channel_id=1, source_target_pairs={{0,3},{1,0},{2,1},{3,2},{4,7},{5,4},{6,5},{7,6},{8,11},{9,8},{10,9... | collective-permute-start | bytes 1966088 | tf_op jit(solution)/shard_map/ppermute | solution.py:30
  17.0 0.8 pad_maximum_fusion.7
  17.8 7.4 %collective-permute-start.4 = (bf16[90,2560]{1,0:T(8,128)(2,1)}, bf16[90,2560]{1,0:T(8,128)(2,1)}, u32[]{:S(2)}, u32[]{:S(2)}) collective-permute-start(bf16[90,2560]{1,0:T(8,128)(2,1)} %pad_maximum_fusion.7), channel_id=1, source_target_pairs={{0,4},{4,0},{1,5},{5,1},{2,6},{6,2},{3,7},{7,3},{8,12},{12,8},{9,1... | collective-permute-start | bytes 1382408 | tf_op jit(solution)/shard_map/ppermute | solution.py:30
  25.5 0.4 fusion.7
  25.9 1.8 subtract_convert_fusion
  27.7 0.9 fusion.19
  28.8 9.6 %collective-permute-done.4 = bf16[90,2560]{1,0:T(8,128)(2,1)} collective-permute-done((bf16[90,2560]{1,0:T(8,128)(2,1)}, bf16[90,2560]{1,0:T(8,128)(2,1)}, u32[]{:S(2)}, u32[]{:S(2)}) %collective-permute-start.4) | collective-permute-done | bytes 460832 | tf_op jit(solution)/shard_map/ppermute | solution.py:30
  38.3 8.0 %collective-permute-start.6 = (bf16[160,1024]{1,0:T(8,128)(2,1)}, bf16[160,1024]{1,0:T(8,128)(2,1)}, u32[]{:S(2)}, u32[]{:S(2)}) collective-permute-start(bf16[160,1024]{1,0:T(8,128)(2,1)} %fusion.19), channel_id=1, source_target_pairs={{0,4},{4,0},{1,5},{5,1},{2,6},{6,2},{3,7},{7,3},{8,12},{12,8},{9,1... | collective-permute-start | bytes 983048 | tf_op jit(solution)/shard_map/ppermute | solution.py:30
  46.4 11.5 %collective-permute-start.5 = (bf16[90,2560]{1,0:T(8,128)(2,1)}, bf16[90,2560]{1,0:T(8,128)(2,1)S(1)}, u32[]{:S(2)}, u32[]{:S(2)}) collective-permute-start(bf16[90,2560]{1,0:T(8,128)(2,1)} %collective-permute-done.4), channel_id=1, source_target_pairs={{0,8},{8,0},{1,9},{9,1},{2,10},{10,2},{3,11},{11,3},{4,12},{12,4},... | collective-permute-start | bytes 1382408 | tf_op jit(solution)/shard_map/ppermute | solution.py:30
  57.9 1.7 join.2
  59.6 1.4 fusion.9
  61.0 0.3 fusion.15
  61.4 0.8 fusion.24.refs_0_
  62.2 1.9 collective-permute-start.7
  64.1 4.6 %collective-permute-start.8 = (bf16[128,2560]{1,0:T(8,128)(2,1)}, bf16[128,2560]{1,0:T(8,128)(2,1)S(1)}, u32[]{:S(2)}, u32[]{:S(2)}) collective-permute-start(bf16[128,2560]{1,0:T(8,128)(2,1)} %collective-permute-done.3.refs_4_), channel_id=1, source_target_pairs={{0,3},{1,0},{2,1},{3,2},{4,7},{5,4},{6,5},{7,6},{8,11},{9,8},{10,9... | collective-permute-start | bytes 1966088 | tf_op jit(solution)/shard_map/ppermute | solution.py:30
  68.7 2.0 %fusion.26 = f32[160,2560]{1,0:T(8,128)} fusion(bf16[768,2560]{1,0:T(8,128)(2,1)S(1)} %join.2, bf16[160,768]{1,0:T(8,128)(2,1)S(1)} %get-tuple-element.25, bf16[160,768]{1,0:T(8,128)(2,1)S(1)} %get-tuple-element.24, pred[]{:T(512)S(6)} %eq.5), kind=kOutput, calls=%fused_computation.51 | convolution fusion | flops 629268480 | bytes 6062081 | tf_op jit(solution)/shard_map/dot_general | solution.py:175
  70.7 1.1 broadcast_select_fusion.1
  71.8 0.8 slice.75
  72.7 0.8 slice.76
  73.6 0.8 reshape.46
  74.3 1.1 copy.12
  75.4 0.4 fusion.3
  75.8 4.0 %fusion.11 = f32[320,768]{1,0:T(8,128)S(1)} fusion(bf16[768,2560]{1,0:T(8,128)(2,1)} %copy-done, bf16[160,2560]{1,0:T(8,128)(2,1)S(1)} %fusion.3, bf16[80,2560]{1,0:T(8,128)(2,1)} %slice.76, bf16[80,2560]{1,0:T(8,128)(2,1)} %slice.75), kind=kOutput, calls=%fused_computation.23 | convolution fusion | flops 1263206400 | bytes 6553600 | tf_op jit(solution)/shard_map/dot_general | solution.py:165
  79.8 1.2 fusion.17
  81.0 1.9 fusion.20.refs_3_
  82.9 1.9 fusion.22
  84.8 0.4 join.3
  85.3 0.5 copy-done.10
  85.9 0.6 fusion.10
  86.5 0.5 copy-done.6
  87.0 0.2 copy-done.8
  87.3 0.6 fusion.8
  87.9 1.0 fusion.37
  88.9 1.3 fusion.38
  90.2 0.2 add.101
  90.4 2.5 %collective-permute-start.10 = (f32[160,2560]{1,0:T(8,128)S(1)}, f32[160,2560]{1,0:T(8,128)S(1)}, u32[]{:S(2)}, u32[]{:S(2)}) collective-permute-start(f32[160,2560]{1,0:T(8,128)S(1)} %add.101), channel_id=1, source_target_pairs={{0,8},{8,0},{1,9},{9,1},{2,10},{10,2},{3,11},{11,3},{4,12},{12,4},... | collective-permute-start | bytes 4915208 | tf_op jit(solution)/shard_map/ppermute | solution.py:30
  92.9 1.0 fusion.34
  93.9 0.4 fusion.42
  94.3 1.0 copy-done.3
  95.4 0.2 add.98
  95.5 1.9 collective-permute-start.9
  97.5 0.4 fusion.44.refs_1_
  97.8 1.3 fusion.40.refs_4_
  99.2 1.8 collective-permute-done.9.refs_2_
  100.9 1.9 cut.1
  102.8 11.1 %all-to-all-start = ((bf16[64,100,128]{2,1,0:T(8,128)(2,1)}), bf16[64,100,128]{2,1,0:T(8,128)(2,1)S(1)}, u32[]{:S(2)}, u32[]{:S(2)}) async-start(bf16[64,100,128]{2,1,0:T(8,128)(2,1)} %cut.1), calls=%async_computation | async-start | bytes 3407872 | tf_op jit(solution)/shard_map/all_to_all | solution.py:196
  113.9 1.9 reshape.43
  116.0 0.2 shift_right_arithmetic.79
  116.2 1.3 shift_right_arithmetic.97
  117.5 0.7 constant_dynamic-slice_fusion
  118.3 0.8 fusion.56
  119.1 36.2 %all-to-all-done = bf16[64,100,128]{2,1,0:T(8,128)(2,1)S(1)} async-done(((bf16[64,100,128]{2,1,0:T(8,128)(2,1)}), bf16[64,100,128]{2,1,0:T(8,128)(2,1)S(1)}, u32[]{:S(2)}, u32[]{:S(2)}) %all-to-all-start) | async-done | bytes 1638432 | tf_op jit(solution)/shard_map/all_to_all | solution.py:196
  155.3 0.3 convert_reduce_fusion
  155.6 4.6 %collective-permute-start.11 = (f32[50,128]{1,0:T(8,128)S(1)}, f32[50,128]{1,0:T(8,128)S(1)}, u32[]{:S(2)}, u32[]{:S(2)}) collective-permute-start(f32[50,128]{1,0:T(8,128)S(1)} %constant_dynamic-slice_fusion.1), channel_id=1, source_target_pairs={{0,8},{8,0},{1,9},{9,1},{2,10},{10,2},{3,11},{11,3},{4,12},{12,4},... | collective-permute-start | bytes 76808 | tf_op jit(solution)/shard_map/ppermute | solution.py:30
  160.3 0.8 collective-permute-done.11
  161.1 0.6 subtract_convert_fusion.1
  161.8 23.7 %all_to_all.10 = bf16[32,50,128]{2,1,0:T(8,128)(2,1)S(1)} all-to-all(bf16[32,50,128]{2,1,0:T(8,128)(2,1)S(1)} %broadcast_in_dim.2), channel_id=1, replica_groups=mesh['yl'=4,'z'=8,'c'=2,'yh'=2,'x'=4] {'yl','z'}, dimensions={0} | all-to-all | bytes 819200 | tf_op jit(solution)/shard_map/all_to_all | solution.py:217
  185.5 4.3 %collective-permute-start.12 = (bf16[32,50,128]{2,1,0:T(8,128)(2,1)S(1)}, bf16[32,50,128]{2,1,0:T(8,128)(2,1)S(1)}, u32[]{:S(2)}, u32[]{:S(2)}) collective-permute-start(bf16[32,50,128]{2,1,0:T(8,128)(2,1)S(1)} %all_to_all.10), channel_id=1, source_target_pairs={{0,8},{8,0},{1,9},{9,1},{2,10},{10,2},{3,11},{11,3},{4,12},{12,4},... | collective-permute-start | bytes 1228808 | tf_op jit(solution)/shard_map/ppermute | solution.py:30
  189.8 1.4 collective-permute-done.12
  191.4 1.8 reshape.44
  (51 shorter events, 1.2 us)
Async XLA Ops:
  0.6 16.2 %copy-start.9 = (s32[5,2560]{1,0:T(8,128)S(1)}, s32[5,2560]{1,0:T(8,128)}, u32[]{:S(2)}) copy-start(s32[5,2560]{1,0:T(8,128)} %param.11) | copy-start | bytes 153604
  0.6 16.3 %copy-start.5 = (bf16[160,2560]{1,0:T(8,128)(2,1)S(1)}, bf16[160,2560]{1,0:T(8,128)(2,1)}, u32[]{:S(2)}) copy-start(bf16[160,2560]{1,0:T(8,128)(2,1)} %param.10) | copy-start | bytes 2457604
  3.2 54.7 %collective-permute-start.3 = (bf16[128,2560]{1,0:T(8,128)(2,1)}, bf16[128,2560]{1,0:T(8,128)(2,1)}, u32[]{:S(2)}, u32[]{:S(2)}) collective-permute-start(bf16[128,2560]{1,0:T(8,128)(2,1)} %get-tuple-element.28), channel_id=1, source_target_pairs={{0,3},{1,0},{2,1},{3,2},{4,7},{5,4},{6,5},{7,6},{8,11},{9,8},{10,9... | collective-permute-start | bytes 1966088 | tf_op jit(solution)/shard_map/ppermute | solution.py:30
  8.4 49.5 %collective-permute-start.1 = (bf16[128,2560]{1,0:T(8,128)(2,1)}, bf16[128,2560]{1,0:T(8,128)(2,1)S(1)}, u32[]{:S(2)}, u32[]{:S(2)}) collective-permute-start(bf16[128,2560]{1,0:T(8,128)(2,1)} %get-tuple-element.28), channel_id=1, source_target_pairs={{0,1},{1,2},{2,3},{3,0},{4,5},{5,6},{6,7},{7,4},{8,9},{9,10},{10,1... | collective-permute-start | bytes 1966088 | tf_op jit(solution)/shard_map/ppermute | solution.py:30
  10.3 36.0 %collective-permute-start = (bf16[128,2560]{1,0:T(8,128)(2,1)}, bf16[128,2560]{1,0:T(8,128)(2,1)}, u32[]{:S(2)}, u32[]{:S(2)}) collective-permute-start(bf16[128,2560]{1,0:T(8,128)(2,1)} %get-tuple-element.29), channel_id=1, source_target_pairs={{0,1},{1,2},{2,3},{3,0},{4,5},{5,6},{6,7},{7,4},{8,9},{9,10},{10,1... | collective-permute-start | bytes 1966088 | tf_op jit(solution)/shard_map/ppermute | solution.py:30
  12.4 45.4 %collective-permute-start.2 = (bf16[128,2560]{1,0:T(8,128)(2,1)}, bf16[128,2560]{1,0:T(8,128)(2,1)S(1)}, u32[]{:S(2)}, u32[]{:S(2)}) collective-permute-start(bf16[128,2560]{1,0:T(8,128)(2,1)} %get-tuple-element.29), channel_id=1, source_target_pairs={{0,3},{1,0},{2,1},{3,2},{4,7},{5,4},{6,5},{7,6},{8,11},{9,8},{10,9... | collective-permute-start | bytes 1966088 | tf_op jit(solution)/shard_map/ppermute | solution.py:30
  17.8 20.5 %collective-permute-start.4 = (bf16[90,2560]{1,0:T(8,128)(2,1)}, bf16[90,2560]{1,0:T(8,128)(2,1)}, u32[]{:S(2)}, u32[]{:S(2)}) collective-permute-start(bf16[90,2560]{1,0:T(8,128)(2,1)} %pad_maximum_fusion.7), channel_id=1, source_target_pairs={{0,4},{4,0},{1,5},{5,1},{2,6},{6,2},{3,7},{7,3},{8,12},{12,8},{9,1... | collective-permute-start | bytes 1382408 | tf_op jit(solution)/shard_map/ppermute | solution.py:30
  25.9 33.7 %copy-start.7 = (bf16[160,2560]{1,0:T(8,128)(2,1)}, bf16[160,2560]{1,0:T(8,128)(2,1)S(1)}, u32[]{:S(2)}) copy-start(bf16[160,2560]{1,0:T(8,128)(2,1)S(1)} %fusion.7) | copy-start | bytes 2457604
  25.9 32.0 %copy-start.2 = (bf16[256,2560]{1,0:T(8,128)(2,1)S(1)}, bf16[256,2560]{1,0:T(8,128)(2,1)}, u32[]{:S(2)}) copy-start(bf16[256,2560]{1,0:T(8,128)(2,1)} %refs_2_.1) | copy-start | bytes 3932164
  28.8 32.3 %copy-start.4 = (f32[160,1024]{1,0:T(8,128)}, f32[160,1024]{1,0:T(8,128)S(1)}, u32[]{:S(2)}) copy-start(f32[160,1024]{1,0:T(8,128)S(1)} %fusion.12) | copy-start | bytes 1966084
  38.3 41.4 %collective-permute-start.6 = (bf16[160,1024]{1,0:T(8,128)(2,1)}, bf16[160,1024]{1,0:T(8,128)(2,1)}, u32[]{:S(2)}, u32[]{:S(2)}) collective-permute-start(bf16[160,1024]{1,0:T(8,128)(2,1)} %fusion.19), channel_id=1, source_target_pairs={{0,4},{4,0},{1,5},{5,1},{2,6},{6,2},{3,7},{7,3},{8,12},{12,8},{9,1... | collective-permute-start | bytes 983048 | tf_op jit(solution)/shard_map/ppermute | solution.py:30
  46.4 24.4 %collective-permute-start.5 = (bf16[90,2560]{1,0:T(8,128)(2,1)}, bf16[90,2560]{1,0:T(8,128)(2,1)S(1)}, u32[]{:S(2)}, u32[]{:S(2)}) collective-permute-start(bf16[90,2560]{1,0:T(8,128)(2,1)} %collective-permute-done.4), channel_id=1, source_target_pairs={{0,8},{8,0},{1,9},{9,1},{2,10},{10,2},{3,11},{11,3},{4,12},{12,4},... | collective-permute-start | bytes 1382408 | tf_op jit(solution)/shard_map/ppermute | solution.py:30
  59.6 9.1 %copy-start = (bf16[768,2560]{1,0:T(8,128)(2,1)}, bf16[768,2560]{1,0:T(8,128)(2,1)S(1)}, u32[]{:S(2)}) copy-start(bf16[768,2560]{1,0:T(8,128)(2,1)S(1)} %join.2) | copy-start | bytes 11796484
  62.2 22.6 %collective-permute-start.7 = (bf16[128,2560]{1,0:T(8,128)(2,1)}, bf16[128,2560]{1,0:T(8,128)(2,1)S(1)}, u32[]{:S(2)}, u32[]{:S(2)}) collective-permute-start(bf16[128,2560]{1,0:T(8,128)(2,1)} %collective-permute-done.refs_0_), channel_id=1, source_target_pairs={{0,1},{1,2},{2,3},{3,0},{4,5},{5,6},{6,7},{7,4},{8,9},{9,10},{10,1... | collective-permute-start | bytes 1966088 | tf_op jit(solution)/shard_map/ppermute | solution.py:30
  64.1 20.7 %collective-permute-start.8 = (bf16[128,2560]{1,0:T(8,128)(2,1)}, bf16[128,2560]{1,0:T(8,128)(2,1)S(1)}, u32[]{:S(2)}, u32[]{:S(2)}) collective-permute-start(bf16[128,2560]{1,0:T(8,128)(2,1)} %collective-permute-done.3.refs_4_), channel_id=1, source_target_pairs={{0,3},{1,0},{2,1},{3,2},{4,7},{5,4},{6,5},{7,6},{8,11},{9,8},{10,9... | collective-permute-start | bytes 1966088 | tf_op jit(solution)/shard_map/ppermute | solution.py:30
  75.8 5.2 %copy-start.1 = (bf16[768,2560]{1,0:T(8,128)(2,1)S(1)}, bf16[768,2560]{1,0:T(8,128)(2,1)}, u32[]{:S(2)}) copy-start(bf16[768,2560]{1,0:T(8,128)(2,1)} %copy-done) | copy-start | bytes 11796484
  84.8 1.0 copy-start.10
  84.8 1.1 copy-start.11
  85.9 1.1 copy-start.6
  85.9 1.4 copy-start.8
  90.4 8.7 %collective-permute-start.10 = (f32[160,2560]{1,0:T(8,128)S(1)}, f32[160,2560]{1,0:T(8,128)S(1)}, u32[]{:S(2)}, u32[]{:S(2)}) collective-permute-start(f32[160,2560]{1,0:T(8,128)S(1)} %add.101), channel_id=1, source_target_pairs={{0,8},{8,0},{1,9},{9,1},{2,10},{10,2},{3,11},{11,3},{4,12},{12,4},... | collective-permute-start | bytes 4915208 | tf_op jit(solution)/shard_map/ppermute | solution.py:30
  93.9 1.4 copy-start.3
  95.5 5.4 %collective-permute-start.9 = (f32[160,2560]{1,0:T(8,128)S(1)}, f32[160,2560]{1,0:T(8,128)S(1)}, u32[]{:S(2)}, u32[]{:S(2)}) collective-permute-start(f32[160,2560]{1,0:T(8,128)S(1)} %add.98), channel_id=1, source_target_pairs={{0,8},{8,0},{1,9},{9,1},{2,10},{10,2},{3,11},{11,3},{4,12},{12,4},... | collective-permute-start | bytes 4915208 | tf_op jit(solution)/shard_map/ppermute | solution.py:30
  102.8 52.5 %all-to-all-start = ((bf16[64,100,128]{2,1,0:T(8,128)(2,1)}), bf16[64,100,128]{2,1,0:T(8,128)(2,1)S(1)}, u32[]{:S(2)}, u32[]{:S(2)}) async-start(bf16[64,100,128]{2,1,0:T(8,128)(2,1)} %cut.1), calls=%async_computation | async-start | bytes 3407872 | tf_op jit(solution)/shard_map/all_to_all | solution.py:196
  117.5 43.6 %copy-start.12 = (f32[50,128]{1,0:T(8,128)S(1)}, f32[50,128]{1,0:T(8,128)}, u32[]{:S(2)}) copy-start(f32[50,128]{1,0:T(8,128)} %param.12) | copy-start | bytes 76804
  117.5 43.6 %copy-start.13 = (f32[50,128]{1,0:T(8,128)S(1)}, f32[50,128]{1,0:T(8,128)}, u32[]{:S(2)}) copy-start(f32[50,128]{1,0:T(8,128)} %param.13) | copy-start | bytes 76804
  155.6 5.5 %collective-permute-start.11 = (f32[50,128]{1,0:T(8,128)S(1)}, f32[50,128]{1,0:T(8,128)S(1)}, u32[]{:S(2)}, u32[]{:S(2)}) collective-permute-start(f32[50,128]{1,0:T(8,128)S(1)} %constant_dynamic-slice_fusion.1), channel_id=1, source_target_pairs={{0,8},{8,0},{1,9},{9,1},{2,10},{10,2},{3,11},{11,3},{4,12},{12,4},... | collective-permute-start | bytes 76808 | tf_op jit(solution)/shard_map/ppermute | solution.py:30
  185.5 5.7 %collective-permute-start.12 = (bf16[32,50,128]{2,1,0:T(8,128)(2,1)S(1)}, bf16[32,50,128]{2,1,0:T(8,128)(2,1)S(1)}, u32[]{:S(2)}, u32[]{:S(2)}) collective-permute-start(bf16[32,50,128]{2,1,0:T(8,128)(2,1)S(1)} %all_to_all.10), channel_id=1, source_target_pairs={{0,8},{8,0},{1,9},{9,1},{2,10},{10,2},{3,11},{11,3},{4,12},{12,4},... | collective-permute-start | bytes 1228808 | tf_op jit(solution)/shard_map/ppermute | solution.py:30

commit v7 on v6

--- a/solution.py
+++ b/solution.py
@@ -1,3 +1,4 @@
+import functools
 import math
 
 import jax
@@ -79,6 +80,78 @@
     )(half.reshape(1).astype(jnp.int32), *terms)
 
 
+def pack_kernel(core_ref, weights_ref, signs_ref, out_ref):
+    core, words = core_ref[0], signs_ref.shape[0]
+    rows = out_ref.shape[0] - 2 * words
+    out_ref[:rows, :] = weights_ref[pl.ds(pl.multiple_of(core * rows, 16), rows), :]
+    for p in range(2):
+        octet = jnp.right_shift(signs_ref[...], 16 * core + 8 * p) & 255
+        out_ref[rows + p * words : rows + (p + 1) * words, :] = octet.astype(jnp.float32).astype(
+            jnp.bfloat16
+        )
+
+
+def pack(core, weights, signs):
+    rows = weights.shape[0] // 2 + 2 * signs.shape[0]
+    whole = pl.BlockSpec(memory_space=pltpu.VMEM)
+    return pl.pallas_call(
+        pack_kernel,
+        out_shape=jax.ShapeDtypeStruct((rows, weights.shape[1]), jnp.bfloat16),
+        in_specs=[pl.BlockSpec(memory_space=pltpu.SMEM), whole, whole],
+        out_specs=whole,
+        compiler_params=pltpu.CompilerParams(vmem_limit_bytes=4 << 20),
+        cost_estimate=pl.CostEstimate(
+            flops=weights.size, bytes_accessed=2 * weights.size, transcendentals=0
+        ),
+        name="pack",
+    )(core.reshape(1).astype(jnp.int32), weights, signs)
+
+
+def unpack_kernel(words, core_ref, part_ref, twin_ref, out_ref):
+    first = core_ref[0] == 0
+    rows = part_ref.shape[0] - 2 * words
+    width = part_ref.shape[1]
+
+    def fill(low_ref, high_ref):
+        out_ref[:rows, :] = low_ref[:rows, :]
+        out_ref[rows : 2 * rows, :] = high_ref[:rows, :]
+        place_in_byte = lax.broadcasted_iota(jnp.int32, (8, width), 0)
+        for k in range(words):
+            for q, source in enumerate((low_ref, high_ref)):
+                signs = []
+                for p in range(2):
+                    at = rows + p * words + k
+                    octet = source[at : at + 1, :].astype(jnp.float32).astype(jnp.int32)
+                    bits = jnp.right_shift(jnp.broadcast_to(octet, (8, width)), place_in_byte) & 1
+                    signs.append((1 - 2 * bits).astype(jnp.float32))
+                base = 2 * rows + 32 * k + 16 * q
+                out_ref[base : base + 16, :] = jnp.concatenate(signs, axis=0).astype(jnp.bfloat16)
+
+    @pl.when(first)
+    def _():
+        fill(part_ref, twin_ref)
+
+    @pl.when(jnp.logical_not(first))
+    def _():
+        fill(twin_ref, part_ref)
+
+
+def unpack(core, part, twin, words):
+    rows = 2 * (part.shape[0] - 2 * words) + 32 * words
+    whole = pl.BlockSpec(memory_space=pltpu.VMEM)
+    return pl.pallas_call(
+        functools.partial(unpack_kernel, words),
+        out_shape=jax.ShapeDtypeStruct((rows, part.shape[1]), jnp.bfloat16),
+        in_specs=[pl.BlockSpec(memory_space=pltpu.SMEM), whole, whole],
+        out_specs=whole,
+        compiler_params=pltpu.CompilerParams(vmem_limit_bytes=6 << 20),
+        cost_estimate=pl.CostEstimate(
+            flops=8 * part.size, bytes_accessed=6 * part.size, transcendentals=0
+        ),
+        name="unpack",
+    )(core.reshape(1).astype(jnp.int32), part, twin)
+
+
 def join_kernel(*refs):
     count = len(refs) - 2
     blocks, out_ref, arrived = refs[:count], refs[count], refs[count + 1]
@@ -111,7 +184,7 @@
 
 
 def step(hidden, resid, target, w_out, signs, m_old, v_old):
-    features, width = w_out.shape
+    features, _ = w_out.shape
     tokens = hidden.shape[0]
     group = tokens * lax.axis_size("x")
     half = lax.axis_index("yh")
@@ -127,16 +200,7 @@
     far_top = shift(left_top, "x", 1)
     far_low = shift(right_low, "x", -1)
 
-    rows = features // 2
-    octets = jnp.stack([(signs >> (16 * core + 8 * p)) & 255 for p in range(2)])
-    part = jnp.concatenate(
-        [
-            lax.dynamic_slice_in_dim(w_out, core * rows, rows, 0),
-            octets.reshape(-1, width).astype(jnp.bfloat16),
-        ],
-        axis=0,
-    )
-    part = shift(part, "yh", 1)
+    part = shift(pack(core, w_out, signs), "yh", 1)
 
     def gap(at, kind):
         def part(whole):
@@ -151,14 +215,7 @@
     probes = unpack_signs(signs)
     own_stack = jnp.concatenate([w_out, probes], axis=0)
     own_gaps = gap(half, jnp.float32)
-    first = jnp.where(core == 0, part, twin)
-    second = jnp.where(core == 0, twin, part)
-    octets = jnp.stack([first[rows:], second[rows:]]).astype(jnp.int32)
-    octets = octets.reshape(4, -1, 1, width).transpose(1, 0, 2, 3)
-    bits = (octets >> jnp.arange(8, dtype=jnp.int32)[None, None, :, None]) & 1
-    other_stack = jnp.concatenate(
-        [first[:rows], second[:rows], (1 - 2 * bits).reshape(-1, width).astype(jnp.bfloat16)], axis=0
-    )
+    other_stack = unpack(core, part, twin, signs.shape[0])
 
     def run(stacked, gaps, block):
         here = gaps[:, : block.shape[0]] if block.shape[0] > tokens else gaps[:, -tokens:]
@@ -216,7 +273,9 @@
     spread_rows = jnp.broadcast_to(fresh[None], (32, *fresh.shape))
     mine_rows = lax.all_to_all(spread_rows, ("yl", "z"), 0, 0, tiled=True)
     twin_rows = shift(mine_rows, "c", 1)
-    both = jnp.stack([jnp.where(core == 0, mine_rows, twin_rows), jnp.where(core == 0, twin_rows, mine_rows)], axis=1)
+    both = jnp.stack(
+        [jnp.where(core == 0, mine_rows, twin_rows), jnp.where(core == 0, twin_rows, mine_rows)], axis=1
+    )
     new_w = both.reshape(w_out.shape)
     return (new_w, new_m, new_v)
 

time: 194 us -> 187 us (0.964)
  waiting for transfers between devices: 49.8 us -> 57.7 us
  matrix products: 16.7 us -> 9.31 us
  local copies, waits for them, and re-layouts: 15 us -> 9.54 us
  other arithmetic: 11.4 us -> 6.23 us
    ppermute x13, waiting for transfers between devices: 13.6 us -> 22.3 us  [shift(): return lax.ppermute(value, axis, hops)]
    dot_general x8, matrix products: 10 us -> 5.16 us  [run(): jnp.dot(terms, block, preferred_element_type=jnp.float32)]
    convert_element_type x3, other arithmetic: 3.19 us -> 0.45 us  [run(): bends = (forward[features:] / (spread * rooted)).astype(jnp.bfloat16)]
    dot_general x4, matrix products: 6.66 us -> 4.15 us  [run(): lax.dot_general(stacked, block, (((1,), (1,)), ((), ())), preferred_eleme...]
    unnamed x28 -> x12, local copies, waits for them, and re-layouts: 2.5 us -> 0.03 us
    pallas_call x0 -> x2, Pallas kernels: none -> 2.42 us  [the longest x1 1.59 us: unpack(): pl.pallas_call(functools.partial(unpack_kernel, words), out_shape=jax.Sha...]
    shift_right_arithmetic x6, local copies, waits for them, and re-layouts: 1.71 us -> 4.07 us  [unpack_signs(): jnp.right_shift(signs[:, None, :], shifts[None, :, None])]
    shift_right_arithmetic x4 -> x0, local copies, waits for them, and re-layouts: 1.96 us -> none  [step(): bits = octets >> jnp.arange(8, dtype=jnp.int32)[None, None, :, None] & 1]
  transfers between devices with their start and end apart: 14 -> 14, of which waited for: 5 -> 7; matrix products, arithmetic and copies ran while one was open for 16% -> 9% of each run, Pallas kernels for 1% -> 2%
where the time goes in v7:
time: 187 us; the launch traced here: 186 us
  starting transfers between devices  72.6 us (39%)
  waiting for transfers between devices  57.7 us (31%)
  blocking collectives  23.7 us (13%)
  local copies, waits for them, and re-layouts  9.54 us (5%)
  matrix products  9.31 us (5%)
  other arithmetic  6.23 us (3%)
  Pallas kernels  5.73 us (3%)
    ppermute x13, starting transfers between devices, shift(): return lax.ppermute(value, axis, hops)  61 us
    all_to_all x1, waiting for transfers between devices, step(): terms = lax.all_to_all(pieces, ('yh', 'yl', 'z'), 0, 0, tiled=True)  35.4 us
    all_to_all x1, blocking collectives, step(): mine_rows = lax.all_to_all(spread_rows, ('yl', 'z'), 0, 0, tiled=True)  23.7 us
    ppermute x13, waiting for transfers between devices, shift(): return lax.ppermute(value, axis, hops)  22.3 us
    all_to_all x1, starting transfers between devices, step(): terms = lax.all_to_all(pieces, ('yh', 'yl', 'z'), 0, 0, tiled=True)  11.5 us
    dot_general x8, matrix products, run(): jnp.dot(terms, block, preferred_element_type=jnp.float32)  5.16 us
    dot_general x4, matrix products, run(): lax.dot_general(stacked, block, (((1,), (1,)), ((), ())), preferred_eleme...  4.15 us
    shift_right_arithmetic x6, local copies, waits for them, and re-layouts, unpack_signs(): jnp.right_shift(signs[:, None, :], shifts[None, :, None])  4.07 us
  transfers between devices with their start and end apart: 14, of which 7 were waited for; matrix products, arithmetic and copies ran while one was open for 9% of the time, Pallas kernels for 2%

profile of v7, /device:TPU:1, one launch (start us, length us, event | category | flops | bytes accessed | tf_op | source)
XLA Modules:
  0.0 185.9 jit_solution(14440392027634003006)
XLA Ops:
  0.7 2.5 %fusion.56 = (bf16[128,2560]{1,0:T(8,128)(2,1)}, bf16[128,2560]{1,0:T(8,128)(2,1)}) fusion(bf16[256,2560]{1,0:T(8,128)(2,1)} %refs_2_.1), kind=kLoop, calls=%fused_computation.85 | loop fusion | bytes 2621440 | tf_op jit(solution)/shard_map/slice | solution.py:195
  3.2 3.9 %collective-permute-start = (bf16[128,2560]{1,0:T(8,128)(2,1)}, bf16[128,2560]{1,0:T(8,128)(2,1)S(1)}, u32[]{:S(2)}, u32[]{:S(2)}) collective-permute-start(bf16[128,2560]{1,0:T(8,128)(2,1)} %get-tuple-element.29), channel_id=1, source_target_pairs={{0,1},{1,2},{2,3},{3,0},{4,5},{5,6},{6,7},{7,4},{8,9},{9,10},{10,1... | collective-permute-start | bytes 1966088 | tf_op jit(solution)/shard_map/ppermute | solution.py:31
  7.1 3.2 %collective-permute-start.3 = (bf16[128,2560]{1,0:T(8,128)(2,1)}, bf16[128,2560]{1,0:T(8,128)(2,1)S(1)}, u32[]{:S(2)}, u32[]{:S(2)}) collective-permute-start(bf16[128,2560]{1,0:T(8,128)(2,1)} %get-tuple-element.28), channel_id=1, source_target_pairs={{0,3},{1,0},{2,1},{3,2},{4,7},{5,4},{6,5},{7,6},{8,11},{9,8},{10,9... | collective-permute-start | bytes 1966088 | tf_op jit(solution)/shard_map/ppermute | solution.py:31
  10.3 2.1 %collective-permute-start.1 = (bf16[128,2560]{1,0:T(8,128)(2,1)}, bf16[128,2560]{1,0:T(8,128)(2,1)S(1)}, u32[]{:S(2)}, u32[]{:S(2)}) collective-permute-start(bf16[128,2560]{1,0:T(8,128)(2,1)} %get-tuple-element.28), channel_id=1, source_target_pairs={{0,1},{1,2},{2,3},{3,0},{4,5},{5,6},{6,7},{7,4},{8,9},{9,10},{10,1... | collective-permute-start | bytes 1966088 | tf_op jit(solution)/shard_map/ppermute | solution.py:31
  12.4 4.4 %collective-permute-start.2 = (bf16[128,2560]{1,0:T(8,128)(2,1)}, bf16[128,2560]{1,0:T(8,128)(2,1)S(1)}, u32[]{:S(2)}, u32[]{:S(2)}) collective-permute-start(bf16[128,2560]{1,0:T(8,128)(2,1)} %get-tuple-element.29), channel_id=1, source_target_pairs={{0,3},{1,0},{2,1},{3,2},{4,7},{5,4},{6,5},{7,6},{8,11},{9,8},{10,9... | collective-permute-start | bytes 1966088 | tf_op jit(solution)/shard_map/ppermute | solution.py:31
  16.8 0.8 pack.1
  17.7 7.6 %collective-permute-start.4 = (bf16[90,2560]{1,0:T(8,128)(2,1)}, bf16[90,2560]{1,0:T(8,128)(2,1)}, u32[]{:S(2)}, u32[]{:S(2)}) collective-permute-start(bf16[90,2560]{1,0:T(8,128)(2,1)} %pack.1), channel_id=1, source_target_pairs={{0,4},{4,0},{1,5},{5,1},{2,6},{6,2},{3,7},{7,3},{8,12},{12,8},{9,1... | collective-permute-start | bytes 1382408 | tf_op jit(solution)/shard_map/ppermute | solution.py:31
  25.3 0.1 shift_right_arithmetic.45
  25.4 1.3 fusion.3
  26.7 1.6 subtract_convert_fusion
  28.3 0.2 fusion.13
  28.5 0.1 fusion.6
  28.6 9.7 %collective-permute-done.4.part_ref = bf16[90,2560]{1,0:T(8,128)(2,1)} collective-permute-done((bf16[90,2560]{1,0:T(8,128)(2,1)}, bf16[90,2560]{1,0:T(8,128)(2,1)}, u32[]{:S(2)}, u32[]{:S(2)}) %collective-permute-start.4) | collective-permute-done | bytes 460832 | tf_op jit(solution)/shard_map/ppermute | solution.py:31
  38.3 8.4 %collective-permute-start.6 = (bf16[160,1024]{1,0:T(8,128)(2,1)S(1)}, bf16[160,1024]{1,0:T(8,128)(2,1)S(1)}, u32[]{:S(2)}, u32[]{:S(2)}) collective-permute-start(bf16[160,1024]{1,0:T(8,128)(2,1)S(1)} %fusion.13), channel_id=1, source_target_pairs={{0,4},{4,0},{1,5},{5,1},{2,6},{6,2},{3,7},{7,3},{8,12},{12,8},{9,1... | collective-permute-start | bytes 983048 | tf_op jit(solution)/shard_map/ppermute | solution.py:31
  46.7 11.1 %collective-permute-start.5 = (bf16[90,2560]{1,0:T(8,128)(2,1)}, bf16[90,2560]{1,0:T(8,128)(2,1)S(1)}, u32[]{:S(2)}, u32[]{:S(2)}) collective-permute-start(bf16[90,2560]{1,0:T(8,128)(2,1)} %collective-permute-done.4.part_ref), channel_id=1, source_target_pairs={{0,8},{8,0},{1,9},{9,1},{2,10},{10,2},{3,11},{11,3},{4,12},{12,4},... | collective-permute-start | bytes 1382408 | tf_op jit(solution)/shard_map/ppermute | solution.py:31
  57.8 1.0 join.2
  58.8 1.4 fusion.5
  60.3 0.3 fusion.9
  60.6 0.8 fusion.18.refs_0_
  61.4 1.9 %collective-permute-start.7 = (bf16[128,2560]{1,0:T(8,128)(2,1)S(1)}, bf16[128,2560]{1,0:T(8,128)(2,1)S(1)}, u32[]{:S(2)}, u32[]{:S(2)}) collective-permute-start(bf16[128,2560]{1,0:T(8,128)(2,1)S(1)} %collective-permute-done.refs_0_), channel_id=1, source_target_pairs={{0,1},{1,2},{2,3},{3,0},{4,5},{5,6},{6,7},{7,4},{8,9},{9,10},{10,1... | collective-permute-start | bytes 1966088 | tf_op jit(solution)/shard_map/ppermute | solution.py:31
  63.3 4.6 %collective-permute-start.8 = (bf16[128,2560]{1,0:T(8,128)(2,1)S(1)}, bf16[128,2560]{1,0:T(8,128)(2,1)S(1)}, u32[]{:S(2)}, u32[]{:S(2)}) collective-permute-start(bf16[128,2560]{1,0:T(8,128)(2,1)S(1)} %collective-permute-done.3.refs_4_), channel_id=1, source_target_pairs={{0,3},{1,0},{2,1},{3,2},{4,7},{5,4},{6,5},{7,6},{8,11},{9,8},{10,9... | collective-permute-start | bytes 1966088 | tf_op jit(solution)/shard_map/ppermute | solution.py:31
  67.9 0.8 fusion.20
  68.8 1.6 unpack.1
  70.4 1.5 fusion.57
  71.8 0.2 fusion.11
  72.1 1.0 fusion.14.refs_3_
  73.0 0.9 fusion.16
  74.0 6.8 %collective-permute-done.7.refs_0_ = bf16[128,2560]{1,0:T(8,128)(2,1)S(1)} collective-permute-done((bf16[128,2560]{1,0:T(8,128)(2,1)S(1)}, bf16[128,2560]{1,0:T(8,128)(2,1)S(1)}, u32[]{:S(2)}, u32[]{:S(2)}) %collective-permute-start.7) | collective-permute-done | bytes 655392 | tf_op jit(solution)/shard_map/ppermute | solution.py:31
  80.8 0.9 collective-permute-done.8.refs_1_
  81.7 0.4 join.3
  82.1 0.6 fusion.58
  82.8 0.6 fusion.4
  83.4 0.1 fusion.31
  83.5 0.4 fusion.32
  83.9 0.2 add.93
  84.1 3.1 %collective-permute-start.10 = (f32[160,2560]{1,0:T(8,128)S(1)}, f32[160,2560]{1,0:T(8,128)S(1)}, u32[]{:S(2)}, u32[]{:S(2)}) collective-permute-start(f32[160,2560]{1,0:T(8,128)S(1)} %add.93), channel_id=1, source_target_pairs={{0,8},{8,0},{1,9},{9,1},{2,10},{10,2},{3,11},{11,3},{4,12},{12,4},... | collective-permute-start | bytes 4915208 | tf_op jit(solution)/shard_map/ppermute | solution.py:31
  87.1 0.1 fusion.28
  87.3 0.4 fusion.36
  87.6 0.2 add.90
  87.8 1.9 %collective-permute-start.9 = (f32[160,2560]{1,0:T(8,128)S(1)}, f32[160,2560]{1,0:T(8,128)S(1)}, u32[]{:S(2)}, u32[]{:S(2)}) collective-permute-start(f32[160,2560]{1,0:T(8,128)S(1)} %add.90), channel_id=1, source_target_pairs={{0,8},{8,0},{1,9},{9,1},{2,10},{10,2},{3,11},{11,3},{4,12},{12,4},... | collective-permute-start | bytes 4915208 | tf_op jit(solution)/shard_map/ppermute | solution.py:31
  89.8 0.4 fusion.38.refs_1_
  90.1 0.4 fusion.34.refs_4_
  90.6 2.6 %collective-permute-done.9.refs_2_ = f32[160,2560]{1,0:T(8,128)S(1)} collective-permute-done((f32[160,2560]{1,0:T(8,128)S(1)}, f32[160,2560]{1,0:T(8,128)S(1)}, u32[]{:S(2)}, u32[]{:S(2)}) %collective-permute-start.9) | collective-permute-done | bytes 1638432 | tf_op jit(solution)/shard_map/ppermute | solution.py:31
  93.2 1.9 %cut.1 = bf16[64,100,128]{2,1,0:T(8,128)(2,1)} custom-call(s32[1]{0:T(128)} %bitcast.half_ref, f32[160,2560]{1,0:T(8,128)S(1)} %fusion.18.refs_0_, f32[160,2560]{1,0:T(8,128)S(1)} %fusion.38.refs_1_, f32[160,2560]{1,0:T(8,128)S(1)} %collective-permute-done.9.refs_2_, f32[160,2560]{1,0:T(8,128)S(1)} %fusion.14.refs_3_, f32[160,2560]{1,0:T(8,128)S(1)} %fusion.34.refs_4_, ...), custom_call_target="tpu_custom_call" | custom-call | flops 1638400 | bytes 11468800 | tf_op jit(solution)/shard_map/cut/pallas_call | solution.py:71
  95.1 11.5 %all-to-all-start = ((bf16[64,100,128]{2,1,0:T(8,128)(2,1)}), bf16[64,100,128]{2,1,0:T(8,128)(2,1)S(1)}, u32[]{:S(2)}, u32[]{:S(2)}) async-start(bf16[64,100,128]{2,1,0:T(8,128)(2,1)} %cut.1), calls=%async_computation | async-start | bytes 3407872 | tf_op jit(solution)/shard_map/all_to_all | solution.py:253
  106.7 1.0 reshape.30
  107.7 0.1 shift_right_arithmetic.49
  107.8 0.1 shift_right_arithmetic.50
  107.9 1.3 shift_right_arithmetic.42
  109.2 2.5 %shift_right_arithmetic.48 = s32[3200,128]{1,0:T(8,128)} reshape(s32[5,32,2560]{2,1,0:T(8,128)} %shift_right_arithmetic.42) | data formatting | bytes 3276800 | tf_op jit(solution)/shard_map/shift_right_arithmetic | solution.py:36
  111.7 0.1 dynamic-slice
  111.8 0.8 fusion.48
  112.6 35.4 %all-to-all-done = bf16[64,100,128]{2,1,0:T(8,128)(2,1)S(1)} async-done(((bf16[64,100,128]{2,1,0:T(8,128)(2,1)}), bf16[64,100,128]{2,1,0:T(8,128)(2,1)S(1)}, u32[]{:S(2)}, u32[]{:S(2)}) %all-to-all-start) | async-done | bytes 1638432 | tf_op jit(solution)/shard_map/all_to_all | solution.py:253
  148.1 0.3 convert_reduce_fusion
  148.4 4.6 %collective-permute-start.11 = (f32[50,128]{1,0:T(8,128)S(1)}, f32[50,128]{1,0:T(8,128)S(1)}, u32[]{:S(2)}, u32[]{:S(2)}) collective-permute-start(f32[50,128]{1,0:T(8,128)S(1)} %constant_dynamic-slice_fusion.1), channel_id=1, source_target_pairs={{0,8},{8,0},{1,9},{9,1},{2,10},{10,2},{3,11},{11,3},{4,12},{12,4},... | collective-permute-start | bytes 76808 | tf_op jit(solution)/shard_map/ppermute | solution.py:31
  153.0 0.8 collective-permute-done.11
  153.9 0.6 subtract_convert_fusion.1
  154.5 0.1 broadcast_in_dim.2
  154.6 23.7 %all_to_all.10 = bf16[32,50,128]{2,1,0:T(8,128)(2,1)S(1)} all-to-all(bf16[32,50,128]{2,1,0:T(8,128)(2,1)S(1)} %broadcast_in_dim.2), channel_id=1, replica_groups=mesh['yl'=4,'z'=8,'c'=2,'yh'=2,'x'=4] {'yl','z'}, dimensions={0} | all-to-all | bytes 819200 | tf_op jit(solution)/shard_map/all_to_all | solution.py:274
  178.2 4.3 %collective-permute-start.12 = (bf16[32,50,128]{2,1,0:T(8,128)(2,1)S(1)}, bf16[32,50,128]{2,1,0:T(8,128)(2,1)S(1)}, u32[]{:S(2)}, u32[]{:S(2)}) collective-permute-start(bf16[32,50,128]{2,1,0:T(8,128)(2,1)S(1)} %all_to_all.10), channel_id=1, source_target_pairs={{0,8},{8,0},{1,9},{9,1},{2,10},{10,2},{3,11},{11,3},{4,12},{12,4},... | collective-permute-start | bytes 1228808 | tf_op jit(solution)/shard_map/ppermute | solution.py:31
  182.5 1.4 collective-permute-done.12
  183.9 0.1 select_bitcast_fusion.1
  184.0 0.1 pad_maximum_fusion.3
  184.1 1.8 reshape.31
  (22 shorter events, 0.1 us)
Async XLA Ops:
  0.6 16.2 %copy-start.1 = (bf16[160,2560]{1,0:T(8,128)(2,1)S(1)}, bf16[160,2560]{1,0:T(8,128)(2,1)}, u32[]{:S(2)}) copy-start(bf16[160,2560]{1,0:T(8,128)(2,1)} %weights_ref.1) | copy-start | bytes 2457604
  0.6 16.2 %copy-start.2 = (s32[5,2560]{1,0:T(8,128)S(1)}, s32[5,2560]{1,0:T(8,128)}, u32[]{:S(2)}) copy-start(s32[5,2560]{1,0:T(8,128)} %signs_ref.1) | copy-start | bytes 153604
  3.2 43.5 %collective-permute-start = (bf16[128,2560]{1,0:T(8,128)(2,1)}, bf16[128,2560]{1,0:T(8,128)(2,1)S(1)}, u32[]{:S(2)}, u32[]{:S(2)}) collective-permute-start(bf16[128,2560]{1,0:T(8,128)(2,1)} %get-tuple-element.29), channel_id=1, source_target_pairs={{0,1},{1,2},{2,3},{3,0},{4,5},{5,6},{6,7},{7,4},{8,9},{9,10},{10,1... | collective-permute-start | bytes 1966088 | tf_op jit(solution)/shard_map/ppermute | solution.py:31
  7.1 50.7 %collective-permute-start.3 = (bf16[128,2560]{1,0:T(8,128)(2,1)}, bf16[128,2560]{1,0:T(8,128)(2,1)S(1)}, u32[]{:S(2)}, u32[]{:S(2)}) collective-permute-start(bf16[128,2560]{1,0:T(8,128)(2,1)} %get-tuple-element.28), channel_id=1, source_target_pairs={{0,3},{1,0},{2,1},{3,2},{4,7},{5,4},{6,5},{7,6},{8,11},{9,8},{10,9... | collective-permute-start | bytes 1966088 | tf_op jit(solution)/shard_map/ppermute | solution.py:31
  10.3 47.5 %collective-permute-start.1 = (bf16[128,2560]{1,0:T(8,128)(2,1)}, bf16[128,2560]{1,0:T(8,128)(2,1)S(1)}, u32[]{:S(2)}, u32[]{:S(2)}) collective-permute-start(bf16[128,2560]{1,0:T(8,128)(2,1)} %get-tuple-element.28), channel_id=1, source_target_pairs={{0,1},{1,2},{2,3},{3,0},{4,5},{5,6},{6,7},{7,4},{8,9},{9,10},{10,1... | collective-permute-start | bytes 1966088 | tf_op jit(solution)/shard_map/ppermute | solution.py:31
  12.4 45.4 %collective-permute-start.2 = (bf16[128,2560]{1,0:T(8,128)(2,1)}, bf16[128,2560]{1,0:T(8,128)(2,1)S(1)}, u32[]{:S(2)}, u32[]{:S(2)}) collective-permute-start(bf16[128,2560]{1,0:T(8,128)(2,1)} %get-tuple-element.29), channel_id=1, source_target_pairs={{0,3},{1,0},{2,1},{3,2},{4,7},{5,4},{6,5},{7,6},{8,11},{9,8},{10,9... | collective-permute-start | bytes 1966088 | tf_op jit(solution)/shard_map/ppermute | solution.py:31
  17.7 20.7 %collective-permute-start.4 = (bf16[90,2560]{1,0:T(8,128)(2,1)}, bf16[90,2560]{1,0:T(8,128)(2,1)}, u32[]{:S(2)}, u32[]{:S(2)}) collective-permute-start(bf16[90,2560]{1,0:T(8,128)(2,1)} %pack.1), channel_id=1, source_target_pairs={{0,4},{4,0},{1,5},{5,1},{2,6},{6,2},{3,7},{7,3},{8,12},{12,8},{9,1... | collective-permute-start | bytes 1382408 | tf_op jit(solution)/shard_map/ppermute | solution.py:31
  26.7 31.2 %copy-start = (bf16[256,2560]{1,0:T(8,128)(2,1)S(1)}, bf16[256,2560]{1,0:T(8,128)(2,1)}, u32[]{:S(2)}) copy-start(bf16[256,2560]{1,0:T(8,128)(2,1)} %refs_2_.1) | copy-start | bytes 3932164
  28.6 30.2 %copy-start.3 = (bf16[160,2560]{1,0:T(8,128)(2,1)S(1)}, bf16[160,2560]{1,0:T(8,128)(2,1)}, u32[]{:S(2)}) copy-start(bf16[160,2560]{1,0:T(8,128)(2,1)} %fusion.3) | copy-start | bytes 2457604
  38.3 33.5 %collective-permute-start.6 = (bf16[160,1024]{1,0:T(8,128)(2,1)S(1)}, bf16[160,1024]{1,0:T(8,128)(2,1)S(1)}, u32[]{:S(2)}, u32[]{:S(2)}) collective-permute-start(bf16[160,1024]{1,0:T(8,128)(2,1)S(1)} %fusion.13), channel_id=1, source_target_pairs={{0,4},{4,0},{1,5},{5,1},{2,6},{6,2},{3,7},{7,3},{8,12},{12,8},{9,1... | collective-permute-start | bytes 983048 | tf_op jit(solution)/shard_map/ppermute | solution.py:31
  46.7 22.0 %collective-permute-start.5 = (bf16[90,2560]{1,0:T(8,128)(2,1)}, bf16[90,2560]{1,0:T(8,128)(2,1)S(1)}, u32[]{:S(2)}, u32[]{:S(2)}) collective-permute-start(bf16[90,2560]{1,0:T(8,128)(2,1)} %collective-permute-done.4.part_ref), channel_id=1, source_target_pairs={{0,8},{8,0},{1,9},{9,1},{2,10},{10,2},{3,11},{11,3},{4,12},{12,4},... | collective-permute-start | bytes 1382408 | tf_op jit(solution)/shard_map/ppermute | solution.py:31
  61.4 19.4 %collective-permute-start.7 = (bf16[128,2560]{1,0:T(8,128)(2,1)S(1)}, bf16[128,2560]{1,0:T(8,128)(2,1)S(1)}, u32[]{:S(2)}, u32[]{:S(2)}) collective-permute-start(bf16[128,2560]{1,0:T(8,128)(2,1)S(1)} %collective-permute-done.refs_0_), channel_id=1, source_target_pairs={{0,1},{1,2},{2,3},{3,0},{4,5},{5,6},{6,7},{7,4},{8,9},{9,10},{10,1... | collective-permute-start | bytes 1966088 | tf_op jit(solution)/shard_map/ppermute | solution.py:31
  63.3 18.3 %collective-permute-start.8 = (bf16[128,2560]{1,0:T(8,128)(2,1)S(1)}, bf16[128,2560]{1,0:T(8,128)(2,1)S(1)}, u32[]{:S(2)}, u32[]{:S(2)}) collective-permute-start(bf16[128,2560]{1,0:T(8,128)(2,1)S(1)} %collective-permute-done.3.refs_4_), channel_id=1, source_target_pairs={{0,3},{1,0},{2,1},{3,2},{4,7},{5,4},{6,5},{7,6},{8,11},{9,8},{10,9... | collective-permute-start | bytes 1966088 | tf_op jit(solution)/shard_map/ppermute | solution.py:31
  84.1 6.5 %collective-permute-start.10 = (f32[160,2560]{1,0:T(8,128)S(1)}, f32[160,2560]{1,0:T(8,128)S(1)}, u32[]{:S(2)}, u32[]{:S(2)}) collective-permute-start(f32[160,2560]{1,0:T(8,128)S(1)} %add.93), channel_id=1, source_target_pairs={{0,8},{8,0},{1,9},{9,1},{2,10},{10,2},{3,11},{11,3},{4,12},{12,4},... | collective-permute-start | bytes 4915208 | tf_op jit(solution)/shard_map/ppermute | solution.py:31
  87.8 5.4 %collective-permute-start.9 = (f32[160,2560]{1,0:T(8,128)S(1)}, f32[160,2560]{1,0:T(8,128)S(1)}, u32[]{:S(2)}, u32[]{:S(2)}) collective-permute-start(f32[160,2560]{1,0:T(8,128)S(1)} %add.90), channel_id=1, source_target_pairs={{0,8},{8,0},{1,9},{9,1},{2,10},{10,2},{3,11},{11,3},{4,12},{12,4},... | collective-permute-start | bytes 4915208 | tf_op jit(solution)/shard_map/ppermute | solution.py:31
  95.1 52.9 %all-to-all-start = ((bf16[64,100,128]{2,1,0:T(8,128)(2,1)}), bf16[64,100,128]{2,1,0:T(8,128)(2,1)S(1)}, u32[]{:S(2)}, u32[]{:S(2)}) async-start(bf16[64,100,128]{2,1,0:T(8,128)(2,1)} %cut.1), calls=%async_computation | async-start | bytes 3407872 | tf_op jit(solution)/shard_map/all_to_all | solution.py:253
  111.7 42.2 %copy-start.4 = (f32[50,128]{1,0:T(8,128)S(1)}, f32[50,128]{1,0:T(8,128)}, u32[]{:S(2)}) copy-start(f32[50,128]{1,0:T(8,128)} %param.12) | copy-start | bytes 76804
  111.7 42.2 %copy-start.5 = (f32[50,128]{1,0:T(8,128)S(1)}, f32[50,128]{1,0:T(8,128)}, u32[]{:S(2)}) copy-start(f32[50,128]{1,0:T(8,128)} %param.13) | copy-start | bytes 76804
  148.4 5.5 %collective-permute-start.11 = (f32[50,128]{1,0:T(8,128)S(1)}, f32[50,128]{1,0:T(8,128)S(1)}, u32[]{:S(2)}, u32[]{:S(2)}) collective-permute-start(f32[50,128]{1,0:T(8,128)S(1)} %constant_dynamic-slice_fusion.1), channel_id=1, source_target_pairs={{0,8},{8,0},{1,9},{9,1},{2,10},{10,2},{3,11},{11,3},{4,12},{12,4},... | collective-permute-start | bytes 76808 | tf_op jit(solution)/shard_map/ppermute | solution.py:31
  178.2 5.7 %collective-permute-start.12 = (bf16[32,50,128]{2,1,0:T(8,128)(2,1)S(1)}, bf16[32,50,128]{2,1,0:T(8,128)(2,1)S(1)}, u32[]{:S(2)}, u32[]{:S(2)}) collective-permute-start(bf16[32,50,128]{2,1,0:T(8,128)(2,1)S(1)} %all_to_all.10), channel_id=1, source_target_pairs={{0,8},{8,0},{1,9},{9,1},{2,10},{10,2},{3,11},{11,3},{4,12},{12,4},... | collective-permute-start | bytes 1228808 | tf_op jit(solution)/shard_map/ppermute | solution.py:31

commit v8 on v7

--- a/solution.py
+++ b/solution.py
@@ -152,6 +152,33 @@
     )(core.reshape(1).astype(jnp.int32), part, twin)
 
 
+def gap_kernel(spot_ref, resid_ref, target_ref, own_ref, other_ref):
+    half, col = spot_ref[0], spot_ref[1]
+    tokens = own_ref.shape[1] // 4
+    for at, out_ref in ((half, own_ref), (1 - half, other_ref)):
+        for j in range(4):
+            start = at * 4 * tokens + lax.rem(col + 3 + j, 4) * tokens
+            cols = pl.ds(pl.multiple_of(start, 128), tokens)
+            gaps = resid_ref[:, cols].astype(jnp.float32) - target_ref[:, cols].astype(jnp.float32)
+            out_ref[:, j * tokens : (j + 1) * tokens] = gaps.astype(out_ref.dtype)
+
+
+def gap_pair(half, col, resid, target, group):
+    whole = pl.BlockSpec(memory_space=pltpu.VMEM)
+    shape = (resid.shape[0], group)
+    return pl.pallas_call(
+        gap_kernel,
+        out_shape=[jax.ShapeDtypeStruct(shape, kind) for kind in (jnp.float32, jnp.bfloat16)],
+        in_specs=[pl.BlockSpec(memory_space=pltpu.SMEM), whole, whole],
+        out_specs=[whole, whole],
+        compiler_params=pltpu.CompilerParams(vmem_limit_bytes=6 << 20),
+        cost_estimate=pl.CostEstimate(
+            flops=resid.size, bytes_accessed=8 * resid.size, transcendentals=0
+        ),
+        name="gap",
+    )(jnp.stack([half, col]).astype(jnp.int32), resid, target)
+
+
 def join_kernel(*refs):
     count = len(refs) - 2
     blocks, out_ref, arrived = refs[:count], refs[count], refs[count + 1]
@@ -202,19 +229,11 @@
 
     part = shift(pack(core, w_out, signs), "yh", 1)
 
-    def gap(at, kind):
-        def part(whole):
-            return lax.dynamic_slice_in_dim(whole, at * group, group, 1).astype(jnp.float32)
-
-        gaps = (part(resid) - part(target)).astype(kind)
-        gaps = jnp.concatenate([gaps, gaps], axis=1)
-        return lax.dynamic_slice_in_dim(gaps, ((col + 3) % 4) * tokens, group, 1)
-
-    other_gaps = shift(gap(1 - half, jnp.bfloat16), "yh", 1)
+    own_gaps, other_gaps = gap_pair(half, col, resid, target, group)
+    other_gaps = shift(other_gaps, "yh", 1)
     twin = shift(part, "c", 1)
     probes = unpack_signs(signs)
     own_stack = jnp.concatenate([w_out, probes], axis=0)
-    own_gaps = gap(half, jnp.float32)
     other_stack = unpack(core, part, twin, signs.shape[0])
 
     def run(stacked, gaps, block):
@@ -229,6 +248,7 @@
         bends = (forward[features:] / (spread * rooted)).astype(jnp.bfloat16)
         away = jnp.where(core == 0, bends, slopes)
         kept = jnp.where(core == 0, slopes, bends)
+        away, kept = lax.optimization_barrier((away, kept))
         return [jnp.dot(terms, block, preferred_element_type=jnp.float32) for terms in (away, kept)]
 
     near = join((left_top, left_low, hidden, right_top, right_low))

time: 187 us -> 189 us (1.011)
  waiting for transfers between devices: 57.7 us -> 61.1 us
    shift_right_arithmetic x6, local copies, waits for them, and re-layouts: 4.07 us -> 0.53 us  [unpack_signs(): jnp.right_shift(signs[:, None, :], shifts[None, :, None])]
    all_to_all x1, waiting for transfers between devices: 35.4 us -> 37.8 us  [step(): terms = lax.all_to_all(pieces, ('yh', 'yl', 'z'), 0, 0, tiled=True)]
    convert_element_type x5 -> x0, other arithmetic: 2.34 us -> none  [the longest x1 1.59 us: gap(): gaps = (part(resid) - part(target)).astype(kind)]
  transfers between devices with their start and end apart: 14 -> 14, of which waited for: 7 -> 7; matrix products, arithmetic and copies ran while one was open for 9% -> 6% of each run, Pallas kernels for 2% -> 3%
where the time goes in v8:
time: 189 us
  starting transfers between devices  72.8 us (39%)
  waiting for transfers between devices  61.1 us (32%)
  blocking collectives  23.6 us (12%)
  local copies, waits for them, and re-layouts  9.26 us (5%)
  matrix products  8.91 us (5%)
  Pallas kernels  7.2 us (4%)
  other arithmetic  4.48 us (2%)
    ppermute x13, starting transfers between devices, shift(): return lax.ppermute(value, axis, hops)  61 us
    all_to_all x1, waiting for transfers between devices, step(): terms = lax.all_to_all(pieces, ('yh', 'yl', 'z'), 0, 0, tiled=True)  37.8 us
    all_to_all x1, blocking collectives, step(): mine_rows = lax.all_to_all(spread_rows, ('yl', 'z'), 0, 0, tiled=True)  23.6 us
    ppermute x13, waiting for transfers between devices, shift(): return lax.ppermute(value, axis, hops)  23.3 us
    all_to_all x1, starting transfers between devices, step(): terms = lax.all_to_all(pieces, ('yh', 'yl', 'z'), 0, 0, tiled=True)  11.8 us
    dot_general x8, matrix products, run(): jnp.dot(terms, block, preferred_element_type=jnp.float32)  4.75 us
    dot_general x4, matrix products, run(): lax.dot_general(stacked, block, (((1,), (1,)), ((), ())), preferred_eleme...  4.17 us
  transfers between devices with their start and end apart: 14, of which 7 were waited for; matrix products, arithmetic and copies ran while one was open for 6% of the time, Pallas kernels for 3%

profile of v8, /device:TPU:1, one launch (start us, length us, event | category | flops | bytes accessed | tf_op | source)
XLA Modules:
  0.0 188.5 jit_solution(3819900128151315156)
XLA Ops:
  0.7 2.6 %fusion.34 = (bf16[128,2560]{1,0:T(8,128)(2,1)}, bf16[128,2560]{1,0:T(8,128)(2,1)}) fusion(bf16[256,2560]{1,0:T(8,128)(2,1)} %refs_2_.1), kind=kLoop, calls=%fused_computation.62 | loop fusion | bytes 2621440 | tf_op jit(solution)/shard_map/slice | solution.py:222
  3.3 3.9 %collective-permute-start = (bf16[128,2560]{1,0:T(8,128)(2,1)}, bf16[128,2560]{1,0:T(8,128)(2,1)}, u32[]{:S(2)}, u32[]{:S(2)}) collective-permute-start(bf16[128,2560]{1,0:T(8,128)(2,1)} %get-tuple-element.57), channel_id=1, source_target_pairs={{0,1},{1,2},{2,3},{3,0},{4,5},{5,6},{6,7},{7,4},{8,9},{9,10},{10,1... | collective-permute-start | bytes 1966088 | tf_op jit(solution)/shard_map/ppermute | solution.py:31
  7.2 3.2 %collective-permute-start.3 = (bf16[128,2560]{1,0:T(8,128)(2,1)}, bf16[128,2560]{1,0:T(8,128)(2,1)}, u32[]{:S(2)}, u32[]{:S(2)}) collective-permute-start(bf16[128,2560]{1,0:T(8,128)(2,1)} %get-tuple-element.56), channel_id=1, source_target_pairs={{0,3},{1,0},{2,1},{3,2},{4,7},{5,4},{6,5},{7,6},{8,11},{9,8},{10,9... | collective-permute-start | bytes 1966088 | tf_op jit(solution)/shard_map/ppermute | solution.py:31
  10.4 2.1 %collective-permute-start.1 = (bf16[128,2560]{1,0:T(8,128)(2,1)}, bf16[128,2560]{1,0:T(8,128)(2,1)}, u32[]{:S(2)}, u32[]{:S(2)}) collective-permute-start(bf16[128,2560]{1,0:T(8,128)(2,1)} %get-tuple-element.56), channel_id=1, source_target_pairs={{0,1},{1,2},{2,3},{3,0},{4,5},{5,6},{6,7},{7,4},{8,9},{9,10},{10,1... | collective-permute-start | bytes 1966088 | tf_op jit(solution)/shard_map/ppermute | solution.py:31
  12.5 4.4 %collective-permute-start.2 = (bf16[128,2560]{1,0:T(8,128)(2,1)}, bf16[128,2560]{1,0:T(8,128)(2,1)}, u32[]{:S(2)}, u32[]{:S(2)}) collective-permute-start(bf16[128,2560]{1,0:T(8,128)(2,1)} %get-tuple-element.57), channel_id=1, source_target_pairs={{0,3},{1,0},{2,1},{3,2},{4,7},{5,4},{6,5},{7,6},{8,11},{9,8},{10,9... | collective-permute-start | bytes 1966088 | tf_op jit(solution)/shard_map/ppermute | solution.py:31
  16.9 0.8 pack.1
  17.8 7.6 %collective-permute-start.4 = (bf16[90,2560]{1,0:T(8,128)(2,1)}, bf16[90,2560]{1,0:T(8,128)(2,1)}, u32[]{:S(2)}, u32[]{:S(2)}) collective-permute-start(bf16[90,2560]{1,0:T(8,128)(2,1)} %pack.1), channel_id=1, source_target_pairs={{0,4},{4,0},{1,5},{5,1},{2,6},{6,2},{3,7},{7,3},{8,12},{12,8},{9,1... | collective-permute-start | bytes 1382408 | tf_op jit(solution)/shard_map/ppermute | solution.py:31
  25.4 0.1 pad_add_fusion.spot_ref
  25.5 0.7 gap.1
  26.2 0.8 copy-done.5
  27.1 0.7 copy-done.7
  27.8 0.1 shift_right_arithmetic.45
  27.9 0.4 fusion.3
  28.2 10.2 %collective-permute-done.4.part_ref = bf16[90,2560]{1,0:T(8,128)(2,1)} collective-permute-done((bf16[90,2560]{1,0:T(8,128)(2,1)}, bf16[90,2560]{1,0:T(8,128)(2,1)}, u32[]{:S(2)}, u32[]{:S(2)}) %collective-permute-start.4) | collective-permute-done | bytes 460832 | tf_op jit(solution)/shard_map/ppermute | solution.py:31
  38.4 8.4 %collective-permute-start.6 = (bf16[160,1024]{1,0:T(8,128)(2,1)}, bf16[160,1024]{1,0:T(8,128)(2,1)S(1)}, u32[]{:S(2)}, u32[]{:S(2)}) collective-permute-start(bf16[160,1024]{1,0:T(8,128)(2,1)} %copy-done.7), channel_id=1, source_target_pairs={{0,4},{4,0},{1,5},{5,1},{2,6},{6,2},{3,7},{7,3},{8,12},{12,8},{9,1... | collective-permute-start | bytes 983048 | tf_op jit(solution)/shard_map/ppermute | solution.py:31
  46.8 11.1 %collective-permute-start.5 = (bf16[90,2560]{1,0:T(8,128)(2,1)}, bf16[90,2560]{1,0:T(8,128)(2,1)S(1)}, u32[]{:S(2)}, u32[]{:S(2)}) collective-permute-start(bf16[90,2560]{1,0:T(8,128)(2,1)} %collective-permute-done.4.part_ref), channel_id=1, source_target_pairs={{0,8},{8,0},{1,9},{9,1},{2,10},{10,2},{3,11},{11,3},{4,12},{12,4},... | collective-permute-start | bytes 1382408 | tf_op jit(solution)/shard_map/ppermute | solution.py:31
  57.9 1.7 join.2
  59.7 1.5 fusion.5
  61.2 0.3 broadcast_select_fusion.2
  61.6 0.8 fusion.36.refs_0_
  62.4 1.9 %collective-permute-start.7 = (bf16[128,2560]{1,0:T(8,128)(2,1)}, bf16[128,2560]{1,0:T(8,128)(2,1)S(1)}, u32[]{:S(2)}, u32[]{:S(2)}) collective-permute-start(bf16[128,2560]{1,0:T(8,128)(2,1)} %collective-permute-done.refs_0_), channel_id=1, source_target_pairs={{0,1},{1,2},{2,3},{3,0},{4,5},{5,6},{6,7},{7,4},{8,9},{9,10},{10,1... | collective-permute-start | bytes 1966088 | tf_op jit(solution)/shard_map/ppermute | solution.py:31
  64.3 4.6 %collective-permute-start.8 = (bf16[128,2560]{1,0:T(8,128)(2,1)}, bf16[128,2560]{1,0:T(8,128)(2,1)S(1)}, u32[]{:S(2)}, u32[]{:S(2)}) collective-permute-start(bf16[128,2560]{1,0:T(8,128)(2,1)} %collective-permute-done.3.refs_4_), channel_id=1, source_target_pairs={{0,3},{1,0},{2,1},{3,2},{4,7},{5,4},{6,5},{7,6},{8,11},{9,8},{10,9... | collective-permute-start | bytes 1966088 | tf_op jit(solution)/shard_map/ppermute | solution.py:31
  68.9 0.8 fusion.35
  69.7 1.6 unpack.1
  71.3 1.5 fusion.37
  72.8 0.4 broadcast_select_fusion
  73.2 0.8 fusion.39.refs_3_
  74.0 0.8 fusion.38
  74.8 7.1 %collective-permute-done.7.refs_0_ = bf16[128,2560]{1,0:T(8,128)(2,1)S(1)} collective-permute-done((bf16[128,2560]{1,0:T(8,128)(2,1)}, bf16[128,2560]{1,0:T(8,128)(2,1)S(1)}, u32[]{:S(2)}, u32[]{:S(2)}) %collective-permute-start.7) | collective-permute-done | bytes 655392 | tf_op jit(solution)/shard_map/ppermute | solution.py:31
  82.0 1.0 collective-permute-done.8.refs_1_
  83.0 0.4 join.3
  83.4 0.6 fusion.4
  84.0 0.6 fusion.42
  84.7 0.1 broadcast_select_fusion.6
  84.8 0.1 broadcast_select_fusion.4
  84.9 0.4 fusion.44
  85.3 0.2 add.67
  85.6 3.1 %collective-permute-start.10 = (f32[160,2560]{1,0:T(8,128)S(1)}, f32[160,2560]{1,0:T(8,128)S(1)}, u32[]{:S(2)}, u32[]{:S(2)}) collective-permute-start(f32[160,2560]{1,0:T(8,128)S(1)} %add.67), channel_id=1, source_target_pairs={{0,8},{8,0},{1,9},{9,1},{2,10},{10,2},{3,11},{11,3},{4,12},{12,4},... | collective-permute-start | bytes 4915208 | tf_op jit(solution)/shard_map/ppermute | solution.py:31
  88.6 0.4 fusion.41
  89.0 0.2 add.64
  89.2 1.9 %collective-permute-start.9 = (f32[160,2560]{1,0:T(8,128)S(1)}, f32[160,2560]{1,0:T(8,128)S(1)}, u32[]{:S(2)}, u32[]{:S(2)}) collective-permute-start(f32[160,2560]{1,0:T(8,128)S(1)} %add.64), channel_id=1, source_target_pairs={{0,8},{8,0},{1,9},{9,1},{2,10},{10,2},{3,11},{11,3},{4,12},{12,4},... | collective-permute-start | bytes 4915208 | tf_op jit(solution)/shard_map/ppermute | solution.py:31
  91.1 0.4 fusion.43.refs_4_
  91.5 0.4 fusion.40.refs_1_
  91.9 2.7 %collective-permute-done.9.refs_2_ = f32[160,2560]{1,0:T(8,128)S(1)} collective-permute-done((f32[160,2560]{1,0:T(8,128)S(1)}, f32[160,2560]{1,0:T(8,128)S(1)}, u32[]{:S(2)}, u32[]{:S(2)}) %collective-permute-start.9) | collective-permute-done | bytes 1638432 | tf_op jit(solution)/shard_map/ppermute | solution.py:31
  94.6 1.9 %cut.1 = bf16[64,100,128]{2,1,0:T(8,128)(2,1)} custom-call(s32[1]{0:T(128)} %bitcast.half_ref, f32[160,2560]{1,0:T(8,128)S(1)} %fusion.36.refs_0_, f32[160,2560]{1,0:T(8,128)S(1)} %fusion.40.refs_1_, f32[160,2560]{1,0:T(8,128)S(1)} %collective-permute-done.9.refs_2_, f32[160,2560]{1,0:T(8,128)S(1)} %fusion.39.refs_3_, f32[160,2560]{1,0:T(8,128)S(1)} %fusion.43.refs_4_, ...), custom_call_target="tpu_custom_call" | custom-call | flops 1638400 | bytes 11468800 | tf_op jit(solution)/shard_map/cut/pallas_call | solution.py:71
  96.5 11.8 %all-to-all-start = ((bf16[64,100,128]{2,1,0:T(8,128)(2,1)}), bf16[64,100,128]{2,1,0:T(8,128)(2,1)}, u32[]{:S(2)}, u32[]{:S(2)}) async-start(bf16[64,100,128]{2,1,0:T(8,128)(2,1)} %cut.1), calls=%async_computation | async-start | bytes 3407872 | tf_op jit(solution)/shard_map/all_to_all | solution.py:273
  108.3 1.9 reshape.30
  110.1 0.1 shift_right_arithmetic.49
  110.2 0.1 shift_right_arithmetic.50
  110.3 0.2 shift_right_arithmetic.42
  110.5 0.1 shift_right_arithmetic.48
  110.7 0.1 dynamic-slice
  110.7 0.7 constant_dynamic-slice_fusion.1
  111.5 0.1 fusion.22
  111.5 37.8 %all-to-all-done = bf16[64,100,128]{2,1,0:T(8,128)(2,1)} async-done(((bf16[64,100,128]{2,1,0:T(8,128)(2,1)}), bf16[64,100,128]{2,1,0:T(8,128)(2,1)}, u32[]{:S(2)}, u32[]{:S(2)}) %all-to-all-start) | async-done | bytes 1638432 | tf_op jit(solution)/shard_map/all_to_all | solution.py:273
  149.4 1.7 convert_reduce_fusion
  151.1 4.6 %collective-permute-start.11 = (f32[50,128]{1,0:T(8,128)S(1)}, f32[50,128]{1,0:T(8,128)S(1)}, u32[]{:S(2)}, u32[]{:S(2)}) collective-permute-start(f32[50,128]{1,0:T(8,128)S(1)} %constant_dynamic-slice_fusion), channel_id=1, source_target_pairs={{0,8},{8,0},{1,9},{9,1},{2,10},{10,2},{3,11},{11,3},{4,12},{12,4},... | collective-permute-start | bytes 76808 | tf_op jit(solution)/shard_map/ppermute | solution.py:31
  155.7 0.8 collective-permute-done.11
  156.5 0.6 subtract_convert_fusion
  157.2 23.6 %all_to_all.10 = bf16[32,50,128]{2,1,0:T(8,128)(2,1)S(1)} all-to-all(bf16[32,50,128]{2,1,0:T(8,128)(2,1)S(1)} %broadcast_in_dim.2), channel_id=1, replica_groups=mesh['yl'=4,'z'=8,'c'=2,'yh'=2,'x'=4] {'yl','z'}, dimensions={0} | all-to-all | bytes 819200 | tf_op jit(solution)/shard_map/all_to_all | solution.py:294
  180.8 4.3 %collective-permute-start.12 = (bf16[32,50,128]{2,1,0:T(8,128)(2,1)S(1)}, bf16[32,50,128]{2,1,0:T(8,128)(2,1)S(1)}, u32[]{:S(2)}, u32[]{:S(2)}) collective-permute-start(bf16[32,50,128]{2,1,0:T(8,128)(2,1)S(1)} %all_to_all.10), channel_id=1, source_target_pairs={{0,8},{8,0},{1,9},{9,1},{2,10},{10,2},{3,11},{11,3},{4,12},{12,4},... | collective-permute-start | bytes 1228808 | tf_op jit(solution)/shard_map/ppermute | solution.py:31
  185.1 1.4 collective-permute-done.12
  186.6 0.1 pad_maximum_fusion.3
  186.7 1.8 reshape.31
  (32 shorter events, 0.3 us)
Async XLA Ops:
  0.6 16.3 %copy-start.1 = (bf16[160,2560]{1,0:T(8,128)(2,1)S(1)}, bf16[160,2560]{1,0:T(8,128)(2,1)}, u32[]{:S(2)}) copy-start(bf16[160,2560]{1,0:T(8,128)(2,1)} %weights_ref.1) | copy-start | bytes 2457604
  0.6 16.3 %copy-start.2 = (s32[5,2560]{1,0:T(8,128)S(1)}, s32[5,2560]{1,0:T(8,128)}, u32[]{:S(2)}) copy-start(s32[5,2560]{1,0:T(8,128)} %signs_ref.1) | copy-start | bytes 153604
  0.7 24.8 %copy-start.3 = (bf16[160,2048]{1,0:T(8,128)(2,1)S(1)}, bf16[160,2048]{1,0:T(8,128)(2,1)}, u32[]{:S(2)}) copy-start(bf16[160,2048]{1,0:T(8,128)(2,1)} %resid_ref.1) | copy-start | bytes 1966084
  0.7 24.8 %copy-start.4 = (bf16[160,2048]{1,0:T(8,128)(2,1)S(1)}, bf16[160,2048]{1,0:T(8,128)(2,1)}, u32[]{:S(2)}) copy-start(bf16[160,2048]{1,0:T(8,128)(2,1)} %target_ref.1) | copy-start | bytes 1966084
  3.3 43.6 %collective-permute-start = (bf16[128,2560]{1,0:T(8,128)(2,1)}, bf16[128,2560]{1,0:T(8,128)(2,1)}, u32[]{:S(2)}, u32[]{:S(2)}) collective-permute-start(bf16[128,2560]{1,0:T(8,128)(2,1)} %get-tuple-element.57), channel_id=1, source_target_pairs={{0,1},{1,2},{2,3},{3,0},{4,5},{5,6},{6,7},{7,4},{8,9},{9,10},{10,1... | collective-permute-start | bytes 1966088 | tf_op jit(solution)/shard_map/ppermute | solution.py:31
  7.2 50.7 %collective-permute-start.3 = (bf16[128,2560]{1,0:T(8,128)(2,1)}, bf16[128,2560]{1,0:T(8,128)(2,1)}, u32[]{:S(2)}, u32[]{:S(2)}) collective-permute-start(bf16[128,2560]{1,0:T(8,128)(2,1)} %get-tuple-element.56), channel_id=1, source_target_pairs={{0,3},{1,0},{2,1},{3,2},{4,7},{5,4},{6,5},{7,6},{8,11},{9,8},{10,9... | collective-permute-start | bytes 1966088 | tf_op jit(solution)/shard_map/ppermute | solution.py:31
  10.4 47.5 %collective-permute-start.1 = (bf16[128,2560]{1,0:T(8,128)(2,1)}, bf16[128,2560]{1,0:T(8,128)(2,1)}, u32[]{:S(2)}, u32[]{:S(2)}) collective-permute-start(bf16[128,2560]{1,0:T(8,128)(2,1)} %get-tuple-element.56), channel_id=1, source_target_pairs={{0,1},{1,2},{2,3},{3,0},{4,5},{5,6},{6,7},{7,4},{8,9},{9,10},{10,1... | collective-permute-start | bytes 1966088 | tf_op jit(solution)/shard_map/ppermute | solution.py:31
  12.5 45.4 %collective-permute-start.2 = (bf16[128,2560]{1,0:T(8,128)(2,1)}, bf16[128,2560]{1,0:T(8,128)(2,1)}, u32[]{:S(2)}, u32[]{:S(2)}) collective-permute-start(bf16[128,2560]{1,0:T(8,128)(2,1)} %get-tuple-element.57), channel_id=1, source_target_pairs={{0,3},{1,0},{2,1},{3,2},{4,7},{5,4},{6,5},{7,6},{8,11},{9,8},{10,9... | collective-permute-start | bytes 1966088 | tf_op jit(solution)/shard_map/ppermute | solution.py:31
  16.9 41.0 %copy-start = (bf16[256,2560]{1,0:T(8,128)(2,1)S(1)}, bf16[256,2560]{1,0:T(8,128)(2,1)}, u32[]{:S(2)}) copy-start(bf16[256,2560]{1,0:T(8,128)(2,1)} %refs_2_.1) | copy-start | bytes 3932164
  17.8 20.7 %collective-permute-start.4 = (bf16[90,2560]{1,0:T(8,128)(2,1)}, bf16[90,2560]{1,0:T(8,128)(2,1)}, u32[]{:S(2)}, u32[]{:S(2)}) collective-permute-start(bf16[90,2560]{1,0:T(8,128)(2,1)} %pack.1), channel_id=1, source_target_pairs={{0,4},{4,0},{1,5},{5,1},{2,6},{6,2},{3,7},{7,3},{8,12},{12,8},{9,1... | collective-permute-start | bytes 1382408 | tf_op jit(solution)/shard_map/ppermute | solution.py:31
  26.2 0.8 copy-start.5
  27.1 0.7 copy-start.7
  38.4 34.4 %collective-permute-start.6 = (bf16[160,1024]{1,0:T(8,128)(2,1)}, bf16[160,1024]{1,0:T(8,128)(2,1)S(1)}, u32[]{:S(2)}, u32[]{:S(2)}) collective-permute-start(bf16[160,1024]{1,0:T(8,128)(2,1)} %copy-done.7), channel_id=1, source_target_pairs={{0,4},{4,0},{1,5},{5,1},{2,6},{6,2},{3,7},{7,3},{8,12},{12,8},{9,1... | collective-permute-start | bytes 983048 | tf_op jit(solution)/shard_map/ppermute | solution.py:31
  46.8 22.9 %collective-permute-start.5 = (bf16[90,2560]{1,0:T(8,128)(2,1)}, bf16[90,2560]{1,0:T(8,128)(2,1)S(1)}, u32[]{:S(2)}, u32[]{:S(2)}) collective-permute-start(bf16[90,2560]{1,0:T(8,128)(2,1)} %collective-permute-done.4.part_ref), channel_id=1, source_target_pairs={{0,8},{8,0},{1,9},{9,1},{2,10},{10,2},{3,11},{11,3},{4,12},{12,4},... | collective-permute-start | bytes 1382408 | tf_op jit(solution)/shard_map/ppermute | solution.py:31
  59.7 1.5 copy-start.6
  62.4 19.6 %collective-permute-start.7 = (bf16[128,2560]{1,0:T(8,128)(2,1)}, bf16[128,2560]{1,0:T(8,128)(2,1)S(1)}, u32[]{:S(2)}, u32[]{:S(2)}) collective-permute-start(bf16[128,2560]{1,0:T(8,128)(2,1)} %collective-permute-done.refs_0_), channel_id=1, source_target_pairs={{0,1},{1,2},{2,3},{3,0},{4,5},{5,6},{6,7},{7,4},{8,9},{9,10},{10,1... | collective-permute-start | bytes 1966088 | tf_op jit(solution)/shard_map/ppermute | solution.py:31
  64.3 18.7 %collective-permute-start.8 = (bf16[128,2560]{1,0:T(8,128)(2,1)}, bf16[128,2560]{1,0:T(8,128)(2,1)S(1)}, u32[]{:S(2)}, u32[]{:S(2)}) collective-permute-start(bf16[128,2560]{1,0:T(8,128)(2,1)} %collective-permute-done.3.refs_4_), channel_id=1, source_target_pairs={{0,3},{1,0},{2,1},{3,2},{4,7},{5,4},{6,5},{7,6},{8,11},{9,8},{10,9... | collective-permute-start | bytes 1966088 | tf_op jit(solution)/shard_map/ppermute | solution.py:31
  85.6 6.3 %collective-permute-start.10 = (f32[160,2560]{1,0:T(8,128)S(1)}, f32[160,2560]{1,0:T(8,128)S(1)}, u32[]{:S(2)}, u32[]{:S(2)}) collective-permute-start(f32[160,2560]{1,0:T(8,128)S(1)} %add.67), channel_id=1, source_target_pairs={{0,8},{8,0},{1,9},{9,1},{2,10},{10,2},{3,11},{11,3},{4,12},{12,4},... | collective-permute-start | bytes 4915208 | tf_op jit(solution)/shard_map/ppermute | solution.py:31
  89.2 5.4 %collective-permute-start.9 = (f32[160,2560]{1,0:T(8,128)S(1)}, f32[160,2560]{1,0:T(8,128)S(1)}, u32[]{:S(2)}, u32[]{:S(2)}) collective-permute-start(f32[160,2560]{1,0:T(8,128)S(1)} %add.64), channel_id=1, source_target_pairs={{0,8},{8,0},{1,9},{9,1},{2,10},{10,2},{3,11},{11,3},{4,12},{12,4},... | collective-permute-start | bytes 4915208 | tf_op jit(solution)/shard_map/ppermute | solution.py:31
  96.5 52.9 %all-to-all-start = ((bf16[64,100,128]{2,1,0:T(8,128)(2,1)}), bf16[64,100,128]{2,1,0:T(8,128)(2,1)}, u32[]{:S(2)}, u32[]{:S(2)}) async-start(bf16[64,100,128]{2,1,0:T(8,128)(2,1)} %cut.1), calls=%async_computation | async-start | bytes 3407872 | tf_op jit(solution)/shard_map/all_to_all | solution.py:273
  110.6 45.9 %copy-start.8 = (f32[50,128]{1,0:T(8,128)S(1)}, f32[50,128]{1,0:T(8,128)}, u32[]{:S(2)}) copy-start(f32[50,128]{1,0:T(8,128)} %param.12) | copy-start | bytes 76804
  110.6 45.9 %copy-start.9 = (f32[50,128]{1,0:T(8,128)S(1)}, f32[50,128]{1,0:T(8,128)}, u32[]{:S(2)}) copy-start(f32[50,128]{1,0:T(8,128)} %param.13) | copy-start | bytes 76804
  151.1 5.4 %collective-permute-start.11 = (f32[50,128]{1,0:T(8,128)S(1)}, f32[50,128]{1,0:T(8,128)S(1)}, u32[]{:S(2)}, u32[]{:S(2)}) collective-permute-start(f32[50,128]{1,0:T(8,128)S(1)} %constant_dynamic-slice_fusion), channel_id=1, source_target_pairs={{0,8},{8,0},{1,9},{9,1},{2,10},{10,2},{3,11},{11,3},{4,12},{12,4},... | collective-permute-start | bytes 76808 | tf_op jit(solution)/shard_map/ppermute | solution.py:31
  180.8 5.7 %collective-permute-start.12 = (bf16[32,50,128]{2,1,0:T(8,128)(2,1)S(1)}, bf16[32,50,128]{2,1,0:T(8,128)(2,1)S(1)}, u32[]{:S(2)}, u32[]{:S(2)}) collective-permute-start(bf16[32,50,128]{2,1,0:T(8,128)(2,1)S(1)} %all_to_all.10), channel_id=1, source_target_pairs={{0,8},{8,0},{1,9},{9,1},{2,10},{10,2},{3,11},{11,3},{4,12},{12,4},... | collective-permute-start | bytes 1228808 | tf_op jit(solution)/shard_map/ppermute | solution.py:31

commit v9 on v8

--- a/solution.py
+++ b/solution.py
@@ -152,31 +152,70 @@
     )(core.reshape(1).astype(jnp.int32), part, twin)
 
 
-def gap_kernel(spot_ref, resid_ref, target_ref, own_ref, other_ref):
-    half, col = spot_ref[0], spot_ref[1]
-    tokens = own_ref.shape[1] // 4
-    for at, out_ref in ((half, own_ref), (1 - half, other_ref)):
-        for j in range(4):
-            start = at * 4 * tokens + lax.rem(col + 3 + j, 4) * tokens
-            cols = pl.ds(pl.multiple_of(start, 128), tokens)
-            gaps = resid_ref[:, cols].astype(jnp.float32) - target_ref[:, cols].astype(jnp.float32)
-            out_ref[:, j * tokens : (j + 1) * tokens] = gaps.astype(out_ref.dtype)
-
-
-def gap_pair(half, col, resid, target, group):
-    whole = pl.BlockSpec(memory_space=pltpu.VMEM)
-    shape = (resid.shape[0], group)
+def gap_kernel(spot_ref, resid_ref, target_ref, out_ref):
+    base, col = spot_ref[0], spot_ref[1]
+    tokens = out_ref.shape[1] // 4
+    for j in range(4):
+        cols = pl.ds(pl.multiple_of(base + lax.rem(col + 3 + j, 4) * tokens, 128), tokens)
+        gaps = resid_ref[:, cols].astype(jnp.float32) - target_ref[:, cols].astype(jnp.float32)
+        out_ref[:, j * tokens : (j + 1) * tokens] = gaps.astype(out_ref.dtype)
+
+
+def gap(base, col, resid, target, group, kind):
+    whole = pl.BlockSpec(memory_space=pltpu.VMEM)
     return pl.pallas_call(
         gap_kernel,
-        out_shape=[jax.ShapeDtypeStruct(shape, kind) for kind in (jnp.float32, jnp.bfloat16)],
+        out_shape=jax.ShapeDtypeStruct((resid.shape[0], group), kind),
         in_specs=[pl.BlockSpec(memory_space=pltpu.SMEM), whole, whole],
-        out_specs=[whole, whole],
+        out_specs=whole,
         compiler_params=pltpu.CompilerParams(vmem_limit_bytes=6 << 20),
         cost_estimate=pl.CostEstimate(
-            flops=resid.size, bytes_accessed=8 * resid.size, transcendentals=0
+            flops=resid.size, bytes_accessed=6 * resid.size, transcendentals=0
         ),
         name="gap",
-    )(jnp.stack([half, col]).astype(jnp.int32), resid, target)
+    )(jnp.stack([base, col]).astype(jnp.int32), resid, target)
+
+
+def lay_kernel(core_ref, mine_ref, twin_ref, out_ref, lines):
+    piece = mine_ref.shape[1]
+    per_row = out_ref.shape[1] // 128
+    block = 8
+    rows = block * 2 * piece // per_row
+
+    def fill(low_ref, high_ref):
+        @pl.loop(0, mine_ref.shape[0] // block)
+        def _(step):
+            for i in range(block):
+                for q, source in enumerate((low_ref, high_ref)):
+                    at = (2 * i + q) * piece
+                    lines[at : at + piece, :] = source[step * block + i].astype(jnp.float32)
+            for group in range(0, rows, 8):
+                lanes = [
+                    lines[pl.ds(group * per_row + lane, 8, stride=per_row), :] for lane in range(per_row)
+                ]
+                at = pl.ds(pl.multiple_of(step * rows + group, 8), 8)
+                out_ref[at, :] = jnp.concatenate(lanes, axis=1).astype(jnp.bfloat16)
+
+    @pl.when(core_ref[0] == 0)
+    def _():
+        fill(mine_ref, twin_ref)
+
+    @pl.when(core_ref[0] != 0)
+    def _():
+        fill(twin_ref, mine_ref)
+
+
+def lay(core, mine, twin, shape):
+    whole = pl.BlockSpec(memory_space=pltpu.VMEM)
+    return pl.pallas_call(
+        lay_kernel,
+        out_shape=jax.ShapeDtypeStruct(shape, jnp.bfloat16),
+        in_specs=[pl.BlockSpec(memory_space=pltpu.SMEM), whole, whole],
+        out_specs=whole,
+        scratch_shapes=[pltpu.VMEM((16 * mine.shape[1], 128), jnp.float32)],
+        compiler_params=pltpu.CompilerParams(vmem_limit_bytes=4 << 20),
+        name="lay",
+    )(core.reshape(1).astype(jnp.int32), mine, twin)
 
 
 def join_kernel(*refs):
@@ -229,11 +268,12 @@
 
     part = shift(pack(core, w_out, signs), "yh", 1)
 
-    own_gaps, other_gaps = gap_pair(half, col, resid, target, group)
+    other_gaps = gap((1 - half) * group, col, resid, target, group, jnp.bfloat16)
     other_gaps = shift(other_gaps, "yh", 1)
     twin = shift(part, "c", 1)
     probes = unpack_signs(signs)
     own_stack = jnp.concatenate([w_out, probes], axis=0)
+    own_gaps = gap(half * group, col, resid, target, group, jnp.float32)
     other_stack = unpack(core, part, twin, signs.shape[0])
 
     def run(stacked, gaps, block):
@@ -293,10 +333,7 @@
     spread_rows = jnp.broadcast_to(fresh[None], (32, *fresh.shape))
     mine_rows = lax.all_to_all(spread_rows, ("yl", "z"), 0, 0, tiled=True)
     twin_rows = shift(mine_rows, "c", 1)
-    both = jnp.stack(
-        [jnp.where(core == 0, mine_rows, twin_rows), jnp.where(core == 0, twin_rows, mine_rows)], axis=1
-    )
-    new_w = both.reshape(w_out.shape)
+    new_w = lay(core, mine_rows, twin_rows, w_out.shape)
     return (new_w, new_m, new_v)
 
 

time: 189 us -> 187 us (0.989)
  waiting for transfers between devices: 61.1 us -> 57.9 us
    shift_right_arithmetic x6, local copies, waits for them, and re-layouts: 0.53 us -> 4.09 us  [unpack_signs(): jnp.right_shift(signs[:, None, :], shifts[None, :, None])]
    all_to_all x1, waiting for transfers between devices: 37.8 us -> 35.2 us  [step(): terms = lax.all_to_all(pieces, ('yh', 'yl', 'z'), 0, 0, tiled=True)]
  transfers between devices with their start and end apart: 14 -> 14, of which waited for: 7 -> 7; matrix products, arithmetic and copies ran while one was open for 6% -> 8% of each run, Pallas kernels for 3% -> 3%
where the time goes in v9:
time: 187 us; the launch traced here: 186 us
  starting transfers between devices  72.6 us (39%)
  waiting for transfers between devices  57.9 us (31%)
  blocking collectives  23.7 us (13%)
  local copies, waits for them, and re-layouts  9.4 us (5%)
  Pallas kernels  8.9 us (5%)
  matrix products  8.88 us (5%)
  other arithmetic  3.71 us (2%)
    ppermute x13, starting transfers between devices, shift(): return lax.ppermute(value, axis, hops)  61.1 us
    all_to_all x1, waiting for transfers between devices, step(): terms = lax.all_to_all(pieces, ('yh', 'yl', 'z'), 0, 0, tiled=True)  35.2 us
    all_to_all x1, blocking collectives, step(): mine_rows = lax.all_to_all(spread_rows, ('yl', 'z'), 0, 0, tiled=True)  23.7 us
    ppermute x13, waiting for transfers between devices, shift(): return lax.ppermute(value, axis, hops)  22.7 us
    all_to_all x1, starting transfers between devices, step(): terms = lax.all_to_all(pieces, ('yh', 'yl', 'z'), 0, 0, tiled=True)  11.5 us
    dot_general x8, matrix products, run(): jnp.dot(terms, block, preferred_element_type=jnp.float32)  4.73 us
    dot_general x4, matrix products, run(): lax.dot_general(stacked, block, (((1,), (1,)), ((), ())), preferred_eleme...  4.15 us
    shift_right_arithmetic x6, local copies, waits for them, and re-layouts, unpack_signs(): jnp.right_shift(signs[:, None, :], shifts[None, :, None])  4.09 us
  transfers between devices with their start and end apart: 14, of which 7 were waited for; matrix products, arithmetic and copies ran while one was open for 8% of the time, Pallas kernels for 3%

profile of v9, /device:TPU:1, one launch (start us, length us, event | category | flops | bytes accessed | tf_op | source)
XLA Modules:
  0.0 186.2 jit_solution(5928025728902544412)
XLA Ops:
  0.7 2.6 %fusion.34 = (bf16[128,2560]{1,0:T(8,128)(2,1)}, bf16[128,2560]{1,0:T(8,128)(2,1)}) fusion(bf16[256,2560]{1,0:T(8,128)(2,1)} %refs_2_.1), kind=kLoop, calls=%fused_computation.60 | loop fusion | bytes 2621440 | tf_op jit(solution)/shard_map/slice | solution.py:261
  3.3 3.9 %collective-permute-start = (bf16[128,2560]{1,0:T(8,128)(2,1)}, bf16[128,2560]{1,0:T(8,128)(2,1)}, u32[]{:S(2)}, u32[]{:S(2)}) collective-permute-start(bf16[128,2560]{1,0:T(8,128)(2,1)} %get-tuple-element.53), channel_id=1, source_target_pairs={{0,1},{1,2},{2,3},{3,0},{4,5},{5,6},{6,7},{7,4},{8,9},{9,10},{10,1... | collective-permute-start | bytes 1966088 | tf_op jit(solution)/shard_map/ppermute | solution.py:31
  7.2 3.2 %collective-permute-start.3 = (bf16[128,2560]{1,0:T(8,128)(2,1)}, bf16[128,2560]{1,0:T(8,128)(2,1)}, u32[]{:S(2)}, u32[]{:S(2)}) collective-permute-start(bf16[128,2560]{1,0:T(8,128)(2,1)} %get-tuple-element.52), channel_id=1, source_target_pairs={{0,3},{1,0},{2,1},{3,2},{4,7},{5,4},{6,5},{7,6},{8,11},{9,8},{10,9... | collective-permute-start | bytes 1966088 | tf_op jit(solution)/shard_map/ppermute | solution.py:31
  10.4 2.1 %collective-permute-start.1 = (bf16[128,2560]{1,0:T(8,128)(2,1)}, bf16[128,2560]{1,0:T(8,128)(2,1)}, u32[]{:S(2)}, u32[]{:S(2)}) collective-permute-start(bf16[128,2560]{1,0:T(8,128)(2,1)} %get-tuple-element.52), channel_id=1, source_target_pairs={{0,1},{1,2},{2,3},{3,0},{4,5},{5,6},{6,7},{7,4},{8,9},{9,10},{10,1... | collective-permute-start | bytes 1966088 | tf_op jit(solution)/shard_map/ppermute | solution.py:31
  12.5 4.4 %collective-permute-start.2 = (bf16[128,2560]{1,0:T(8,128)(2,1)}, bf16[128,2560]{1,0:T(8,128)(2,1)}, u32[]{:S(2)}, u32[]{:S(2)}) collective-permute-start(bf16[128,2560]{1,0:T(8,128)(2,1)} %get-tuple-element.53), channel_id=1, source_target_pairs={{0,3},{1,0},{2,1},{3,2},{4,7},{5,4},{6,5},{7,6},{8,11},{9,8},{10,9... | collective-permute-start | bytes 1966088 | tf_op jit(solution)/shard_map/ppermute | solution.py:31
  16.9 0.8 pack.1
  17.8 7.6 %collective-permute-start.4 = (bf16[90,2560]{1,0:T(8,128)(2,1)}, bf16[90,2560]{1,0:T(8,128)(2,1)}, u32[]{:S(2)}, u32[]{:S(2)}) collective-permute-start(bf16[90,2560]{1,0:T(8,128)(2,1)} %pack.1), channel_id=1, source_target_pairs={{0,4},{4,0},{1,5},{5,1},{2,6},{6,2},{3,7},{7,3},{8,12},{12,8},{9,1... | collective-permute-start | bytes 1382408 | tf_op jit(solution)/shard_map/ppermute | solution.py:31
  25.4 0.1 pad_add_fusion.1.spot_ref
  25.5 0.1 pad_add_fusion.spot_ref
  25.6 0.6 gap.3
  26.2 0.7 copy-done.7
  26.9 0.6 gap.2
  27.6 0.8 copy-done.4
  28.4 0.1 shift_right_arithmetic.45
  28.5 0.4 fusion.3
  28.9 9.6 %collective-permute-done.4.part_ref = bf16[90,2560]{1,0:T(8,128)(2,1)} collective-permute-done((bf16[90,2560]{1,0:T(8,128)(2,1)}, bf16[90,2560]{1,0:T(8,128)(2,1)}, u32[]{:S(2)}, u32[]{:S(2)}) %collective-permute-start.4) | collective-permute-done | bytes 460832 | tf_op jit(solution)/shard_map/ppermute | solution.py:31
  38.4 8.4 %collective-permute-start.6 = (bf16[160,1024]{1,0:T(8,128)(2,1)}, bf16[160,1024]{1,0:T(8,128)(2,1)S(1)}, u32[]{:S(2)}, u32[]{:S(2)}) collective-permute-start(bf16[160,1024]{1,0:T(8,128)(2,1)} %copy-done.7), channel_id=1, source_target_pairs={{0,4},{4,0},{1,5},{5,1},{2,6},{6,2},{3,7},{7,3},{8,12},{12,8},{9,1... | collective-permute-start | bytes 983048 | tf_op jit(solution)/shard_map/ppermute | solution.py:31
  46.8 11.1 %collective-permute-start.5 = (bf16[90,2560]{1,0:T(8,128)(2,1)}, bf16[90,2560]{1,0:T(8,128)(2,1)S(1)}, u32[]{:S(2)}, u32[]{:S(2)}) collective-permute-start(bf16[90,2560]{1,0:T(8,128)(2,1)} %collective-permute-done.4.part_ref), channel_id=1, source_target_pairs={{0,8},{8,0},{1,9},{9,1},{2,10},{10,2},{3,11},{11,3},{4,12},{12,4},... | collective-permute-start | bytes 1382408 | tf_op jit(solution)/shard_map/ppermute | solution.py:31
  57.9 1.7 join.2
  59.7 1.5 fusion.5
  61.2 0.3 broadcast_select_fusion.2
  61.6 0.8 fusion.36.refs_0_
  62.4 1.9 %collective-permute-start.7 = (bf16[128,2560]{1,0:T(8,128)(2,1)}, bf16[128,2560]{1,0:T(8,128)(2,1)S(1)}, u32[]{:S(2)}, u32[]{:S(2)}) collective-permute-start(bf16[128,2560]{1,0:T(8,128)(2,1)} %collective-permute-done.refs_0_), channel_id=1, source_target_pairs={{0,1},{1,2},{2,3},{3,0},{4,5},{5,6},{6,7},{7,4},{8,9},{9,10},{10,1... | collective-permute-start | bytes 1966088 | tf_op jit(solution)/shard_map/ppermute | solution.py:31
  64.3 4.6 %collective-permute-start.8 = (bf16[128,2560]{1,0:T(8,128)(2,1)}, bf16[128,2560]{1,0:T(8,128)(2,1)S(1)}, u32[]{:S(2)}, u32[]{:S(2)}) collective-permute-start(bf16[128,2560]{1,0:T(8,128)(2,1)} %collective-permute-done.3.refs_4_), channel_id=1, source_target_pairs={{0,3},{1,0},{2,1},{3,2},{4,7},{5,4},{6,5},{7,6},{8,11},{9,8},{10,9... | collective-permute-start | bytes 1966088 | tf_op jit(solution)/shard_map/ppermute | solution.py:31
  68.9 0.8 fusion.35
  69.7 1.6 unpack.1
  71.3 1.5 fusion.37
  72.8 0.4 broadcast_select_fusion
  73.2 0.8 fusion.39.refs_3_
  74.0 0.8 fusion.38
  74.8 7.2 %collective-permute-done.7.refs_0_ = bf16[128,2560]{1,0:T(8,128)(2,1)S(1)} collective-permute-done((bf16[128,2560]{1,0:T(8,128)(2,1)}, bf16[128,2560]{1,0:T(8,128)(2,1)S(1)}, u32[]{:S(2)}, u32[]{:S(2)}) %collective-permute-start.7) | collective-permute-done | bytes 655392 | tf_op jit(solution)/shard_map/ppermute | solution.py:31
  82.0 1.0 collective-permute-done.8.refs_1_
  83.0 0.4 join.3
  83.4 0.6 fusion.4
  84.0 0.6 fusion.42
  84.7 0.1 broadcast_select_fusion.6
  84.8 0.1 broadcast_select_fusion.4
  85.0 0.4 fusion.44
  85.3 0.2 add.67
  85.5 3.1 %collective-permute-start.10 = (f32[160,2560]{1,0:T(8,128)S(1)}, f32[160,2560]{1,0:T(8,128)S(1)}, u32[]{:S(2)}, u32[]{:S(2)}) collective-permute-start(f32[160,2560]{1,0:T(8,128)S(1)} %add.67), channel_id=1, source_target_pairs={{0,8},{8,0},{1,9},{9,1},{2,10},{10,2},{3,11},{11,3},{4,12},{12,4},... | collective-permute-start | bytes 4915208 | tf_op jit(solution)/shard_map/ppermute | solution.py:31
  88.6 0.4 fusion.41
  89.0 0.2 add.64
  89.1 1.9 %collective-permute-start.9 = (f32[160,2560]{1,0:T(8,128)S(1)}, f32[160,2560]{1,0:T(8,128)S(1)}, u32[]{:S(2)}, u32[]{:S(2)}) collective-permute-start(f32[160,2560]{1,0:T(8,128)S(1)} %add.64), channel_id=1, source_target_pairs={{0,8},{8,0},{1,9},{9,1},{2,10},{10,2},{3,11},{11,3},{4,12},{12,4},... | collective-permute-start | bytes 4915208 | tf_op jit(solution)/shard_map/ppermute | solution.py:31
  91.1 0.4 fusion.43.refs_4_
  91.5 0.4 fusion.40.refs_1_
  91.9 2.7 %collective-permute-done.9.refs_2_ = f32[160,2560]{1,0:T(8,128)S(1)} collective-permute-done((f32[160,2560]{1,0:T(8,128)S(1)}, f32[160,2560]{1,0:T(8,128)S(1)}, u32[]{:S(2)}, u32[]{:S(2)}) %collective-permute-start.9) | collective-permute-done | bytes 1638432 | tf_op jit(solution)/shard_map/ppermute | solution.py:31
  94.5 2.0 %cut.1 = bf16[64,100,128]{2,1,0:T(8,128)(2,1)} custom-call(s32[1]{0:T(128)} %bitcast.1.half_ref, f32[160,2560]{1,0:T(8,128)S(1)} %fusion.36.refs_0_, f32[160,2560]{1,0:T(8,128)S(1)} %fusion.40.refs_1_, f32[160,2560]{1,0:T(8,128)S(1)} %collective-permute-done.9.refs_2_, f32[160,2560]{1,0:T(8,128)S(1)} %fusion.39.refs_3_, f32[160,2560]{1,0:T(8,128)S(1)} %fusion.43.refs_4_, ...), custom_call_target="tpu_custom_call" | custom-call | flops 1638400 | bytes 11468800 | tf_op jit(solution)/shard_map/cut/pallas_call | solution.py:71
  96.5 11.5 %all-to-all-start = ((bf16[64,100,128]{2,1,0:T(8,128)(2,1)}), bf16[64,100,128]{2,1,0:T(8,128)(2,1)S(1)}, u32[]{:S(2)}, u32[]{:S(2)}) async-start(bf16[64,100,128]{2,1,0:T(8,128)(2,1)} %cut.1), calls=%async_computation | async-start | bytes 3407872 | tf_op jit(solution)/shard_map/all_to_all | solution.py:313
  108.0 1.0 reshape.28
  109.0 0.1 shift_right_arithmetic.49
  109.1 0.1 shift_right_arithmetic.50
  109.2 1.3 shift_right_arithmetic.42
  110.6 2.5 %shift_right_arithmetic.48 = s32[3200,128]{1,0:T(8,128)} reshape(s32[5,32,2560]{2,1,0:T(8,128)} %shift_right_arithmetic.42) | data formatting | bytes 3276800 | tf_op jit(solution)/shard_map/shift_right_arithmetic | solution.py:36
  113.1 0.1 dynamic-slice
  113.1 0.8 fusion.22
  114.0 35.2 %all-to-all-done = bf16[64,100,128]{2,1,0:T(8,128)(2,1)S(1)} async-done(((bf16[64,100,128]{2,1,0:T(8,128)(2,1)}), bf16[64,100,128]{2,1,0:T(8,128)(2,1)S(1)}, u32[]{:S(2)}, u32[]{:S(2)}) %all-to-all-start) | async-done | bytes 1638432 | tf_op jit(solution)/shard_map/all_to_all | solution.py:313
  149.2 0.3 convert_reduce_fusion
  149.5 4.7 %collective-permute-start.11 = (f32[50,128]{1,0:T(8,128)S(1)}, f32[50,128]{1,0:T(8,128)S(1)}, u32[]{:S(2)}, u32[]{:S(2)}) collective-permute-start(f32[50,128]{1,0:T(8,128)S(1)} %constant_dynamic-slice_fusion), channel_id=1, source_target_pairs={{0,8},{8,0},{1,9},{9,1},{2,10},{10,2},{3,11},{11,3},{4,12},{12,4},... | collective-permute-start | bytes 76808 | tf_op jit(solution)/shard_map/ppermute | solution.py:31
  154.2 0.8 collective-permute-done.11
  155.0 0.6 subtract_convert_fusion
  155.7 23.7 %all_to_all.10.mine_ref = bf16[32,50,128]{2,1,0:T(8,128)(2,1)S(1)} all-to-all(bf16[32,50,128]{2,1,0:T(8,128)(2,1)S(1)} %broadcast_in_dim.2), channel_id=1, replica_groups=mesh['yl'=4,'z'=8,'c'=2,'yh'=2,'x'=4] {'yl','z'}, dimensions={0} | all-to-all | bytes 819200 | tf_op jit(solution)/shard_map/all_to_all | solution.py:334
  179.4 4.3 %collective-permute-start.12 = (bf16[32,50,128]{2,1,0:T(8,128)(2,1)S(1)}, bf16[32,50,128]{2,1,0:T(8,128)(2,1)S(1)}, u32[]{:S(2)}, u32[]{:S(2)}) collective-permute-start(bf16[32,50,128]{2,1,0:T(8,128)(2,1)S(1)} %all_to_all.10.mine_ref), channel_id=1, source_target_pairs={{0,8},{8,0},{1,9},{9,1},{2,10},{10,2},{3,11},{11,3},{4,12},{12,4},... | collective-permute-start | bytes 1228808 | tf_op jit(solution)/shard_map/ppermute | solution.py:31
  183.7 1.4 collective-permute-done.12.twin_ref
  185.1 1.1 lay.1
  (32 shorter events, 0.2 us)
Async XLA Ops:
  0.6 16.3 %copy-start.1 = (bf16[160,2560]{1,0:T(8,128)(2,1)S(1)}, bf16[160,2560]{1,0:T(8,128)(2,1)}, u32[]{:S(2)}) copy-start(bf16[160,2560]{1,0:T(8,128)(2,1)} %weights_ref.1) | copy-start | bytes 2457604
  0.6 16.3 %copy-start.6 = (s32[5,2560]{1,0:T(8,128)S(1)}, s32[5,2560]{1,0:T(8,128)}, u32[]{:S(2)}) copy-start(s32[5,2560]{1,0:T(8,128)} %signs_ref.1) | copy-start | bytes 153604
  0.7 24.9 %copy-start.2 = (bf16[160,2048]{1,0:T(8,128)(2,1)S(1)}, bf16[160,2048]{1,0:T(8,128)(2,1)}, u32[]{:S(2)}) copy-start(bf16[160,2048]{1,0:T(8,128)(2,1)} %resid_ref.3) | copy-start | bytes 1966084
  0.7 24.9 %copy-start.3 = (bf16[160,2048]{1,0:T(8,128)(2,1)S(1)}, bf16[160,2048]{1,0:T(8,128)(2,1)}, u32[]{:S(2)}) copy-start(bf16[160,2048]{1,0:T(8,128)(2,1)} %target_ref.3) | copy-start | bytes 1966084
  3.3 43.5 %collective-permute-start = (bf16[128,2560]{1,0:T(8,128)(2,1)}, bf16[128,2560]{1,0:T(8,128)(2,1)}, u32[]{:S(2)}, u32[]{:S(2)}) collective-permute-start(bf16[128,2560]{1,0:T(8,128)(2,1)} %get-tuple-element.53), channel_id=1, source_target_pairs={{0,1},{1,2},{2,3},{3,0},{4,5},{5,6},{6,7},{7,4},{8,9},{9,10},{10,1... | collective-permute-start | bytes 1966088 | tf_op jit(solution)/shard_map/ppermute | solution.py:31
  7.2 50.7 %collective-permute-start.3 = (bf16[128,2560]{1,0:T(8,128)(2,1)}, bf16[128,2560]{1,0:T(8,128)(2,1)}, u32[]{:S(2)}, u32[]{:S(2)}) collective-permute-start(bf16[128,2560]{1,0:T(8,128)(2,1)} %get-tuple-element.52), channel_id=1, source_target_pairs={{0,3},{1,0},{2,1},{3,2},{4,7},{5,4},{6,5},{7,6},{8,11},{9,8},{10,9... | collective-permute-start | bytes 1966088 | tf_op jit(solution)/shard_map/ppermute | solution.py:31
  10.4 47.5 %collective-permute-start.1 = (bf16[128,2560]{1,0:T(8,128)(2,1)}, bf16[128,2560]{1,0:T(8,128)(2,1)}, u32[]{:S(2)}, u32[]{:S(2)}) collective-permute-start(bf16[128,2560]{1,0:T(8,128)(2,1)} %get-tuple-element.52), channel_id=1, source_target_pairs={{0,1},{1,2},{2,3},{3,0},{4,5},{5,6},{6,7},{7,4},{8,9},{9,10},{10,1... | collective-permute-start | bytes 1966088 | tf_op jit(solution)/shard_map/ppermute | solution.py:31
  12.5 45.4 %collective-permute-start.2 = (bf16[128,2560]{1,0:T(8,128)(2,1)}, bf16[128,2560]{1,0:T(8,128)(2,1)}, u32[]{:S(2)}, u32[]{:S(2)}) collective-permute-start(bf16[128,2560]{1,0:T(8,128)(2,1)} %get-tuple-element.53), channel_id=1, source_target_pairs={{0,3},{1,0},{2,1},{3,2},{4,7},{5,4},{6,5},{7,6},{8,11},{9,8},{10,9... | collective-permute-start | bytes 1966088 | tf_op jit(solution)/shard_map/ppermute | solution.py:31
  17.8 20.7 %collective-permute-start.4 = (bf16[90,2560]{1,0:T(8,128)(2,1)}, bf16[90,2560]{1,0:T(8,128)(2,1)}, u32[]{:S(2)}, u32[]{:S(2)}) collective-permute-start(bf16[90,2560]{1,0:T(8,128)(2,1)} %pack.1), channel_id=1, source_target_pairs={{0,4},{4,0},{1,5},{5,1},{2,6},{6,2},{3,7},{7,3},{8,12},{12,8},{9,1... | collective-permute-start | bytes 1382408 | tf_op jit(solution)/shard_map/ppermute | solution.py:31
  26.2 0.7 copy-start.7
  26.9 31.0 %copy-start = (bf16[256,2560]{1,0:T(8,128)(2,1)S(1)}, bf16[256,2560]{1,0:T(8,128)(2,1)}, u32[]{:S(2)}) copy-start(bf16[256,2560]{1,0:T(8,128)(2,1)} %refs_2_.1) | copy-start | bytes 3932164
  27.6 0.8 copy-start.4
  38.4 34.3 %collective-permute-start.6 = (bf16[160,1024]{1,0:T(8,128)(2,1)}, bf16[160,1024]{1,0:T(8,128)(2,1)S(1)}, u32[]{:S(2)}, u32[]{:S(2)}) collective-permute-start(bf16[160,1024]{1,0:T(8,128)(2,1)} %copy-done.7), channel_id=1, source_target_pairs={{0,4},{4,0},{1,5},{5,1},{2,6},{6,2},{3,7},{7,3},{8,12},{12,8},{9,1... | collective-permute-start | bytes 983048 | tf_op jit(solution)/shard_map/ppermute | solution.py:31
  46.8 22.9 %collective-permute-start.5 = (bf16[90,2560]{1,0:T(8,128)(2,1)}, bf16[90,2560]{1,0:T(8,128)(2,1)S(1)}, u32[]{:S(2)}, u32[]{:S(2)}) collective-permute-start(bf16[90,2560]{1,0:T(8,128)(2,1)} %collective-permute-done.4.part_ref), channel_id=1, source_target_pairs={{0,8},{8,0},{1,9},{9,1},{2,10},{10,2},{3,11},{11,3},{4,12},{12,4},... | collective-permute-start | bytes 1382408 | tf_op jit(solution)/shard_map/ppermute | solution.py:31
  59.7 1.5 copy-start.5
  62.4 19.6 %collective-permute-start.7 = (bf16[128,2560]{1,0:T(8,128)(2,1)}, bf16[128,2560]{1,0:T(8,128)(2,1)S(1)}, u32[]{:S(2)}, u32[]{:S(2)}) collective-permute-start(bf16[128,2560]{1,0:T(8,128)(2,1)} %collective-permute-done.refs_0_), channel_id=1, source_target_pairs={{0,1},{1,2},{2,3},{3,0},{4,5},{5,6},{6,7},{7,4},{8,9},{9,10},{10,1... | collective-permute-start | bytes 1966088 | tf_op jit(solution)/shard_map/ppermute | solution.py:31
  64.3 18.7 %collective-permute-start.8 = (bf16[128,2560]{1,0:T(8,128)(2,1)}, bf16[128,2560]{1,0:T(8,128)(2,1)S(1)}, u32[]{:S(2)}, u32[]{:S(2)}) collective-permute-start(bf16[128,2560]{1,0:T(8,128)(2,1)} %collective-permute-done.3.refs_4_), channel_id=1, source_target_pairs={{0,3},{1,0},{2,1},{3,2},{4,7},{5,4},{6,5},{7,6},{8,11},{9,8},{10,9... | collective-permute-start | bytes 1966088 | tf_op jit(solution)/shard_map/ppermute | solution.py:31
  85.5 6.3 %collective-permute-start.10 = (f32[160,2560]{1,0:T(8,128)S(1)}, f32[160,2560]{1,0:T(8,128)S(1)}, u32[]{:S(2)}, u32[]{:S(2)}) collective-permute-start(f32[160,2560]{1,0:T(8,128)S(1)} %add.67), channel_id=1, source_target_pairs={{0,8},{8,0},{1,9},{9,1},{2,10},{10,2},{3,11},{11,3},{4,12},{12,4},... | collective-permute-start | bytes 4915208 | tf_op jit(solution)/shard_map/ppermute | solution.py:31
  89.1 5.4 %collective-permute-start.9 = (f32[160,2560]{1,0:T(8,128)S(1)}, f32[160,2560]{1,0:T(8,128)S(1)}, u32[]{:S(2)}, u32[]{:S(2)}) collective-permute-start(f32[160,2560]{1,0:T(8,128)S(1)} %add.64), channel_id=1, source_target_pairs={{0,8},{8,0},{1,9},{9,1},{2,10},{10,2},{3,11},{11,3},{4,12},{12,4},... | collective-permute-start | bytes 4915208 | tf_op jit(solution)/shard_map/ppermute | solution.py:31
  96.5 52.6 %all-to-all-start = ((bf16[64,100,128]{2,1,0:T(8,128)(2,1)}), bf16[64,100,128]{2,1,0:T(8,128)(2,1)S(1)}, u32[]{:S(2)}, u32[]{:S(2)}) async-start(bf16[64,100,128]{2,1,0:T(8,128)(2,1)} %cut.1), calls=%async_computation | async-start | bytes 3407872 | tf_op jit(solution)/shard_map/all_to_all | solution.py:313
  113.1 42.0 %copy-start.8 = (f32[50,128]{1,0:T(8,128)S(1)}, f32[50,128]{1,0:T(8,128)}, u32[]{:S(2)}) copy-start(f32[50,128]{1,0:T(8,128)} %param.12) | copy-start | bytes 76804
  113.1 42.0 %copy-start.9 = (f32[50,128]{1,0:T(8,128)S(1)}, f32[50,128]{1,0:T(8,128)}, u32[]{:S(2)}) copy-start(f32[50,128]{1,0:T(8,128)} %param.13) | copy-start | bytes 76804
  149.5 5.5 %collective-permute-start.11 = (f32[50,128]{1,0:T(8,128)S(1)}, f32[50,128]{1,0:T(8,128)S(1)}, u32[]{:S(2)}, u32[]{:S(2)}) collective-permute-start(f32[50,128]{1,0:T(8,128)S(1)} %constant_dynamic-slice_fusion), channel_id=1, source_target_pairs={{0,8},{8,0},{1,9},{9,1},{2,10},{10,2},{3,11},{11,3},{4,12},{12,4},... | collective-permute-start | bytes 76808 | tf_op jit(solution)/shard_map/ppermute | solution.py:31
  179.4 5.7 %collective-permute-start.12 = (bf16[32,50,128]{2,1,0:T(8,128)(2,1)S(1)}, bf16[32,50,128]{2,1,0:T(8,128)(2,1)S(1)}, u32[]{:S(2)}, u32[]{:S(2)}) collective-permute-start(bf16[32,50,128]{2,1,0:T(8,128)(2,1)S(1)} %all_to_all.10.mine_ref), channel_id=1, source_target_pairs={{0,8},{8,0},{1,9},{9,1},{2,10},{10,2},{3,11},{11,3},{4,12},{12,4},... | collective-permute-start | bytes 1228808 | tf_op jit(solution)/shard_map/ppermute | solution.py:31

commit v10 on v9

--- a/solution.py
+++ b/solution.py
@@ -152,28 +152,31 @@
     )(core.reshape(1).astype(jnp.int32), part, twin)
 
 
-def gap_kernel(spot_ref, resid_ref, target_ref, out_ref):
-    base, col = spot_ref[0], spot_ref[1]
-    tokens = out_ref.shape[1] // 4
-    for j in range(4):
-        cols = pl.ds(pl.multiple_of(base + lax.rem(col + 3 + j, 4) * tokens, 128), tokens)
-        gaps = resid_ref[:, cols].astype(jnp.float32) - target_ref[:, cols].astype(jnp.float32)
-        out_ref[:, j * tokens : (j + 1) * tokens] = gaps.astype(out_ref.dtype)
-
-
-def gap(base, col, resid, target, group, kind):
-    whole = pl.BlockSpec(memory_space=pltpu.VMEM)
+def gap_kernel(spot_ref, resid_ref, target_ref, own_ref, other_ref):
+    half, col = spot_ref[0], spot_ref[1]
+    tokens = own_ref.shape[1] // 4
+    for at, out_ref in ((half, own_ref), (1 - half, other_ref)):
+        for j in range(4):
+            start = at * 4 * tokens + lax.rem(col + 3 + j, 4) * tokens
+            cols = pl.ds(pl.multiple_of(start, 128), tokens)
+            gaps = resid_ref[:, cols].astype(jnp.float32) - target_ref[:, cols].astype(jnp.float32)
+            out_ref[:, j * tokens : (j + 1) * tokens] = gaps.astype(out_ref.dtype)
+
+
+def gap_pair(half, col, resid, target, group):
+    whole = pl.BlockSpec(memory_space=pltpu.VMEM)
+    shape = (resid.shape[0], group)
     return pl.pallas_call(
         gap_kernel,
-        out_shape=jax.ShapeDtypeStruct((resid.shape[0], group), kind),
+        out_shape=[jax.ShapeDtypeStruct(shape, kind) for kind in (jnp.float32, jnp.bfloat16)],
         in_specs=[pl.BlockSpec(memory_space=pltpu.SMEM), whole, whole],
-        out_specs=whole,
+        out_specs=[whole, whole],
         compiler_params=pltpu.CompilerParams(vmem_limit_bytes=6 << 20),
         cost_estimate=pl.CostEstimate(
-            flops=resid.size, bytes_accessed=6 * resid.size, transcendentals=0
+            flops=resid.size, bytes_accessed=8 * resid.size, transcendentals=0
         ),
         name="gap",
-    )(jnp.stack([base, col]).astype(jnp.int32), resid, target)
+    )(jnp.stack([half, col]).astype(jnp.int32), resid, target)
 
 
 def lay_kernel(core_ref, mine_ref, twin_ref, out_ref, lines):
@@ -258,7 +261,9 @@
     col = lax.axis_index("x")
 
     cutoff = tokens // 2
-    top, low = hidden[:cutoff], hidden[cutoff:]
+    top = hidden[:cutoff]
+    later, _ = lax.optimization_barrier((hidden, top))
+    low = later[cutoff:]
     left_top = shift(top, "x", 1)
     right_low = shift(low, "x", -1)
     left_low = shift(low, "x", 1)
@@ -268,12 +273,11 @@
 
     part = shift(pack(core, w_out, signs), "yh", 1)
 
-    other_gaps = gap((1 - half) * group, col, resid, target, group, jnp.bfloat16)
+    own_gaps, other_gaps = gap_pair(half, col, resid, target, group)
     other_gaps = shift(other_gaps, "yh", 1)
     twin = shift(part, "c", 1)
     probes = unpack_signs(signs)
     own_stack = jnp.concatenate([w_out, probes], axis=0)
-    own_gaps = gap(half * group, col, resid, target, group, jnp.float32)
     other_stack = unpack(core, part, twin, signs.shape[0])
 
     def run(stacked, gaps, block):

time: 187 us -> 191 us (1.021)
  waiting for transfers between devices: 57.9 us -> 64.4 us
    ppermute x13, waiting for transfers between devices: 22.7 us -> 26.6 us  [shift(): return lax.ppermute(value, axis, hops)]
    shift_right_arithmetic x6, local copies, waits for them, and re-layouts: 4.09 us -> 0.53 us  [unpack_signs(): jnp.right_shift(signs[:, None, :], shifts[None, :, None])]
    all_to_all x1, waiting for transfers between devices: 35.2 us -> 37.8 us  [step(): terms = lax.all_to_all(pieces, ('yh', 'yl', 'z'), 0, 0, tiled=True)]
  transfers between devices with their start and end apart: 14 -> 14, of which waited for: 7 -> 7; matrix products, arithmetic and copies ran while one was open for 8% -> 6% of each run, Pallas kernels for 3% -> 3%
where the time goes in v10:
time: 191 us; the launch traced here: 190 us
  starting transfers between devices  71.4 us (37%)
  waiting for transfers between devices  64.4 us (34%)
  blocking collectives  23.6 us (12%)
  matrix products  8.91 us (5%)
  Pallas kernels  8.29 us (4%)
  local copies, waits for them, and re-layouts  7.89 us (4%)
  other arithmetic  4.32 us (2%)
    ppermute x13, starting transfers between devices, shift(): return lax.ppermute(value, axis, hops)  59.9 us
    all_to_all x1, waiting for transfers between devices, step(): terms = lax.all_to_all(pieces, ('yh', 'yl', 'z'), 0, 0, tiled=True)  37.8 us
    ppermute x13, waiting for transfers between devices, shift(): return lax.ppermute(value, axis, hops)  26.6 us
    all_to_all x1, blocking collectives, step(): mine_rows = lax.all_to_all(spread_rows, ('yl', 'z'), 0, 0, tiled=True)  23.6 us
    all_to_all x1, starting transfers between devices, step(): terms = lax.all_to_all(pieces, ('yh', 'yl', 'z'), 0, 0, tiled=True)  11.5 us
    dot_general x8, matrix products, run(): jnp.dot(terms, block, preferred_element_type=jnp.float32)  4.74 us
    dot_general x4, matrix products, run(): lax.dot_general(stacked, block, (((1,), (1,)), ((), ())), preferred_eleme...  4.17 us
  transfers between devices with their start and end apart: 14, of which 7 were waited for; matrix products, arithmetic and copies ran while one was open for 6% of the time, Pallas kernels for 3%

profile of v10, /device:TPU:1, one launch (start us, length us, event | category | flops | bytes accessed | tf_op | source)
XLA Modules:
  0.0 190.0 jit_solution(6087852469256401492)
XLA Ops:
  0.7 2.1 %slice.42 = bf16[128,2560]{1,0:T(8,128)(2,1)} slice(bf16[256,2560]{1,0:T(8,128)(2,1)} %refs_2_.1), slice={[0:128], [0:2560]} | slice | bytes 1310720 | tf_op jit(solution)/shard_map/slice | solution.py:264
  2.8 0.9 slice.43
  3.7 5.2 %collective-permute-start.3 = (bf16[128,2560]{1,0:T(8,128)(2,1)}, bf16[128,2560]{1,0:T(8,128)(2,1)}, u32[]{:S(2)}, u32[]{:S(2)}) collective-permute-start(bf16[128,2560]{1,0:T(8,128)(2,1)} %slice.43), channel_id=1, source_target_pairs={{0,3},{1,0},{2,1},{3,2},{4,7},{5,4},{6,5},{7,6},{8,11},{9,8},{10,9... | collective-permute-start | bytes 1966088 | tf_op jit(solution)/shard_map/ppermute | solution.py:31
  8.9 1.9 %collective-permute-start.1 = (bf16[128,2560]{1,0:T(8,128)(2,1)}, bf16[128,2560]{1,0:T(8,128)(2,1)}, u32[]{:S(2)}, u32[]{:S(2)}) collective-permute-start(bf16[128,2560]{1,0:T(8,128)(2,1)} %slice.43), channel_id=1, source_target_pairs={{0,1},{1,2},{2,3},{3,0},{4,5},{5,6},{6,7},{7,4},{8,9},{9,10},{10,1... | collective-permute-start | bytes 1966088 | tf_op jit(solution)/shard_map/ppermute | solution.py:31
  10.8 2.1 %collective-permute-start = (bf16[128,2560]{1,0:T(8,128)(2,1)}, bf16[128,2560]{1,0:T(8,128)(2,1)}, u32[]{:S(2)}, u32[]{:S(2)}) collective-permute-start(bf16[128,2560]{1,0:T(8,128)(2,1)} %slice.42), channel_id=1, source_target_pairs={{0,1},{1,2},{2,3},{3,0},{4,5},{5,6},{6,7},{7,4},{8,9},{9,10},{10,1... | collective-permute-start | bytes 1966088 | tf_op jit(solution)/shard_map/ppermute | solution.py:31
  12.9 4.4 %collective-permute-start.2 = (bf16[128,2560]{1,0:T(8,128)(2,1)}, bf16[128,2560]{1,0:T(8,128)(2,1)}, u32[]{:S(2)}, u32[]{:S(2)}) collective-permute-start(bf16[128,2560]{1,0:T(8,128)(2,1)} %slice.42), channel_id=1, source_target_pairs={{0,3},{1,0},{2,1},{3,2},{4,7},{5,4},{6,5},{7,6},{8,11},{9,8},{10,9... | collective-permute-start | bytes 1966088 | tf_op jit(solution)/shard_map/ppermute | solution.py:31
  17.4 0.8 pack.1
  18.2 7.4 %collective-permute-start.4 = (bf16[90,2560]{1,0:T(8,128)(2,1)}, bf16[90,2560]{1,0:T(8,128)(2,1)}, u32[]{:S(2)}, u32[]{:S(2)}) collective-permute-start(bf16[90,2560]{1,0:T(8,128)(2,1)} %pack.1), channel_id=1, source_target_pairs={{0,4},{4,0},{1,5},{5,1},{2,6},{6,2},{3,7},{7,3},{8,12},{12,8},{9,1... | collective-permute-start | bytes 1382408 | tf_op jit(solution)/shard_map/ppermute | solution.py:31
  25.6 0.1 pad_add_fusion.spot_ref
  25.7 0.7 gap.1
  26.5 0.8 copy-done.5
  27.3 0.7 copy-done.7
  28.0 0.1 shift_right_arithmetic.45
  28.1 0.4 fusion.3
  28.5 10.2 %collective-permute-done.4.part_ref = bf16[90,2560]{1,0:T(8,128)(2,1)} collective-permute-done((bf16[90,2560]{1,0:T(8,128)(2,1)}, bf16[90,2560]{1,0:T(8,128)(2,1)}, u32[]{:S(2)}, u32[]{:S(2)}) %collective-permute-start.4) | collective-permute-done | bytes 460832 | tf_op jit(solution)/shard_map/ppermute | solution.py:31
  38.7 8.0 %collective-permute-start.6 = (bf16[160,1024]{1,0:T(8,128)(2,1)}, bf16[160,1024]{1,0:T(8,128)(2,1)S(1)}, u32[]{:S(2)}, u32[]{:S(2)}) collective-permute-start(bf16[160,1024]{1,0:T(8,128)(2,1)} %copy-done.7), channel_id=1, source_target_pairs={{0,4},{4,0},{1,5},{5,1},{2,6},{6,2},{3,7},{7,3},{8,12},{12,8},{9,1... | collective-permute-start | bytes 983048 | tf_op jit(solution)/shard_map/ppermute | solution.py:31
  46.7 11.5 %collective-permute-start.5 = (bf16[90,2560]{1,0:T(8,128)(2,1)}, bf16[90,2560]{1,0:T(8,128)(2,1)S(1)}, u32[]{:S(2)}, u32[]{:S(2)}) collective-permute-start(bf16[90,2560]{1,0:T(8,128)(2,1)} %collective-permute-done.4.part_ref), channel_id=1, source_target_pairs={{0,8},{8,0},{1,9},{9,1},{2,10},{10,2},{3,11},{11,3},{4,12},{12,4},... | collective-permute-start | bytes 1382408 | tf_op jit(solution)/shard_map/ppermute | solution.py:31
  58.2 1.7 join.2
  60.0 1.5 fusion.5
  61.5 0.3 broadcast_select_fusion.2
  61.8 0.8 fusion.35.refs_0_
  62.6 3.6 %collective-permute-start.8 = (bf16[128,2560]{1,0:T(8,128)(2,1)}, bf16[128,2560]{1,0:T(8,128)(2,1)S(1)}, u32[]{:S(2)}, u32[]{:S(2)}) collective-permute-start(bf16[128,2560]{1,0:T(8,128)(2,1)} %collective-permute-done.3.refs_4_), channel_id=1, source_target_pairs={{0,3},{1,0},{2,1},{3,2},{4,7},{5,4},{6,5},{7,6},{8,11},{9,8},{10,9... | collective-permute-start | bytes 1966088 | tf_op jit(solution)/shard_map/ppermute | solution.py:31
  66.3 1.9 %collective-permute-start.7 = (bf16[128,2560]{1,0:T(8,128)(2,1)}, bf16[128,2560]{1,0:T(8,128)(2,1)S(1)}, u32[]{:S(2)}, u32[]{:S(2)}) collective-permute-start(bf16[128,2560]{1,0:T(8,128)(2,1)} %collective-permute-done.refs_0_), channel_id=1, source_target_pairs={{0,1},{1,2},{2,3},{3,0},{4,5},{5,6},{6,7},{7,4},{8,9},{9,10},{10,1... | collective-permute-start | bytes 1966088 | tf_op jit(solution)/shard_map/ppermute | solution.py:31
  68.2 0.8 fusion.34
  69.0 1.6 unpack.1
  70.6 1.5 fusion.36
  72.1 0.4 broadcast_select_fusion
  72.5 0.8 fusion.38.refs_3_
  73.3 0.8 fusion.37
  74.1 6.9 %collective-permute-done.8.refs_1_ = bf16[128,2560]{1,0:T(8,128)(2,1)S(1)} collective-permute-done((bf16[128,2560]{1,0:T(8,128)(2,1)}, bf16[128,2560]{1,0:T(8,128)(2,1)S(1)}, u32[]{:S(2)}, u32[]{:S(2)}) %collective-permute-start.8) | collective-permute-done | bytes 655392 | tf_op jit(solution)/shard_map/ppermute | solution.py:31
  81.0 4.5 %collective-permute-done.7.refs_0_ = bf16[128,2560]{1,0:T(8,128)(2,1)S(1)} collective-permute-done((bf16[128,2560]{1,0:T(8,128)(2,1)}, bf16[128,2560]{1,0:T(8,128)(2,1)S(1)}, u32[]{:S(2)}, u32[]{:S(2)}) %collective-permute-start.7) | collective-permute-done | bytes 655392 | tf_op jit(solution)/shard_map/ppermute | solution.py:31
  85.6 0.4 join.3
  86.0 0.6 fusion.4
  86.6 0.6 fusion.41
  87.3 0.1 broadcast_select_fusion.6
  87.4 0.1 broadcast_select_fusion.4
  87.6 0.4 fusion.43
  87.9 0.2 add.67
  88.2 3.1 %collective-permute-start.10 = (f32[160,2560]{1,0:T(8,128)S(1)}, f32[160,2560]{1,0:T(8,128)S(1)}, u32[]{:S(2)}, u32[]{:S(2)}) collective-permute-start(f32[160,2560]{1,0:T(8,128)S(1)} %add.67), channel_id=1, source_target_pairs={{0,8},{8,0},{1,9},{9,1},{2,10},{10,2},{3,11},{11,3},{4,12},{12,4},... | collective-permute-start | bytes 4915208 | tf_op jit(solution)/shard_map/ppermute | solution.py:31
  91.3 0.4 fusion.40
  91.6 0.2 add.64
  91.8 1.9 %collective-permute-start.9 = (f32[160,2560]{1,0:T(8,128)S(1)}, f32[160,2560]{1,0:T(8,128)S(1)}, u32[]{:S(2)}, u32[]{:S(2)}) collective-permute-start(f32[160,2560]{1,0:T(8,128)S(1)} %add.64), channel_id=1, source_target_pairs={{0,8},{8,0},{1,9},{9,1},{2,10},{10,2},{3,11},{11,3},{4,12},{12,4},... | collective-permute-start | bytes 4915208 | tf_op jit(solution)/shard_map/ppermute | solution.py:31
  93.8 0.4 fusion.42.refs_4_
  94.1 0.4 fusion.39.refs_1_
  94.5 2.7 %collective-permute-done.9.refs_2_ = f32[160,2560]{1,0:T(8,128)S(1)} collective-permute-done((f32[160,2560]{1,0:T(8,128)S(1)}, f32[160,2560]{1,0:T(8,128)S(1)}, u32[]{:S(2)}, u32[]{:S(2)}) %collective-permute-start.9) | collective-permute-done | bytes 1638432 | tf_op jit(solution)/shard_map/ppermute | solution.py:31
  97.2 1.9 %cut.1 = bf16[64,100,128]{2,1,0:T(8,128)(2,1)} custom-call(s32[1]{0:T(128)} %bitcast.1.half_ref, f32[160,2560]{1,0:T(8,128)S(1)} %fusion.35.refs_0_, f32[160,2560]{1,0:T(8,128)S(1)} %fusion.39.refs_1_, f32[160,2560]{1,0:T(8,128)S(1)} %collective-permute-done.9.refs_2_, f32[160,2560]{1,0:T(8,128)S(1)} %fusion.38.refs_3_, f32[160,2560]{1,0:T(8,128)S(1)} %fusion.42.refs_4_, ...), custom_call_target="tpu_custom_call" | custom-call | flops 1638400 | bytes 11468800 | tf_op jit(solution)/shard_map/cut/pallas_call | solution.py:71
  99.1 11.5 %all-to-all-start = ((bf16[64,100,128]{2,1,0:T(8,128)(2,1)}), bf16[64,100,128]{2,1,0:T(8,128)(2,1)}, u32[]{:S(2)}, u32[]{:S(2)}) async-start(bf16[64,100,128]{2,1,0:T(8,128)(2,1)} %cut.1), calls=%async_computation | async-start | bytes 3407872 | tf_op jit(solution)/shard_map/all_to_all | solution.py:317
  110.6 1.9 reshape.28
  112.5 0.1 shift_right_arithmetic.49
  112.5 0.1 shift_right_arithmetic.50
  112.7 0.2 shift_right_arithmetic.42
  112.8 0.1 shift_right_arithmetic.48
  113.0 0.1 dynamic-slice
  113.0 0.7 constant_dynamic-slice_fusion.1
  113.8 0.1 fusion.22
  113.9 37.8 %all-to-all-done = bf16[64,100,128]{2,1,0:T(8,128)(2,1)} async-done(((bf16[64,100,128]{2,1,0:T(8,128)(2,1)}), bf16[64,100,128]{2,1,0:T(8,128)(2,1)}, u32[]{:S(2)}, u32[]{:S(2)}) %all-to-all-start) | async-done | bytes 1638432 | tf_op jit(solution)/shard_map/all_to_all | solution.py:317
  151.7 1.7 convert_reduce_fusion
  153.4 4.6 %collective-permute-start.11 = (f32[50,128]{1,0:T(8,128)S(1)}, f32[50,128]{1,0:T(8,128)S(1)}, u32[]{:S(2)}, u32[]{:S(2)}) collective-permute-start(f32[50,128]{1,0:T(8,128)S(1)} %constant_dynamic-slice_fusion), channel_id=1, source_target_pairs={{0,8},{8,0},{1,9},{9,1},{2,10},{10,2},{3,11},{11,3},{4,12},{12,4},... | collective-permute-start | bytes 76808 | tf_op jit(solution)/shard_map/ppermute | solution.py:31
  158.0 0.8 collective-permute-done.11
  158.8 0.6 subtract_convert_fusion
  159.5 23.6 %all_to_all.10.mine_ref = bf16[32,50,128]{2,1,0:T(8,128)(2,1)S(1)} all-to-all(bf16[32,50,128]{2,1,0:T(8,128)(2,1)S(1)} %broadcast_in_dim.2), channel_id=1, replica_groups=mesh['yl'=4,'z'=8,'c'=2,'yh'=2,'x'=4] {'yl','z'}, dimensions={0} | all-to-all | bytes 819200 | tf_op jit(solution)/shard_map/all_to_all | solution.py:338
  183.2 4.3 %collective-permute-start.12 = (bf16[32,50,128]{2,1,0:T(8,128)(2,1)S(1)}, bf16[32,50,128]{2,1,0:T(8,128)(2,1)S(1)}, u32[]{:S(2)}, u32[]{:S(2)}) collective-permute-start(bf16[32,50,128]{2,1,0:T(8,128)(2,1)S(1)} %all_to_all.10.mine_ref), channel_id=1, source_target_pairs={{0,8},{8,0},{1,9},{9,1},{2,10},{10,2},{3,11},{11,3},{4,12},{12,4},... | collective-permute-start | bytes 1228808 | tf_op jit(solution)/shard_map/ppermute | solution.py:31
  187.4 1.4 collective-permute-done.12.twin_ref
  188.9 1.1 lay.1
  (31 shorter events, 0.2 us)
Async XLA Ops:
  0.6 2.1 %copy-start = (bf16[256,2560]{1,0:T(8,128)(2,1)S(1)}, bf16[256,2560]{1,0:T(8,128)(2,1)}, u32[]{:S(2)}) copy-start(bf16[256,2560]{1,0:T(8,128)(2,1)} %refs_2_.1) | copy-start | bytes 3932164
  0.6 16.7 %copy-start.1 = (bf16[160,2560]{1,0:T(8,128)(2,1)S(1)}, bf16[160,2560]{1,0:T(8,128)(2,1)}, u32[]{:S(2)}) copy-start(bf16[160,2560]{1,0:T(8,128)(2,1)} %weights_ref.1) | copy-start | bytes 2457604
  0.7 16.7 %copy-start.2 = (s32[5,2560]{1,0:T(8,128)S(1)}, s32[5,2560]{1,0:T(8,128)}, u32[]{:S(2)}) copy-start(s32[5,2560]{1,0:T(8,128)} %signs_ref.1) | copy-start | bytes 153604
  2.8 22.9 %copy-start.3 = (bf16[160,2048]{1,0:T(8,128)(2,1)S(1)}, bf16[160,2048]{1,0:T(8,128)(2,1)}, u32[]{:S(2)}) copy-start(bf16[160,2048]{1,0:T(8,128)(2,1)} %resid_ref.1) | copy-start | bytes 1966084
  2.8 22.9 %copy-start.4 = (bf16[160,2048]{1,0:T(8,128)(2,1)S(1)}, bf16[160,2048]{1,0:T(8,128)(2,1)}, u32[]{:S(2)}) copy-start(bf16[160,2048]{1,0:T(8,128)(2,1)} %target_ref.1) | copy-start | bytes 1966084
  3.7 43.0 %collective-permute-start.3 = (bf16[128,2560]{1,0:T(8,128)(2,1)}, bf16[128,2560]{1,0:T(8,128)(2,1)}, u32[]{:S(2)}, u32[]{:S(2)}) collective-permute-start(bf16[128,2560]{1,0:T(8,128)(2,1)} %slice.43), channel_id=1, source_target_pairs={{0,3},{1,0},{2,1},{3,2},{4,7},{5,4},{6,5},{7,6},{8,11},{9,8},{10,9... | collective-permute-start | bytes 1966088 | tf_op jit(solution)/shard_map/ppermute | solution.py:31
  8.9 49.3 %collective-permute-start.1 = (bf16[128,2560]{1,0:T(8,128)(2,1)}, bf16[128,2560]{1,0:T(8,128)(2,1)}, u32[]{:S(2)}, u32[]{:S(2)}) collective-permute-start(bf16[128,2560]{1,0:T(8,128)(2,1)} %slice.43), channel_id=1, source_target_pairs={{0,1},{1,2},{2,3},{3,0},{4,5},{5,6},{6,7},{7,4},{8,9},{9,10},{10,1... | collective-permute-start | bytes 1966088 | tf_op jit(solution)/shard_map/ppermute | solution.py:31
  10.8 47.4 %collective-permute-start = (bf16[128,2560]{1,0:T(8,128)(2,1)}, bf16[128,2560]{1,0:T(8,128)(2,1)}, u32[]{:S(2)}, u32[]{:S(2)}) collective-permute-start(bf16[128,2560]{1,0:T(8,128)(2,1)} %slice.42), channel_id=1, source_target_pairs={{0,1},{1,2},{2,3},{3,0},{4,5},{5,6},{6,7},{7,4},{8,9},{9,10},{10,1... | collective-permute-start | bytes 1966088 | tf_op jit(solution)/shard_map/ppermute | solution.py:31
  12.9 45.3 %collective-permute-start.2 = (bf16[128,2560]{1,0:T(8,128)(2,1)}, bf16[128,2560]{1,0:T(8,128)(2,1)}, u32[]{:S(2)}, u32[]{:S(2)}) collective-permute-start(bf16[128,2560]{1,0:T(8,128)(2,1)} %slice.42), channel_id=1, source_target_pairs={{0,3},{1,0},{2,1},{3,2},{4,7},{5,4},{6,5},{7,6},{8,11},{9,8},{10,9... | collective-permute-start | bytes 1966088 | tf_op jit(solution)/shard_map/ppermute | solution.py:31
  18.2 20.5 %collective-permute-start.4 = (bf16[90,2560]{1,0:T(8,128)(2,1)}, bf16[90,2560]{1,0:T(8,128)(2,1)}, u32[]{:S(2)}, u32[]{:S(2)}) collective-permute-start(bf16[90,2560]{1,0:T(8,128)(2,1)} %pack.1), channel_id=1, source_target_pairs={{0,4},{4,0},{1,5},{5,1},{2,6},{6,2},{3,7},{7,3},{8,12},{12,8},{9,1... | collective-permute-start | bytes 1382408 | tf_op jit(solution)/shard_map/ppermute | solution.py:31
  26.4 0.8 copy-start.5
  27.3 0.7 copy-start.7
  38.7 33.4 %collective-permute-start.6 = (bf16[160,1024]{1,0:T(8,128)(2,1)}, bf16[160,1024]{1,0:T(8,128)(2,1)S(1)}, u32[]{:S(2)}, u32[]{:S(2)}) collective-permute-start(bf16[160,1024]{1,0:T(8,128)(2,1)} %copy-done.7), channel_id=1, source_target_pairs={{0,4},{4,0},{1,5},{5,1},{2,6},{6,2},{3,7},{7,3},{8,12},{12,8},{9,1... | collective-permute-start | bytes 983048 | tf_op jit(solution)/shard_map/ppermute | solution.py:31
  46.7 22.3 %collective-permute-start.5 = (bf16[90,2560]{1,0:T(8,128)(2,1)}, bf16[90,2560]{1,0:T(8,128)(2,1)S(1)}, u32[]{:S(2)}, u32[]{:S(2)}) collective-permute-start(bf16[90,2560]{1,0:T(8,128)(2,1)} %collective-permute-done.4.part_ref), channel_id=1, source_target_pairs={{0,8},{8,0},{1,9},{9,1},{2,10},{10,2},{3,11},{11,3},{4,12},{12,4},... | collective-permute-start | bytes 1382408 | tf_op jit(solution)/shard_map/ppermute | solution.py:31
  60.0 1.5 copy-start.6
  62.6 18.4 %collective-permute-start.8 = (bf16[128,2560]{1,0:T(8,128)(2,1)}, bf16[128,2560]{1,0:T(8,128)(2,1)S(1)}, u32[]{:S(2)}, u32[]{:S(2)}) collective-permute-start(bf16[128,2560]{1,0:T(8,128)(2,1)} %collective-permute-done.3.refs_4_), channel_id=1, source_target_pairs={{0,3},{1,0},{2,1},{3,2},{4,7},{5,4},{6,5},{7,6},{8,11},{9,8},{10,9... | collective-permute-start | bytes 1966088 | tf_op jit(solution)/shard_map/ppermute | solution.py:31
  66.3 19.3 %collective-permute-start.7 = (bf16[128,2560]{1,0:T(8,128)(2,1)}, bf16[128,2560]{1,0:T(8,128)(2,1)S(1)}, u32[]{:S(2)}, u32[]{:S(2)}) collective-permute-start(bf16[128,2560]{1,0:T(8,128)(2,1)} %collective-permute-done.refs_0_), channel_id=1, source_target_pairs={{0,1},{1,2},{2,3},{3,0},{4,5},{5,6},{6,7},{7,4},{8,9},{9,10},{10,1... | collective-permute-start | bytes 1966088 | tf_op jit(solution)/shard_map/ppermute | solution.py:31
  88.2 6.3 %collective-permute-start.10 = (f32[160,2560]{1,0:T(8,128)S(1)}, f32[160,2560]{1,0:T(8,128)S(1)}, u32[]{:S(2)}, u32[]{:S(2)}) collective-permute-start(f32[160,2560]{1,0:T(8,128)S(1)} %add.67), channel_id=1, source_target_pairs={{0,8},{8,0},{1,9},{9,1},{2,10},{10,2},{3,11},{11,3},{4,12},{12,4},... | collective-permute-start | bytes 4915208 | tf_op jit(solution)/shard_map/ppermute | solution.py:31
  91.8 5.4 %collective-permute-start.9 = (f32[160,2560]{1,0:T(8,128)S(1)}, f32[160,2560]{1,0:T(8,128)S(1)}, u32[]{:S(2)}, u32[]{:S(2)}) collective-permute-start(f32[160,2560]{1,0:T(8,128)S(1)} %add.64), channel_id=1, source_target_pairs={{0,8},{8,0},{1,9},{9,1},{2,10},{10,2},{3,11},{11,3},{4,12},{12,4},... | collective-permute-start | bytes 4915208 | tf_op jit(solution)/shard_map/ppermute | solution.py:31
  99.1 52.5 %all-to-all-start = ((bf16[64,100,128]{2,1,0:T(8,128)(2,1)}), bf16[64,100,128]{2,1,0:T(8,128)(2,1)}, u32[]{:S(2)}, u32[]{:S(2)}) async-start(bf16[64,100,128]{2,1,0:T(8,128)(2,1)} %cut.1), calls=%async_computation | async-start | bytes 3407872 | tf_op jit(solution)/shard_map/all_to_all | solution.py:317
  112.9 45.9 %copy-start.8 = (f32[50,128]{1,0:T(8,128)S(1)}, f32[50,128]{1,0:T(8,128)}, u32[]{:S(2)}) copy-start(f32[50,128]{1,0:T(8,128)} %param.12) | copy-start | bytes 76804
  112.9 45.9 %copy-start.9 = (f32[50,128]{1,0:T(8,128)S(1)}, f32[50,128]{1,0:T(8,128)}, u32[]{:S(2)}) copy-start(f32[50,128]{1,0:T(8,128)} %param.13) | copy-start | bytes 76804
  153.4 5.4 %collective-permute-start.11 = (f32[50,128]{1,0:T(8,128)S(1)}, f32[50,128]{1,0:T(8,128)S(1)}, u32[]{:S(2)}, u32[]{:S(2)}) collective-permute-start(f32[50,128]{1,0:T(8,128)S(1)} %constant_dynamic-slice_fusion), channel_id=1, source_target_pairs={{0,8},{8,0},{1,9},{9,1},{2,10},{10,2},{3,11},{11,3},{4,12},{12,4},... | collective-permute-start | bytes 76808 | tf_op jit(solution)/shard_map/ppermute | solution.py:31
  183.2 5.7 %collective-permute-start.12 = (bf16[32,50,128]{2,1,0:T(8,128)(2,1)S(1)}, bf16[32,50,128]{2,1,0:T(8,128)(2,1)S(1)}, u32[]{:S(2)}, u32[]{:S(2)}) collective-permute-start(bf16[32,50,128]{2,1,0:T(8,128)(2,1)S(1)} %all_to_all.10.mine_ref), channel_id=1, source_target_pairs={{0,8},{8,0},{1,9},{9,1},{2,10},{10,2},{3,11},{11,3},{4,12},{12,4},... | collective-permute-start | bytes 1228808 | tf_op jit(solution)/shard_map/ppermute | solution.py:31
